TPU v7x, 768 devices: a whole 4x8x12 slice. The times are simulated.
768 devices in a mesh: face: 6 (over z_lo), fy: 8 (over x, core), fx: 16 (over y, z_hi).
Axes of the slice: x: 4, y: 8, z: 12 (z_hi: 2, z_lo: 6; z = z_hi * 6 + z_lo), core: 2. Of those that a mesh axis runs over, the one named last changes fastest.
Arguments:
- state: float32 [6, 128, 128, 192], P('face', 'fy', 'fx'), may hold values from -6 to 6
- jacobian: float32 [6, 128, 128], P('face', 'fy', 'fx'), may hold values from 0.5 to 2
- metric_diag: float32 [2, 6, 128, 128], P(None, 'face', 'fy', 'fx'), may hold values from 0.6 to 1.4
- metric_cross: float32 [6, 128, 128], P('face', 'fy', 'fx'), may hold values from -0.3 to 0.3
- coriolis: float32 [6, 128, 128], P('face', 'fy', 'fx'), may hold values from -2 to 2
- nbr_face: int32 [6, 4], replicated, may hold values from 0 to 5, as said below
- nbr_edge: int32 [6, 4], replicated, may hold values from 0 to 3, as said below
Outputs:
- updated: float32 [6, 128, 128, 192], P('face', 'fy', 'fx')
Inputs may be any that keep to these rules, and one draw needn't show every extreme that they name: Edge e of a face is 0 south (row 0), 1 east (last column), 2 north (last row), 3 west (column 0). Edge e of face f is glued to edge nbr_edge[f, e] of face nbr_face[f, e], and that edge back to it; the 6 faces are glued as the surface of a cube, three faces at each corner, the two glued edges running in opposite senses when both are read counterclockwise. `nbr_edge`: see nbr_face.
All inputs are finite; a program needn't handle non-finite values.
Results may differ from a plain program's by a relative error of at most 0.0001.
Values sent between devices are 32-bit elements; how exact they have to be, the bound alone decides.
No kernel may reach another device: no remote copies, remote signals or barrier semaphores. Data moves between devices by JAX's collectives and lax.ppermute only.
A program may use at most 32 MiB of HBM per device.

v0:
```python
import jax
import jax.numpy as jnp
import numpy as np
from jax import lax
from jax.sharding import PartitionSpec as P

time_step = 0.05
hyper_coeff = 0.0005


def padded_2(cells, sides, width):
    for axis, dim in sides:
        count = lax.axis_size(axis)
        ends = count - 1
        head = lax.slice_in_dim(cells, 0, width, axis=dim)
        tail = lax.slice_in_dim(cells, cells.shape[dim] - width, cells.shape[dim], axis=dim)
        cells = jnp.concatenate(
            [
                lax.ppermute(tail, axis, [(i, (i + 1) % count) for i in range(ends)]),
                cells,
                lax.ppermute(head, axis, [((i + 1) % count, i) for i in range(ends)]),
            ],
            axis=dim,
        )
    return cells


def sent_together(arrays, axis, split_dim, concat_dim, along):
    widths = [a.shape[along] for a in arrays]
    both = jnp.concatenate(arrays, axis=along)
    out = lax.all_to_all(both, axis, split_axis=split_dim, concat_axis=concat_dim, tiled=True)
    return tuple(jnp.split(out, [sum(widths[:k]) for k in range(1, len(widths))], axis=along))


def cut_along(shard, dim, devices):
    dims = shard.shape
    tiles = shard.reshape(*dims[:dim], devices, dims[dim] // devices, *dims[dim + 1 :])
    return jnp.moveaxis(tiles, dim, 0)


def summed_on_arrival(shard, axis, dim):
    tiles = cut_along(shard, dim, lax.axis_size(axis))
    arrived = lax.all_to_all(tiles, axis, split_axis=0, concat_axis=0, tiled=True)
    return arrived.sum(axis=0)


def copy_for_each(shard, axis):
    devices = lax.axis_size(axis)
    return lax.all_to_all(
        jnp.broadcast_to(shard[None], (devices, *shard.shape)), axis, 0, 0, tiled=True
    )


def of_everyone(shard, axis):
    return copy_for_each(shard, axis).sum(axis=0)


def deriv_table():
    gll_nodes = np.array([-1.0, -1.0 / np.sqrt(5.0), 1.0 / np.sqrt(5.0), 1.0])
    bary_weights = np.ones(4)
    for j in range(4):
        for m in range(4):
            if m != j:
                bary_weights[j] = bary_weights[j] / (gll_nodes[j] - gll_nodes[m])
    matrix = np.zeros((4, 4))
    for i in range(4):
        for j in range(4):
            if i != j:
                matrix[i, j] = bary_weights[j] / bary_weights[i] / (gll_nodes[i] - gll_nodes[j])
        matrix[i, i] = -np.sum(matrix[i])
    return matrix


def along_x(values):
    face_count, row_count, col_count, chan_count = values.shape
    blocks = values.reshape(face_count, row_count, col_count // 4, 4, chan_count)
    result = jnp.einsum(
        "jk,abekc->abejc",
        jnp.asarray(deriv_table(), jnp.float32),
        blocks,
        precision=lax.Precision.HIGHEST,
    )
    return result.reshape(values.shape)


def along_y(values):
    face_count, row_count, col_count, chan_count = values.shape
    blocks = values.reshape(face_count, row_count // 4, 4, col_count, chan_count)
    result = jnp.einsum(
        "ik,aekxc->aeixc",
        jnp.asarray(deriv_table(), jnp.float32),
        blocks,
        precision=lax.Precision.HIGHEST,
    )
    return result.reshape(values.shape)


def mass_of(jacobian):
    weights = jnp.asarray([1.0 / 6.0, 5.0 / 6.0, 5.0 / 6.0, 1.0 / 6.0], jnp.float32)
    row_weight = jnp.tile(weights, jacobian.shape[1] // 4)
    col_weight = jnp.tile(weights, jacobian.shape[2] // 4)
    return jacobian * row_weight[None, :, None] * col_weight[None, None, :]


def tendency(state, geometry, planet):
    volume, metric_xx, metric_yy, metric_xy = geometry
    levels = state.shape[-1] // 3
    wind_u = state[..., :levels]
    wind_v = state[..., levels : 2 * levels]
    temper = state[..., 2 * levels :]
    contra_u = metric_xx * wind_u + metric_xy * wind_v
    contra_v = metric_xy * wind_u + metric_yy * wind_v
    energy = 0.5 * (wind_u * contra_u + wind_v * contra_v) + temper
    xderivs = along_x(jnp.concatenate([wind_v, temper, energy], -1))
    yderivs = along_y(jnp.concatenate([wind_u, temper, energy], -1))
    absolute = (xderivs[..., :levels] - yderivs[..., :levels]) / volume + planet
    tend_u = absolute * volume * contra_v - xderivs[..., 2 * levels :]
    tend_v = -absolute * volume * contra_u - yderivs[..., 2 * levels :]
    tend_t = -(
        contra_u * xderivs[..., levels : 2 * levels] + contra_v * yderivs[..., levels : 2 * levels]
    )
    return state + time_step * jnp.concatenate([tend_u, tend_v, tend_t], -1)


def laplace(values, geometry):
    volume, metric_xx, metric_yy, metric_xy = geometry
    grad_x = along_x(values)
    grad_y = along_y(values)
    flux_x = volume * (metric_xx * grad_x + metric_xy * grad_y)
    flux_y = volume * (metric_xy * grad_x + metric_yy * grad_y)
    return (along_x(flux_x) + along_y(flux_y)) / volume


def combine(values, axis):
    length = values.shape[axis] - 2
    positions = jnp.arange(length)
    leading = (positions % 4 == 0).astype(jnp.float32)
    trailing = (positions % 4 == 3).astype(jnp.float32)
    broad_shape = [1, 1, 1, 1]
    broad_shape[axis] = length
    leading = leading.reshape(broad_shape)
    trailing = trailing.reshape(broad_shape)
    middle = lax.slice_in_dim(values, 1, length + 1, axis=axis)
    previous = lax.slice_in_dim(values, 0, length, axis=axis)
    following = lax.slice_in_dim(values, 2, length + 2, axis=axis)
    return middle + leading * previous + trailing * following


def rotate(segment, quarter, levels):
    cosine = ((quarter == 0).astype(jnp.float32) - (quarter == 2).astype(jnp.float32))[..., None]
    sine_part = ((quarter == 1).astype(jnp.float32) - (quarter == 3).astype(jnp.float32))[..., None]
    wind_u = segment[..., :levels]
    wind_v = segment[..., levels : 2 * levels]
    return jnp.concatenate(
        [
            cosine * wind_u - sine_part * wind_v,
            sine_part * wind_u + cosine * wind_v,
            segment[..., 2 * levels :],
        ],
        -1,
    )


def in_face(values):
    padded = padded_2(values, (("fy", 1), ("fx", 2)), 1)
    return combine(combine(padded, 2), 1)


def place_pieces(
    got_flat,
    got_tall,
    vector,
    nbr_edge,
    flat_edge,
    tall_edge,
    on_south,
    on_west,
    flat_start,
    tall_start,
    face_local,
    side_nodes,
    chan_count,
    levels,
):
    edge_ids = jnp.arange(4, dtype=jnp.int32)
    flat_target = nbr_edge[:, flat_edge]
    tall_target = nbr_edge[:, tall_edge]
    if vector:
        got_flat = rotate(got_flat, ((flat_target - flat_edge + 2) % 4)[None, :, None], levels)
        got_tall = rotate(got_tall, ((tall_target - tall_edge + 2) % 4)[None, :, None], levels)
    got_flat = jnp.where(on_south, got_flat[:, :, ::-1], got_flat)
    got_tall = jnp.where(on_west, got_tall, got_tall[:, :, ::-1])
    flat_pick = (flat_target[:, None] == edge_ids[None, :]).astype(jnp.float32)
    tall_pick = (tall_target[:, None] == edge_ids[None, :]).astype(jnp.float32)
    flat_rims = jnp.einsum("se,gsjc->gejc", flat_pick, got_flat, precision=lax.Precision.HIGHEST)
    tall_rims = jnp.einsum("se,gsjc->gejc", tall_pick, got_tall, precision=lax.Precision.HIGHEST)
    empty_rims = jnp.zeros((face_local, 4, side_nodes, chan_count), jnp.float32)
    rim_strips = lax.dynamic_update_slice(empty_rims, flat_rims, (0, 0, flat_start, 0))
    return rim_strips + lax.dynamic_update_slice(empty_rims, tall_rims, (0, 0, tall_start, 0))


def outgoing(
    summed, nbr_face, face_ids, flat_edge, tall_edge, on_south, on_west, flat_live, tall_live
):
    row_count = summed.shape[1]
    col_count = summed.shape[2]
    all_faces = jnp.arange(nbr_face.shape[0], dtype=jnp.int32)
    flat_piece = jnp.where(on_south, summed[:, 0], summed[:, row_count - 1])
    tall_piece = jnp.where(on_west, summed[:, :, 0], summed[:, :, col_count - 1])
    flat_dest = nbr_face[face_ids, flat_edge]
    tall_dest = nbr_face[face_ids, tall_edge]
    flat_send = ((all_faces[:, None] == flat_dest[None, :]) & flat_live).astype(jnp.float32)
    tall_send = ((all_faces[:, None] == tall_dest[None, :]) & tall_live).astype(jnp.float32)
    return (
        flat_send[:, :, None, None] * flat_piece[None],
        tall_send[:, :, None, None] * tall_piece[None],
    )


def assemble(values, vector, nbr_face, nbr_edge):
    summed = in_face(values)
    face_local, row_count, col_count, chan_count = summed.shape
    levels = chan_count // 3
    row_index = lax.axis_index("fy")
    col_index = lax.axis_index("fx")
    side_nodes = row_count * lax.axis_size("fy")
    face_ids = lax.axis_index("face") * face_local + jnp.arange(face_local, dtype=jnp.int32)
    on_south = row_index == 0
    on_north = row_index == lax.axis_size("fy") - 1
    on_west = col_index == 0
    on_east = col_index == lax.axis_size("fx") - 1
    flat_live = on_south | on_north
    tall_live = on_west | on_east
    flat_edge = jnp.where(on_south, 0, 2).astype(jnp.int32)
    tall_edge = jnp.where(on_west, 3, 1).astype(jnp.int32)
    flat_start = jnp.where(
        on_south, side_nodes - (col_index + 1) * col_count, col_index * col_count
    )
    tall_start = jnp.where(on_west, row_index * row_count, side_nodes - (row_index + 1) * row_count)
    send_flat, send_tall = outgoing(
        summed, nbr_face, face_ids, flat_edge, tall_edge, on_south, on_west, flat_live, tall_live
    )
    got_flat, got_tall = sent_together((send_flat, send_tall), "face", 0, 1, 2)
    rim_strips = place_pieces(
        got_flat,
        got_tall,
        vector,
        nbr_edge,
        flat_edge,
        tall_edge,
        on_south,
        on_west,
        flat_start,
        tall_start,
        face_local,
        side_nodes,
        chan_count,
        levels,
    )
    flat_lines = jnp.stack([rim_strips[:, 0], rim_strips[:, 2, ::-1]], axis=1)
    flat_lines = flat_lines.reshape(face_local, 2, lax.axis_size("fx"), col_count, chan_count)
    tall_lines = jnp.stack([rim_strips[:, 1], rim_strips[:, 3, ::-1]], axis=1)
    tall_lines = tall_lines.reshape(face_local, 2, lax.axis_size("fy"), row_count, chan_count)
    flat_block = summed_on_arrival(flat_lines, "fx", 2)
    tall_block = summed_on_arrival(tall_lines, "fy", 2)
    flat_block = of_everyone(flat_block, "fy")
    tall_block = of_everyone(tall_block, "fx")
    flat_add = jnp.where(on_south, flat_block[:, 0, 0], flat_block[:, 1, 0])
    tall_add = jnp.where(on_west, tall_block[:, 1, 0], tall_block[:, 0, 0])
    result = summed.at[:, 0].add(jnp.where(on_south, flat_add, 0.0))
    result = result.at[:, row_count - 1].add(jnp.where(on_north, flat_add, 0.0))
    result = result.at[:, :, 0].add(jnp.where(on_west, tall_add, 0.0))
    result = result.at[:, :, col_count - 1].add(jnp.where(on_east, tall_add, 0.0))
    return result


def per_device(state, jacobian, metric_diag, metric_cross, coriolis, nbr_face, nbr_edge):
    node_mass = mass_of(jacobian)[..., None]
    total_mass = assemble(node_mass, False, nbr_face, nbr_edge)
    geometry = (
        jacobian[..., None],
        metric_diag[0][..., None],
        metric_diag[1][..., None],
        metric_cross[..., None],
    )
    raw = tendency(state, geometry, coriolis[..., None])
    sectioned = assemble(node_mass * raw, True, nbr_face, nbr_edge) / total_mass
    first_lap = (
        assemble(node_mass * laplace(sectioned, geometry), True, nbr_face, nbr_edge) / total_mass
    )
    second_lap = (
        assemble(node_mass * laplace(first_lap, geometry), True, nbr_face, nbr_edge) / total_mass
    )
    return sectioned - hyper_coeff * second_lap


def solution(mesh):
    return jax.shard_map(
        per_device,
        mesh=mesh,
        in_specs=(
            P("face", "fy", "fx", None),
            P("face", "fy", "fx"),
            P(None, "face", "fy", "fx"),
            P("face", "fy", "fx"),
            P("face", "fy", "fx"),
            P(),
            P(),
        ),
        out_specs=P("face", "fy", "fx", None),
        check_vma=False,
    )
```

profile of v0, /device:TPU:72, one launch (start us, length us, event | category | flops | bytes accessed | tf_op | source)
XLA Modules:
  0.0 472.9 jit_solution(1327678987756762462)
XLA Ops:
  15.5 3.6 collective-permute-start.4
  21.9 14.1 %collective-permute-start.7 = (f32[1,18,1,1]{1,2,3,0:T(1,128)S(1)}, f32[1,18,1,1]{1,2,3,0:T(1,128)S(1)}, u32[]{:S(2)}, u32[]{:S(2)}) collective-permute-start(f32[1,18,1,1]{1,2,3,0:T(1,128)S(1)} %get-tuple-element.281), channel_id=1, source_target_pairs={{1,0},{2,1},{3,2},{4,3},{5,4},{6,5},{7,6},{8,7},{9,8},{10,9},{11,1... | collective-permute-start | bytes 224 | tf_op jit(solution)/shard_map/ppermute | solution.py:21
  38.1 10.6 %collective-permute-done.6 = f32[1,18,1,1]{1,2,3,0:T(1,128)S(1)} collective-permute-done((f32[1,18,1,1]{1,2,3,0:T(1,128)S(1)}, f32[1,18,1,1]{1,2,3,0:T(1,128)S(1)}, u32[]{:S(2)}, u32[]{:S(2)}) %collective-permute-start.6) | collective-permute-done | bytes 104 | tf_op jit(solution)/shard_map/ppermute | solution.py:19
  49.9 6.9 %all-to-all-start.5 = ((f32[6,1,24,1]{2,3,1,0:T(1,128)}), f32[6,1,24,1]{2,3,1,0:T(1,128)S(1)}, u32[]{:S(2)}, u32[]{:S(2)}) async-start(f32[6,1,24,1]{2,3,1,0:T(1,128)} %pad_maximum_fusion.45), calls=%async_computation.5 | async-start | bytes 6144 | tf_op jit(solution)/shard_map/all_to_all | solution.py:31
  56.9 7.0 %all-to-all-done.5 = f32[6,1,24,1]{2,3,1,0:T(1,128)S(1)} async-done(((f32[6,1,24,1]{2,3,1,0:T(1,128)}), f32[6,1,24,1]{2,3,1,0:T(1,128)S(1)}, u32[]{:S(2)}, u32[]{:S(2)}) %all-to-all-start.5) | async-done | bytes 608 | tf_op jit(solution)/shard_map/all_to_all | solution.py:31
  65.7 8.8 %all-to-all-start.6 = ((f32[16,1,2,1,8,1]{4,2,5,3,1,0:T(2,128)}), f32[16,1,2,1,8,1]{4,2,5,3,1,0:T(2,128)S(1)}, u32[]{:S(2)}, u32[]{:S(2)}) async-start(f32[16,1,2,1,8,1]{4,2,5,3,1,0:T(2,128)} %copy.327), calls=%async_computation.6 | async-start | bytes 32768 | tf_op jit(solution)/shard_map/all_to_all | solution.py:43
  74.8 9.7 %collective-permute-start.3 = (f32[1,18,1,192]{3,0,2,1:T(1,128)S(1)}, f32[1,18,1,192]{3,0,2,1:T(1,128)S(1)}, u32[]{:S(2)}, u32[]{:S(2)}) collective-permute-start(f32[1,18,1,192]{3,0,2,1:T(1,128)S(1)} %get-tuple-element.261), channel_id=1, source_target_pairs={{1,0},{2,1},{3,2},{4,3},{5,4},{6,5},{7,6},{8,7},{9,8},{10,9},{11,1... | collective-permute-start | bytes 41480 | tf_op jit(solution)/shard_map/ppermute | solution.py:21
  88.5 4.4 all-to-all-start.8
  92.9 4.8 %collective-permute-done.2 = f32[1,18,1,192]{3,0,2,1:T(1,128)S(1)} collective-permute-done((f32[1,18,1,192]{3,0,2,1:T(1,128)S(1)}, f32[1,18,1,192]{3,0,2,1:T(1,128)S(1)}, u32[]{:S(2)}, u32[]{:S(2)}) %collective-permute-start.2) | collective-permute-done | bytes 13856 | tf_op jit(solution)/shard_map/ppermute | solution.py:19
  99.1 4.7 all-to-all-start.7
  104.5 4.7 all-to-all-done.7
  109.2 4.4 all-to-all-start
  114.5 7.8 %all-to-all-done = f32[6,1,24,192]{3,2,1,0:T(8,128)S(1)} async-done(((f32[6,1,24,192]{3,2,1,0:T(8,128)}), f32[6,1,24,192]{3,2,1,0:T(8,128)S(1)}, u32[]{:S(2)}, u32[]{:S(2)}) %all-to-all-start) | async-done | bytes 110624 | tf_op jit(solution)/shard_map/all_to_all | solution.py:31
  122.9 12.8 %all-to-all-start.9 = ((f32[16,1,2,1,16,1]{4,2,5,3,1,0:T(2,128)}), f32[16,1,2,1,16,1]{4,2,5,3,1,0:T(2,128)S(1)}, u32[]{:S(2)}, u32[]{:S(2)}) async-start(f32[16,1,2,1,16,1]{4,2,5,3,1,0:T(2,128)} %broadcast_in_dim.65), calls=%async_computation.9 | async-start | bytes 32768 | tf_op jit(solution)/shard_map/all_to_all | solution.py:49
  138.4 10.8 %all-to-all-done.9 = f32[16,1,2,1,16,1]{4,2,5,3,1,0:T(2,128)S(1)} async-done(((f32[16,1,2,1,16,1]{4,2,5,3,1,0:T(2,128)}), f32[16,1,2,1,16,1]{4,2,5,3,1,0:T(2,128)S(1)}, u32[]{:S(2)}, u32[]{:S(2)}) %all-to-all-start.9) | async-done | bytes 2080 | tf_op jit(solution)/shard_map/all_to_all | solution.py:49
  149.2 4.8 %all-to-all-start.1 = ((f32[16,1,2,1,8,192]{5,2,4,3,1,0:T(2,128)}), f32[16,1,2,1,8,192]{5,2,4,3,1,0:T(2,128)S(1)}, u32[]{:S(2)}, u32[]{:S(2)}) async-start(f32[16,1,2,1,8,192]{5,2,4,3,1,0:T(2,128)} %bitcast.32), calls=%async_computation.1 | async-start | bytes 524288 | tf_op jit(solution)/shard_map/all_to_all | solution.py:43
  155.4 16.4 %all-to-all-done.1 = f32[16,1,2,1,8,192]{5,2,4,3,1,0:T(2,128)S(1)} async-done(((f32[16,1,2,1,8,192]{5,2,4,3,1,0:T(2,128)}), f32[16,1,2,1,8,192]{5,2,4,3,1,0:T(2,128)S(1)}, u32[]{:S(2)}, u32[]{:S(2)}) %all-to-all-start.1) | async-done | bytes 196640 | tf_op jit(solution)/shard_map/all_to_all | solution.py:43
  171.8 3.4 all-to-all-start.3
  175.3 7.3 %all-to-all-done.3 = f32[8,1,2,1,16,192]{5,2,4,3,1,0:T(2,128)S(1)} async-done(((f32[8,1,2,1,16,192]{5,2,4,3,1,0:T(2,128)}), f32[8,1,2,1,16,192]{5,2,4,3,1,0:T(2,128)S(1)}, u32[]{:S(2)}, u32[]{:S(2)}) %all-to-all-start.3) | async-done | bytes 196640 | tf_op jit(solution)/shard_map/all_to_all | solution.py:43
  183.3 3.4 all-to-all-start.2
  186.8 5.9 %all-to-all-done.2 = f32[8,1,2,1,8,192]{5,4,3,2,1,0:T(8,128)S(1)} async-done(((f32[8,1,2,1,8,192]{5,4,3,2,1,0:T(8,128)}), f32[8,1,2,1,8,192]{5,4,3,2,1,0:T(8,128)S(1)}, u32[]{:S(2)}, u32[]{:S(2)}) %all-to-all-start.2) | async-done | bytes 98336 | tf_op jit(solution)/shard_map/all_to_all | solution.py:49
  193.6 4.8 %all-to-all-start.4 = ((f32[16,1,2,1,16,192]{5,4,3,2,1,0:T(8,128)}), f32[16,1,2,1,16,192]{5,4,3,2,1,0:T(8,128)S(1)}, u32[]{:S(2)}, u32[]{:S(2)}) async-start(f32[16,1,2,1,16,192]{5,4,3,2,1,0:T(8,128)} %broadcast_in_dim.57), calls=%async_computation.4 | async-start | bytes 1048576 | tf_op jit(solution)/shard_map/all_to_all | solution.py:49
  198.5 28.2 %all-to-all-done.4 = f32[16,1,2,1,16,192]{5,4,3,2,1,0:T(8,128)S(1)} async-done(((f32[16,1,2,1,16,192]{5,4,3,2,1,0:T(8,128)}), f32[16,1,2,1,16,192]{5,4,3,2,1,0:T(8,128)S(1)}, u32[]{:S(2)}, u32[]{:S(2)}) %all-to-all-start.4) | async-done | bytes 393248 | tf_op jit(solution)/shard_map/all_to_all | solution.py:49
  231.2 3.0 collective-permute-start.8
  235.2 3.1 collective-permute-start.11
  238.3 9.1 %collective-permute-start.10 = (f32[1,18,1,192]{3,0,2,1:T(1,128)S(1)}, f32[1,18,1,192]{3,0,2,1:T(1,128)S(1)}, u32[]{:S(2)}, u32[]{:S(2)}) collective-permute-start(f32[1,18,1,192]{3,0,2,1:T(1,128)S(1)} %get-tuple-element.256), channel_id=1, source_target_pairs={{0,1},{1,2},{2,3},{3,4},{4,5},{5,6},{6,7},{7,8},{8,9},{9,10},{10,1... | collective-permute-start | bytes 41480 | tf_op jit(solution)/shard_map/ppermute | solution.py:19
  247.4 3.8 collective-permute-done.10
  251.9 11.5 %all_to_all.128 = f32[6,1,24,192]{3,2,1,0:T(8,128)S(1)} all-to-all(f32[6,1,24,192]{3,2,1,0:T(8,128)S(1)} %pad_maximum_fusion.27), channel_id=1, replica_groups=mesh['face'=6,'fy'=8,'fx'=16] {'face'}, dimensions={0} | all-to-all | bytes 221184 | tf_op jit(solution)/shard_map/all_to_all | solution.py:31
  266.1 9.7 %all-to-all-start.11 = ((f32[16,1,2,1,8,192]{5,2,4,3,1,0:T(2,128)}), f32[16,1,2,1,8,192]{5,2,4,3,1,0:T(2,128)S(1)}, u32[]{:S(2)}, u32[]{:S(2)}) async-start(f32[16,1,2,1,8,192]{5,2,4,3,1,0:T(2,128)} %bitcast.93), calls=%async_computation.11 | async-start | bytes 524288 | tf_op jit(solution)/shard_map/all_to_all | solution.py:43
  276.9 17.5 %all-to-all-done.11 = f32[16,1,2,1,8,192]{5,2,4,3,1,0:T(2,128)S(1)} async-done(((f32[16,1,2,1,8,192]{5,2,4,3,1,0:T(2,128)}), f32[16,1,2,1,8,192]{5,2,4,3,1,0:T(2,128)S(1)}, u32[]{:S(2)}, u32[]{:S(2)}) %all-to-all-start.11) | async-done | bytes 196640 | tf_op jit(solution)/shard_map/all_to_all | solution.py:43
  294.3 3.4 all-to-all-start.13
  297.8 7.3 %all-to-all-done.13 = f32[8,1,2,1,16,192]{5,2,4,3,1,0:T(2,128)S(1)} async-done(((f32[8,1,2,1,16,192]{5,2,4,3,1,0:T(2,128)}), f32[8,1,2,1,16,192]{5,2,4,3,1,0:T(2,128)S(1)}, u32[]{:S(2)}, u32[]{:S(2)}) %all-to-all-start.13) | async-done | bytes 196640 | tf_op jit(solution)/shard_map/all_to_all | solution.py:43
  305.8 3.4 all-to-all-start.12
  309.3 5.9 %all-to-all-done.12 = f32[8,1,2,1,8,192]{5,4,3,2,1,0:T(8,128)S(1)} async-done(((f32[8,1,2,1,8,192]{5,4,3,2,1,0:T(8,128)}), f32[8,1,2,1,8,192]{5,4,3,2,1,0:T(8,128)S(1)}, u32[]{:S(2)}, u32[]{:S(2)}) %all-to-all-start.12) | async-done | bytes 98336 | tf_op jit(solution)/shard_map/all_to_all | solution.py:49
  316.1 4.7 all-to-all-start.14
  320.9 27.6 %all-to-all-done.14 = f32[16,1,2,1,16,192]{5,4,3,2,1,0:T(8,128)S(1)} async-done(((f32[16,1,2,1,16,192]{5,4,3,2,1,0:T(8,128)}), f32[16,1,2,1,16,192]{5,4,3,2,1,0:T(8,128)S(1)}, u32[]{:S(2)}, u32[]{:S(2)}) %all-to-all-start.14) | async-done | bytes 393248 | tf_op jit(solution)/shard_map/all_to_all | solution.py:49
  356.7 3.2 collective-permute-start.15
  359.9 9.0 %collective-permute-start.14 = (f32[1,18,1,192]{3,0,2,1:T(1,128)S(1)}, f32[1,18,1,192]{3,0,2,1:T(1,128)S(1)}, u32[]{:S(2)}, u32[]{:S(2)}) collective-permute-start(f32[1,18,1,192]{3,0,2,1:T(1,128)S(1)} %get-tuple-element.252), channel_id=1, source_target_pairs={{0,1},{1,2},{2,3},{3,4},{4,5},{5,6},{6,7},{7,8},{8,9},{9,10},{10,1... | collective-permute-start | bytes 41480 | tf_op jit(solution)/shard_map/ppermute | solution.py:19
  368.8 3.9 collective-permute-done.14
  373.5 14.7 %all_to_all.129 = f32[6,1,24,192]{3,2,1,0:T(8,128)S(1)} all-to-all(f32[6,1,24,192]{3,2,1,0:T(8,128)S(1)} %pad_maximum_fusion.29), channel_id=1, replica_groups=mesh['face'=6,'fy'=8,'fx'=16] {'face'}, dimensions={0} | all-to-all | bytes 221184 | tf_op jit(solution)/shard_map/all_to_all | solution.py:31
  390.8 8.5 %all-to-all-start.16 = ((f32[16,1,2,1,8,192]{5,2,4,3,1,0:T(2,128)}), f32[16,1,2,1,8,192]{5,2,4,3,1,0:T(2,128)S(1)}, u32[]{:S(2)}, u32[]{:S(2)}) async-start(f32[16,1,2,1,8,192]{5,2,4,3,1,0:T(2,128)} %bitcast.127), calls=%async_computation.16 | async-start | bytes 524288 | tf_op jit(solution)/shard_map/all_to_all | solution.py:43
  400.3 17.4 %all-to-all-done.16 = f32[16,1,2,1,8,192]{5,2,4,3,1,0:T(2,128)S(1)} async-done(((f32[16,1,2,1,8,192]{5,2,4,3,1,0:T(2,128)}), f32[16,1,2,1,8,192]{5,2,4,3,1,0:T(2,128)S(1)}, u32[]{:S(2)}, u32[]{:S(2)}) %all-to-all-start.16) | async-done | bytes 196640 | tf_op jit(solution)/shard_map/all_to_all | solution.py:43
  417.8 3.4 all-to-all-start.18
  421.3 7.3 %all-to-all-done.18 = f32[8,1,2,1,16,192]{5,2,4,3,1,0:T(2,128)S(1)} async-done(((f32[8,1,2,1,16,192]{5,2,4,3,1,0:T(2,128)}), f32[8,1,2,1,16,192]{5,2,4,3,1,0:T(2,128)S(1)}, u32[]{:S(2)}, u32[]{:S(2)}) %all-to-all-start.18) | async-done | bytes 196640 | tf_op jit(solution)/shard_map/all_to_all | solution.py:43
  429.3 3.4 all-to-all-start.17
  432.8 5.9 %all-to-all-done.17 = f32[8,1,2,1,8,192]{5,4,3,2,1,0:T(8,128)S(1)} async-done(((f32[8,1,2,1,8,192]{5,4,3,2,1,0:T(8,128)}), f32[8,1,2,1,8,192]{5,4,3,2,1,0:T(8,128)S(1)}, u32[]{:S(2)}, u32[]{:S(2)}) %all-to-all-start.17) | async-done | bytes 98336 | tf_op jit(solution)/shard_map/all_to_all | solution.py:49
  439.6 4.7 all-to-all-start.19
  444.4 27.6 %all-to-all-done.19 = f32[16,1,2,1,16,192]{5,4,3,2,1,0:T(8,128)S(1)} async-done(((f32[16,1,2,1,16,192]{5,4,3,2,1,0:T(8,128)}), f32[16,1,2,1,16,192]{5,4,3,2,1,0:T(8,128)S(1)}, u32[]{:S(2)}, u32[]{:S(2)}) %all-to-all-start.19) | async-done | bytes 393248 | tf_op jit(solution)/shard_map/all_to_all | solution.py:49
  (288 shorter events, 63.1 us)
Async XLA Ops:
  0.0 1.1 copy-start
  1.1 0.7 copy-start.4
  1.8 0.7 copy-start.3
  3.3 0.7 copy-start.1
  4.3 0.7 copy-start.2
  5.0 0.7 copy-start.5
  6.5 0.7 copy-start.8
  9.8 64.8 %collective-permute-start.1 = (f32[1,1,8,192]{3,0,2,1:T(1,128)S(1)}, f32[1,1,8,192]{3,0,2,1:T(1,128)S(1)}, u32[]{:S(2)}, u32[]{:S(2)}) collective-permute-start(f32[1,1,8,192]{3,0,2,1:T(1,128)S(1)} %get-tuple-element.267), channel_id=1, source_target_pairs={{16,0},{32,16},{48,32},{64,48},{80,64},{96,80},{112,96},{17,1},{33... | collective-permute-start | bytes 18440 | tf_op jit(solution)/shard_map/ppermute | solution.py:21
  11.1 63.5 %collective-permute-start = (f32[1,1,8,192]{3,0,2,1:T(1,128)S(1)}, f32[1,1,8,192]{3,0,2,1:T(1,128)S(1)}, u32[]{:S(2)}, u32[]{:S(2)}) collective-permute-start(f32[1,1,8,192]{3,0,2,1:T(1,128)S(1)} %get-tuple-element.266), channel_id=1, source_target_pairs={{0,16},{16,32},{32,48},{48,64},{64,80},{80,96},{96,112},{1,17},{17... | collective-permute-start | bytes 18440 | tf_op jit(solution)/shard_map/ppermute | solution.py:19
  14.2 7.7 %collective-permute-start.5 = (f32[1,1,8,1]{1,2,3,0:T(8,128)S(1)}, f32[1,1,8,1]{1,2,3,0:T(8,128)S(1)}, u32[]{:S(2)}, u32[]{:S(2)}) collective-permute-start(f32[1,1,8,1]{1,2,3,0:T(8,128)S(1)} %get-tuple-element.283), channel_id=1, source_target_pairs={{16,0},{32,16},{48,32},{64,48},{80,64},{96,80},{112,96},{17,1},{33... | collective-permute-start | bytes 104 | tf_op jit(solution)/shard_map/ppermute | solution.py:21
  15.5 4.4 copy-start.7
  15.5 6.4 %collective-permute-start.4 = (f32[1,1,8,1]{1,2,3,0:T(8,128)S(1)}, f32[1,1,8,1]{1,2,3,0:T(8,128)S(1)}, u32[]{:S(2)}, u32[]{:S(2)}) collective-permute-start(f32[1,1,8,1]{1,2,3,0:T(8,128)S(1)} %get-tuple-element.282), channel_id=1, source_target_pairs={{0,16},{16,32},{32,48},{48,64},{64,80},{80,96},{96,112},{1,17},{17... | collective-permute-start | bytes 104 | tf_op jit(solution)/shard_map/ppermute | solution.py:19
  19.2 0.7 copy-start.6
  21.9 16.2 %collective-permute-start.7 = (f32[1,18,1,1]{1,2,3,0:T(1,128)S(1)}, f32[1,18,1,1]{1,2,3,0:T(1,128)S(1)}, u32[]{:S(2)}, u32[]{:S(2)}) collective-permute-start(f32[1,18,1,1]{1,2,3,0:T(1,128)S(1)} %get-tuple-element.281), channel_id=1, source_target_pairs={{1,0},{2,1},{3,2},{4,3},{5,4},{6,5},{7,6},{8,7},{9,8},{10,9},{11,1... | collective-permute-start | bytes 224 | tf_op jit(solution)/shard_map/ppermute | solution.py:21
  36.1 12.7 %collective-permute-start.6 = (f32[1,18,1,1]{1,2,3,0:T(1,128)S(1)}, f32[1,18,1,1]{1,2,3,0:T(1,128)S(1)}, u32[]{:S(2)}, u32[]{:S(2)}) collective-permute-start(f32[1,18,1,1]{1,2,3,0:T(1,128)S(1)} %get-tuple-element.280), channel_id=1, source_target_pairs={{0,1},{1,2},{2,3},{3,4},{4,5},{5,6},{6,7},{7,8},{8,9},{9,10},{10,1... | collective-permute-start | bytes 224 | tf_op jit(solution)/shard_map/ppermute | solution.py:19
  49.9 14.0 %all-to-all-start.5 = ((f32[6,1,24,1]{2,3,1,0:T(1,128)}), f32[6,1,24,1]{2,3,1,0:T(1,128)S(1)}, u32[]{:S(2)}, u32[]{:S(2)}) async-start(f32[6,1,24,1]{2,3,1,0:T(1,128)} %pad_maximum_fusion.45), calls=%async_computation.5 | async-start | bytes 6144 | tf_op jit(solution)/shard_map/all_to_all | solution.py:31
  65.7 22.7 %all-to-all-start.6 = ((f32[16,1,2,1,8,1]{4,2,5,3,1,0:T(2,128)}), f32[16,1,2,1,8,1]{4,2,5,3,1,0:T(2,128)S(1)}, u32[]{:S(2)}, u32[]{:S(2)}) async-start(f32[16,1,2,1,8,1]{4,2,5,3,1,0:T(2,128)} %copy.327), calls=%async_computation.6 | async-start | bytes 32768 | tf_op jit(solution)/shard_map/all_to_all | solution.py:43
  74.8 18.1 %collective-permute-start.3 = (f32[1,18,1,192]{3,0,2,1:T(1,128)S(1)}, f32[1,18,1,192]{3,0,2,1:T(1,128)S(1)}, u32[]{:S(2)}, u32[]{:S(2)}) collective-permute-start(f32[1,18,1,192]{3,0,2,1:T(1,128)S(1)} %get-tuple-element.261), channel_id=1, source_target_pairs={{1,0},{2,1},{3,2},{4,3},{5,4},{6,5},{7,6},{8,7},{9,8},{10,9},{11,1... | collective-permute-start | bytes 41480 | tf_op jit(solution)/shard_map/ppermute | solution.py:21
  84.5 13.2 %collective-permute-start.2 = (f32[1,18,1,192]{3,0,2,1:T(1,128)S(1)}, f32[1,18,1,192]{3,0,2,1:T(1,128)S(1)}, u32[]{:S(2)}, u32[]{:S(2)}) collective-permute-start(f32[1,18,1,192]{3,0,2,1:T(1,128)S(1)} %get-tuple-element.260), channel_id=1, source_target_pairs={{0,1},{1,2},{2,3},{3,4},{4,5},{5,6},{6,7},{7,8},{8,9},{9,10},{10,1... | collective-permute-start | bytes 41480 | tf_op jit(solution)/shard_map/ppermute | solution.py:19
  88.5 10.0 %all-to-all-start.8 = ((f32[8,1,2,1,16,1]{4,2,5,3,1,0:T(2,128)}), f32[8,1,2,1,16,1]{4,2,5,3,1,0:T(2,128)S(1)}, u32[]{:S(2)}, u32[]{:S(2)}) async-start(f32[8,1,2,1,16,1]{4,2,5,3,1,0:T(2,128)} %bitcast.376), calls=%async_computation.8 | async-start | bytes 16384 | tf_op jit(solution)/shard_map/all_to_all | solution.py:43
  99.1 10.0 %all-to-all-start.7 = ((f32[8,1,2,1,8,1]{4,2,5,3,1,0:T(2,128)}), f32[8,1,2,1,8,1]{4,2,5,3,1,0:T(2,128)S(1)}, u32[]{:S(2)}, u32[]{:S(2)}) async-start(f32[8,1,2,1,8,1]{4,2,5,3,1,0:T(2,128)} %broadcast_in_dim.63), calls=%async_computation.7 | async-start | bytes 16384 | tf_op jit(solution)/shard_map/all_to_all | solution.py:49
  109.2 13.1 %all-to-all-start = ((f32[6,1,24,192]{3,2,1,0:T(8,128)}), f32[6,1,24,192]{3,2,1,0:T(8,128)S(1)}, u32[]{:S(2)}, u32[]{:S(2)}) async-start(f32[6,1,24,192]{3,2,1,0:T(8,128)} %pad_maximum_fusion.25), calls=%async_computation | async-start | bytes 294912 | tf_op jit(solution)/shard_map/all_to_all | solution.py:31
  122.9 26.3 %all-to-all-start.9 = ((f32[16,1,2,1,16,1]{4,2,5,3,1,0:T(2,128)}), f32[16,1,2,1,16,1]{4,2,5,3,1,0:T(2,128)S(1)}, u32[]{:S(2)}, u32[]{:S(2)}) async-start(f32[16,1,2,1,16,1]{4,2,5,3,1,0:T(2,128)} %broadcast_in_dim.65), calls=%async_computation.9 | async-start | bytes 32768 | tf_op jit(solution)/shard_map/all_to_all | solution.py:49
  149.2 22.5 %all-to-all-start.1 = ((f32[16,1,2,1,8,192]{5,2,4,3,1,0:T(2,128)}), f32[16,1,2,1,8,192]{5,2,4,3,1,0:T(2,128)S(1)}, u32[]{:S(2)}, u32[]{:S(2)}) async-start(f32[16,1,2,1,8,192]{5,2,4,3,1,0:T(2,128)} %bitcast.32), calls=%async_computation.1 | async-start | bytes 524288 | tf_op jit(solution)/shard_map/all_to_all | solution.py:43
  171.8 10.8 %all-to-all-start.3 = ((f32[8,1,2,1,16,192]{5,2,4,3,1,0:T(2,128)}), f32[8,1,2,1,16,192]{5,2,4,3,1,0:T(2,128)S(1)}, u32[]{:S(2)}, u32[]{:S(2)}) async-start(f32[8,1,2,1,16,192]{5,2,4,3,1,0:T(2,128)} %bitcast.39), calls=%async_computation.3 | async-start | bytes 524288 | tf_op jit(solution)/shard_map/all_to_all | solution.py:43
  183.3 9.4 %all-to-all-start.2 = ((f32[8,1,2,1,8,192]{5,4,3,2,1,0:T(8,128)}), f32[8,1,2,1,8,192]{5,4,3,2,1,0:T(8,128)S(1)}, u32[]{:S(2)}, u32[]{:S(2)}) async-start(f32[8,1,2,1,8,192]{5,4,3,2,1,0:T(8,128)} %broadcast_in_dim.55), calls=%async_computation.2 | async-start | bytes 262144 | tf_op jit(solution)/shard_map/all_to_all | solution.py:49
  193.6 33.2 %all-to-all-start.4 = ((f32[16,1,2,1,16,192]{5,4,3,2,1,0:T(8,128)}), f32[16,1,2,1,16,192]{5,4,3,2,1,0:T(8,128)S(1)}, u32[]{:S(2)}, u32[]{:S(2)}) async-start(f32[16,1,2,1,16,192]{5,4,3,2,1,0:T(8,128)} %broadcast_in_dim.57), calls=%async_computation.4 | async-start | bytes 1048576 | tf_op jit(solution)/shard_map/all_to_all | solution.py:49
  229.9 4.3 collective-permute-start.9
  231.2 3.8 collective-permute-start.8
  235.2 12.2 %collective-permute-start.11 = (f32[1,18,1,192]{3,0,2,1:T(1,128)S(1)}, f32[1,18,1,192]{3,0,2,1:T(1,128)S(1)}, u32[]{:S(2)}, u32[]{:S(2)}) collective-permute-start(f32[1,18,1,192]{3,0,2,1:T(1,128)S(1)} %get-tuple-element.257), channel_id=1, source_target_pairs={{1,0},{2,1},{3,2},{4,3},{5,4},{6,5},{7,6},{8,7},{9,8},{10,9},{11,1... | collective-permute-start | bytes 41480 | tf_op jit(solution)/shard_map/ppermute | solution.py:21
  238.3 12.9 %collective-permute-start.10 = (f32[1,18,1,192]{3,0,2,1:T(1,128)S(1)}, f32[1,18,1,192]{3,0,2,1:T(1,128)S(1)}, u32[]{:S(2)}, u32[]{:S(2)}) collective-permute-start(f32[1,18,1,192]{3,0,2,1:T(1,128)S(1)} %get-tuple-element.256), channel_id=1, source_target_pairs={{0,1},{1,2},{2,3},{3,4},{4,5},{5,6},{6,7},{7,8},{8,9},{9,10},{10,1... | collective-permute-start | bytes 41480 | tf_op jit(solution)/shard_map/ppermute | solution.py:19
  266.1 28.2 %all-to-all-start.11 = ((f32[16,1,2,1,8,192]{5,2,4,3,1,0:T(2,128)}), f32[16,1,2,1,8,192]{5,2,4,3,1,0:T(2,128)S(1)}, u32[]{:S(2)}, u32[]{:S(2)}) async-start(f32[16,1,2,1,8,192]{5,2,4,3,1,0:T(2,128)} %bitcast.93), calls=%async_computation.11 | async-start | bytes 524288 | tf_op jit(solution)/shard_map/all_to_all | solution.py:43
  294.3 10.8 %all-to-all-start.13 = ((f32[8,1,2,1,16,192]{5,2,4,3,1,0:T(2,128)}), f32[8,1,2,1,16,192]{5,2,4,3,1,0:T(2,128)S(1)}, u32[]{:S(2)}, u32[]{:S(2)}) async-start(f32[8,1,2,1,16,192]{5,2,4,3,1,0:T(2,128)} %bitcast.99), calls=%async_computation.13 | async-start | bytes 524288 | tf_op jit(solution)/shard_map/all_to_all | solution.py:43
  305.8 9.4 %all-to-all-start.12 = ((f32[8,1,2,1,8,192]{5,4,3,2,1,0:T(8,128)}), f32[8,1,2,1,8,192]{5,4,3,2,1,0:T(8,128)S(1)}, u32[]{:S(2)}, u32[]{:S(2)}) async-start(f32[8,1,2,1,8,192]{5,4,3,2,1,0:T(8,128)} %broadcast_in_dim.67), calls=%async_computation.12 | async-start | bytes 262144 | tf_op jit(solution)/shard_map/all_to_all | solution.py:49
  316.1 32.4 %all-to-all-start.14 = ((f32[16,1,2,1,16,192]{5,4,3,2,1,0:T(8,128)}), f32[16,1,2,1,16,192]{5,4,3,2,1,0:T(8,128)S(1)}, u32[]{:S(2)}, u32[]{:S(2)}) async-start(f32[16,1,2,1,16,192]{5,4,3,2,1,0:T(8,128)} %broadcast_in_dim.68), calls=%async_computation.14 | async-start | bytes 1048576 | tf_op jit(solution)/shard_map/all_to_all | solution.py:49
  351.3 4.3 collective-permute-start.13
  352.6 3.8 collective-permute-start.12
  356.7 12.2 %collective-permute-start.15 = (f32[1,18,1,192]{3,0,2,1:T(1,128)S(1)}, f32[1,18,1,192]{3,0,2,1:T(1,128)S(1)}, u32[]{:S(2)}, u32[]{:S(2)}) collective-permute-start(f32[1,18,1,192]{3,0,2,1:T(1,128)S(1)} %get-tuple-element.253), channel_id=1, source_target_pairs={{1,0},{2,1},{3,2},{4,3},{5,4},{6,5},{7,6},{8,7},{9,8},{10,9},{11,1... | collective-permute-start | bytes 41480 | tf_op jit(solution)/shard_map/ppermute | solution.py:21
  359.9 12.9 %collective-permute-start.14 = (f32[1,18,1,192]{3,0,2,1:T(1,128)S(1)}, f32[1,18,1,192]{3,0,2,1:T(1,128)S(1)}, u32[]{:S(2)}, u32[]{:S(2)}) collective-permute-start(f32[1,18,1,192]{3,0,2,1:T(1,128)S(1)} %get-tuple-element.252), channel_id=1, source_target_pairs={{0,1},{1,2},{2,3},{3,4},{4,5},{5,6},{6,7},{7,8},{8,9},{9,10},{10,1... | collective-permute-start | bytes 41480 | tf_op jit(solution)/shard_map/ppermute | solution.py:19
  390.8 26.9 %all-to-all-start.16 = ((f32[16,1,2,1,8,192]{5,2,4,3,1,0:T(2,128)}), f32[16,1,2,1,8,192]{5,2,4,3,1,0:T(2,128)S(1)}, u32[]{:S(2)}, u32[]{:S(2)}) async-start(f32[16,1,2,1,8,192]{5,2,4,3,1,0:T(2,128)} %bitcast.127), calls=%async_computation.16 | async-start | bytes 524288 | tf_op jit(solution)/shard_map/all_to_all | solution.py:43
  417.8 10.8 %all-to-all-start.18 = ((f32[8,1,2,1,16,192]{5,2,4,3,1,0:T(2,128)}), f32[8,1,2,1,16,192]{5,2,4,3,1,0:T(2,128)S(1)}, u32[]{:S(2)}, u32[]{:S(2)}) async-start(f32[8,1,2,1,16,192]{5,2,4,3,1,0:T(2,128)} %bitcast.133), calls=%async_computation.18 | async-start | bytes 524288 | tf_op jit(solution)/shard_map/all_to_all | solution.py:43
  429.3 9.4 %all-to-all-start.17 = ((f32[8,1,2,1,8,192]{5,4,3,2,1,0:T(8,128)}), f32[8,1,2,1,8,192]{5,4,3,2,1,0:T(8,128)S(1)}, u32[]{:S(2)}, u32[]{:S(2)}) async-start(f32[8,1,2,1,8,192]{5,4,3,2,1,0:T(8,128)} %broadcast_in_dim.69), calls=%async_computation.17 | async-start | bytes 262144 | tf_op jit(solution)/shard_map/all_to_all | solution.py:49
  439.6 32.4 %all-to-all-start.19 = ((f32[16,1,2,1,16,192]{5,4,3,2,1,0:T(8,128)}), f32[16,1,2,1,16,192]{5,4,3,2,1,0:T(8,128)S(1)}, u32[]{:S(2)}, u32[]{:S(2)}) async-start(f32[16,1,2,1,16,192]{5,4,3,2,1,0:T(8,128)} %broadcast_in_dim.70), calls=%async_computation.19 | async-start | bytes 1048576 | tf_op jit(solution)/shard_map/all_to_all | solution.py:49
where the time goes:
time: 475 us; the launch traced here: 473 us
  waiting for transfers between devices  230 us (48%)
  starting transfers between devices  170 us (36%)
  blocking collectives  26.2 us (6%)
  local copies, waits for them, and re-layouts  19.9 us (4%)
  other arithmetic  19.5 us (4%)
  matrix products  5.55 us (1%)
    all_to_all x8, waiting for transfers between devices, copy_for_each(): lax.all_to_all(jnp.broadcast_to(shard[None], (devices, *shard.shape)), ax...  117 us
    all_to_all x8, waiting for transfers between devices, summed_on_arrival(): lax.all_to_all(tiles, axis, split_axis=0, concat_axis=0, tiled=True)  74.1 us
    all_to_all x8, starting transfers between devices, summed_on_arrival(): lax.all_to_all(tiles, axis, split_axis=0, concat_axis=0, tiled=True)  46.4 us
    all_to_all x8, starting transfers between devices, copy_for_each(): lax.all_to_all(jnp.broadcast_to(shard[None], (devices, *shard.shape)), ax...  41.8 us
    ppermute x8, starting transfers between devices, padded_2(): lax.ppermute(tail, axis, [(i, (i + 1) % count) for i in range(ends)])  35.3 us
    ppermute x8, starting transfers between devices, padded_2(): lax.ppermute(head, axis, [((i + 1) % count, i) for i in range(ends)])  35.2 us
    all_to_all x2, blocking collectives, sent_together(): lax.all_to_all(both, axis, split_axis=split_dim, concat_axis=concat_dim,...  26.2 us
    ppermute x8, waiting for transfers between devices, padded_2(): lax.ppermute(tail, axis, [(i, (i + 1) % count) for i in range(ends)])  24.7 us
  transfers between devices with their start and end apart: 34, of which 23 were waited for; matrix products, arithmetic and copies ran while one was open for 3% of the time, Pallas kernels for 0%

commit v1 on v0

v1 whole, which is shorter than its diff:
```python
import functools

import jax
import jax.numpy as jnp
import numpy as np
from jax import lax
from jax.experimental import pallas as pl
from jax.experimental.pallas import tpu as pltpu
from jax.sharding import PartitionSpec as P

time_step = 0.05
hyper_coeff = 0.0005

FACES = 6
ROWS = 128
LANES = 128
EDGES = 4


def deriv_table():
    gll_nodes = np.array([-1.0, -1.0 / np.sqrt(5.0), 1.0 / np.sqrt(5.0), 1.0])
    bary_weights = np.ones(4)
    for j in range(4):
        for m in range(4):
            if m != j:
                bary_weights[j] = bary_weights[j] / (gll_nodes[j] - gll_nodes[m])
    matrix = np.zeros((4, 4))
    for i in range(4):
        for j in range(4):
            if i != j:
                matrix[i, j] = bary_weights[j] / bary_weights[i] / (gll_nodes[i] - gll_nodes[j])
        matrix[i, i] = -np.sum(matrix[i])
    return matrix


def deriv_operands():
    table = deriv_table()
    along_x = np.kron(np.eye(32), table.T)
    along_y = np.kron(np.kron(np.eye(4), table.T), np.eye(8))
    return along_x.astype(np.float32), along_y.astype(np.float32)


def roll(values, shift, axis):
    return pltpu.roll(values, shift % values.shape[axis], axis)


def iota(shape, dim):
    return lax.broadcasted_iota(jnp.int32, shape, dim)


def dot(a, b):
    return jnp.dot(a, b, precision=lax.Precision.HIGHEST, preferred_element_type=jnp.float32)


def dot_t(a, b):
    return lax.dot_general(
        a,
        b,
        (((1,), (1,)), ((), ())),
        precision=lax.Precision.HIGHEST,
        preferred_element_type=jnp.float32,
    )


def stacked(parts, axis=0):
    return jnp.concatenate(parts, axis=axis)


def gll_weight(position):
    return jnp.where((position % 4 == 0) | (position % 4 == 3), 1.0 / 6.0, 5.0 / 6.0)


def mass_weight():
    lane = iota((1, LANES), 1)
    return gll_weight(lane // 8) * gll_weight(lane % 8)


def in_face(field):
    lane = iota((ROWS, LANES), 1)
    col_block = iota((ROWS, LANES), 0) % 16
    c = lane % 8
    r = lane // 8
    before = roll(field, 1, 1)
    after = roll(field, -1, 1)
    before_block = roll(roll(field, 1, 0), -7, 1)
    after_block = roll(roll(field, -1, 0), 7, 1)
    summed = field + jnp.where(
        c == 4, before, jnp.where((c == 0) & (col_block > 0), before_block, 0.0)
    )
    summed = summed + jnp.where(
        c == 3, after, jnp.where((c == 7) & (col_block < 15), after_block, 0.0)
    )
    above = roll(summed, 8, 1)
    below = roll(summed, -8, 1)
    edge_rows = jnp.zeros((16, LANES), jnp.float32)
    above_block = stacked([edge_rows, above[: ROWS - 16]])
    below_block = stacked([below[16:], edge_rows])
    total = summed + jnp.where(
        r == 0, above_block, jnp.where(r % 4 == 0, above, 0.0)
    )
    return total + jnp.where(r == 15, below_block, jnp.where(r % 4 == 3, below, 0.0))


def rim_tables(edge):
    lane = iota((LANES, LANES), 0)
    k = iota((LANES, LANES), 1)
    count = 16 if edge in (0, 2) else 8
    block = iota((count, LANES), 0)
    at = iota((count, LANES), 1)
    if edge == 0:
        hit, mask = lane == k % 8, block == at // 8
    elif edge == 1:
        hit, mask = lane == 8 * (k % 16) + 7, block == at // 16
    elif edge == 2:
        hit, mask = lane == 127 - k % 8, block == 15 - at // 8
    else:
        hit, mask = lane == 8 * (15 - k % 16), block == 7 - at // 16
    return jnp.where(hit, 1.0, 0.0), jnp.where(mask, 1.0, 0.0)


def rim_rows(edge):
    if edge == 0:
        return pl.ds(0, 16)
    if edge == 1:
        return pl.ds(15, 8, 16)
    if edge == 2:
        return pl.ds(112, 16)
    return pl.ds(0, 8, 16)


def shifted_rows(edge, channel):
    rows = rim_rows(edge)
    return pl.ds(rows.start + ROWS * channel, rows.size, rows.stride)


def turned(u, v, quarter):
    quarter = quarter % 4
    if quarter == 0:
        return u, v
    if quarter == 1:
        return -v, u
    if quarter == 2:
        return -u, -v
    return v, -u


def put_rims(summed_ref, channels, nbr_ref, face, send_ref):
    rims = []
    for edge in range(EDGES):
        spread, mask = rim_tables(edge)
        count = mask.shape[0]
        rows = stacked([summed_ref[shifted_rows(edge, ch), :] for ch in range(channels)])
        spread_rows = dot(rows, spread)
        vectors = [
            jnp.sum(spread_rows[ch * count : (ch + 1) * count] * mask, axis=0, keepdims=True)
            for ch in range(channels)
        ]
        u, v = turned(vectors[0], vectors[1], -edge)
        pad = [jnp.zeros((8 - channels, LANES), jnp.float32)]
        rims.append(stacked([u, v, *vectors[2:], *pad]))
    for other in range(FACES):
        slot = jnp.zeros((8, LANES), jnp.float32)
        for edge in range(EDGES):
            glued = jnp.where(nbr_ref[face, edge] == other, 1.0, 0.0).astype(jnp.float32)
            slot = slot + glued * rims[edge]
        send_ref[8 * other : 8 * other + 8, :] = slot


def add_rims(total_ref, channels, nbr_ref, face, got_ref):
    flip = jnp.where(iota((LANES, LANES), 0) + iota((LANES, LANES), 1) == 127, 1.0, 0.0)
    got = stacked(
        [got_ref[pl.ds(pl.multiple_of(8 * nbr_ref[face, edge], 8), 8), :] for edge in range(EDGES)]
    )
    got = dot(got, flip)
    for edge in range(EDGES):
        rim = got[8 * edge : 8 * edge + 8]
        u, v = turned(rim[0:1], rim[1:2], edge + 2)
        vectors = [u, v] + [rim[ch : ch + 1] for ch in range(2, channels)]
        spread, mask = rim_tables(edge)
        count = mask.shape[0]
        placed = dot_t(stacked([vector * mask for vector in vectors]), spread)
        for ch in range(channels):
            rows = shifted_rows(edge, ch)
            total_ref[rows, :] = total_ref[rows, :] + placed[ch * count : (ch + 1) * count]


def pack_kernel(state_ref, jac_ref, diag_ref, cross_ref, cor_ref, out_ref):
    turned_state = jnp.transpose(state_ref[...])
    for part in range(3):
        out_ref[pl.ds(part, 64, 8), :] = turned_state[64 * part : 64 * part + 64]
    spread = jnp.where(iota((8, LANES), 1) % 8 == iota((8, LANES), 0), 1.0, 0.0)
    mask = jnp.where(iota((16, LANES), 1) // 8 == iota((16, LANES), 0), 1.0, 0.0)
    fields = [jac_ref[...], diag_ref[0], diag_ref[1], cross_ref[...], cor_ref[...]]
    lines = dot(stacked(fields), spread)
    for k in range(5):
        line = jnp.sum(lines[16 * k : 16 * k + 16] * mask, axis=0, keepdims=True)
        out_ref[pl.ds(3 + k, 64, 8), :] = jnp.broadcast_to(line, (64, LANES))


def first_kernel(nbr_ref, own_ref, other_ref, dx_ref, dy_ref, summed_ref, geometry_ref, send_ref):
    core = lax.axis_index("fy") % 2
    face = lax.axis_index("face")
    fields = []
    for k in range(8):
        own = own_ref[pl.ds(k, 64, 8), :]
        other = other_ref[pl.ds(k, 64, 8), :]
        even = jnp.where(core == 0, own, other)
        odd = jnp.where(core == 0, other, own)
        pieces = []
        for x in range(4):
            pieces += [even[16 * x : 16 * x + 16], odd[16 * x : 16 * x + 16]]
        fields.append(stacked(pieces))
    u, v, t, volume, m_xx, m_yy, m_xy, planet = fields
    contra_u = m_xx * u + m_xy * v
    contra_v = m_xy * u + m_yy * v
    energy = 0.5 * (u * contra_u + v * contra_v) + t
    x_derivs = dot(stacked([v, t, energy]), dx_ref[...])
    y_derivs = dot(stacked([u, t, energy]), dy_ref[...])
    dx_v, dx_t, dx_e = x_derivs[:ROWS], x_derivs[ROWS : 2 * ROWS], x_derivs[2 * ROWS :]
    dy_u, dy_t, dy_e = y_derivs[:ROWS], y_derivs[ROWS : 2 * ROWS], y_derivs[2 * ROWS :]
    absolute = (dx_v - dy_u) / volume + planet
    mass = mass_weight() * volume
    raw_u = u + time_step * (absolute * volume * contra_v - dx_e)
    raw_v = v + time_step * (-absolute * volume * contra_u - dy_e)
    raw_t = t - time_step * (contra_u * dx_t + contra_v * dy_t)
    for ch, field in enumerate([mass * raw_u, mass * raw_v, mass * raw_t, mass]):
        summed_ref[ROWS * ch : ROWS * ch + ROWS, :] = in_face(field)
    for k, field in enumerate([volume, m_xx, m_yy, m_xy]):
        geometry_ref[ROWS * k : ROWS * k + ROWS, :] = field
    put_rims(summed_ref, 4, nbr_ref, face, send_ref)


def laplace(fields, geometry_ref, dx_ref, dy_ref):
    volume, m_xx, m_yy, m_xy = [
        geometry_ref[ROWS * k : ROWS * k + ROWS, :] for k in range(4)
    ]
    along_x, along_y = dx_ref[...], dy_ref[...]
    values = stacked(fields)
    grad_x, grad_y = dot(values, along_x), dot(values, along_y)
    flux_x, flux_y = [], []
    for ch in range(3):
        part = slice(ROWS * ch, ROWS * ch + ROWS)
        flux_x.append(volume * (m_xx * grad_x[part] + m_xy * grad_y[part]))
        flux_y.append(volume * (m_xy * grad_x[part] + m_yy * grad_y[part]))
    spread = dot(stacked(flux_x), along_x) + dot(stacked(flux_y), along_y)
    mass = mass_weight() * volume
    return [mass * (spread[ROWS * ch : ROWS * ch + ROWS] / volume) for ch in range(3)]


def second_kernel(
    nbr_ref, got_ref, summed_ref, geometry_ref, dx_ref, dy_ref,
    sectioned_ref, mass_ref, next_ref, send_ref, total_ref,
):
    face = lax.axis_index("face")
    total_ref[...] = summed_ref[...]
    add_rims(total_ref, 4, nbr_ref, face, got_ref)
    total_mass = total_ref[3 * ROWS : 4 * ROWS, :]
    mass_ref[...] = total_mass
    fields = [total_ref[ROWS * ch : ROWS * ch + ROWS, :] / total_mass for ch in range(3)]
    for ch in range(3):
        sectioned_ref[ROWS * ch : ROWS * ch + ROWS, :] = fields[ch]
    for ch, field in enumerate(laplace(fields, geometry_ref, dx_ref, dy_ref)):
        next_ref[ROWS * ch : ROWS * ch + ROWS, :] = in_face(field)
    put_rims(next_ref, 3, nbr_ref, face, send_ref)


def third_kernel(
    nbr_ref, got_ref, summed_ref, mass_ref, geometry_ref, dx_ref, dy_ref,
    next_ref, send_ref, total_ref,
):
    face = lax.axis_index("face")
    total_ref[...] = summed_ref[...]
    add_rims(total_ref, 3, nbr_ref, face, got_ref)
    fields = [total_ref[ROWS * ch : ROWS * ch + ROWS, :] / mass_ref[...] for ch in range(3)]
    for ch, field in enumerate(laplace(fields, geometry_ref, dx_ref, dy_ref)):
        next_ref[ROWS * ch : ROWS * ch + ROWS, :] = in_face(field)
    put_rims(next_ref, 3, nbr_ref, face, send_ref)


def last_kernel(nbr_ref, got_ref, summed_ref, mass_ref, sectioned_ref, out_ref, total_ref):
    face = lax.axis_index("face")
    core = lax.axis_index("fy") % 2
    total_ref[...] = summed_ref[...]
    add_rims(total_ref, 3, nbr_ref, face, got_ref)
    for ch in range(3):
        part = pl.ds(ROWS * ch, ROWS)
        total_ref[part, :] = (
            sectioned_ref[part, :] - hyper_coeff * (total_ref[part, :] / mass_ref[...])
        )
    for x in range(4):
        for ch in range(3):
            start = pl.multiple_of(ROWS * ch + 32 * x + 16 * core, 16)
            out_ref[16 * x : 16 * x + 16, LANES * ch : LANES * ch + LANES] = total_ref[
                pl.ds(start, 16), :
            ]


def unpack_kernel(got_ref, out_ref):
    levels = got_ref[...]
    columns = stacked([levels[:, LANES * ch : LANES * ch + LANES] for ch in range(3)])
    out_ref[...] = jnp.transpose(columns)


def f32(*shape):
    return jax.ShapeDtypeStruct(shape, jnp.float32)


VMEM = pl.BlockSpec(memory_space=pltpu.VMEM)
SMEM = pl.BlockSpec(memory_space=pltpu.SMEM)


def call(kernel, outs, ins, scratch=(), name=None):
    return pl.pallas_call(
        kernel,
        out_shape=outs,
        in_specs=ins,
        out_specs=jax.tree.map(lambda _: VMEM, outs),
        scratch_shapes=scratch,
        name=name,
    )


def level_groups():
    return [
        [(8 * face + 2 * x + core) * 16 + fx for x in range(4) for fx in range(16)]
        for face in range(FACES)
        for core in range(2)
    ]


def per_device(state, jacobian, metric_diag, metric_cross, coriolis, nbr_face, nbr_edge):
    axes = ("face", "fy", "fx")
    groups = level_groups()
    along_x, along_y = deriv_operands()
    total = pltpu.VMEM((4 * ROWS, LANES), jnp.float32)
    total_3 = pltpu.VMEM((3 * ROWS, LANES), jnp.float32)

    packed = call(pack_kernel, f32(512, LANES), [VMEM] * 5, name="pack")(
        state.reshape(128, 192), jacobian[0], metric_diag[:, 0], metric_cross[0], coriolis[0]
    )
    own = lax.all_to_all(
        packed.reshape(64, 8, LANES), axes, 0, 0, axis_index_groups=groups, tiled=True
    )
    other = lax.ppermute(own, "fy", [(i, i ^ 1) for i in range(8)])

    def across(send):
        return lax.all_to_all(send.reshape(FACES, 8, LANES), "face", 0, 0, tiled=True).reshape(
            8 * FACES, LANES
        )

    send = f32(8 * FACES, LANES)
    summed, geometry, out = call(
        first_kernel,
        [f32(4 * ROWS, LANES), f32(4 * ROWS, LANES), send],
        [SMEM] + [VMEM] * 4,
        name="first",
    )(nbr_face, own.reshape(512, LANES), other.reshape(512, LANES), along_x, along_y)
    sectioned, total_mass, summed, out = call(
        second_kernel,
        [f32(3 * ROWS, LANES), f32(ROWS, LANES), f32(3 * ROWS, LANES), send],
        [SMEM] + [VMEM] * 5,
        [total],
        name="second",
    )(nbr_face, across(out), summed, geometry, along_x, along_y)
    summed, out = call(
        third_kernel,
        [f32(3 * ROWS, LANES), send],
        [SMEM] + [VMEM] * 6,
        [total_3],
        name="third",
    )(nbr_face, across(out), summed, total_mass, geometry, along_x, along_y)
    updated = call(
        last_kernel, f32(64, 3 * LANES), [SMEM] + [VMEM] * 4, [total_3], name="last"
    )(nbr_face, across(out), summed, total_mass, sectioned)
    back = lax.all_to_all(
        updated.reshape(64, 1, 3 * LANES), axes, 0, 0, axis_index_groups=groups, tiled=True
    )
    nodes = call(unpack_kernel, f32(128, 192), [VMEM], name="unpack")(
        back.reshape(64, 3 * LANES)
    )
    return nodes.reshape(1, 16, 8, 192)


def solution(mesh):
    return jax.shard_map(
        per_device,
        mesh=mesh,
        in_specs=(
            P("face", "fy", "fx", None),
            P("face", "fy", "fx"),
            P(None, "face", "fy", "fx"),
            P("face", "fy", "fx"),
            P("face", "fy", "fx"),
            P(),
            P(),
        ),
        out_specs=P("face", "fy", "fx", None),
        check_vma=False,
    )
```

time: 475 us -> 134 us (0.28)
  the two profiles are of different devices: /device:TPU:72 before, /device:TPU:2 now
where the time goes in v1:
time: 134 us; the launch traced here: 133 us
  blocking collectives  107 us (80%)
  Pallas kernels  17.7 us (13%)
  local copies, waits for them, and re-layouts  6.42 us (5%)
  starting transfers between devices  1.91 us (1%)
    all_to_all x3, blocking collectives, across(): lax.all_to_all(send.reshape(FACES, 8, LANES), 'face', 0, 0, tiled=True)  44.6 us
    all_to_all x1, blocking collectives, per_device(): lax.all_to_all(packed.reshape(64, 8, LANES), axes, 0, 0, axis_index_group...  39.9 us
    all_to_all x1, blocking collectives, per_device(): lax.all_to_all(updated.reshape(64, 1, 3 * LANES), axes, 0, 0, axis_index_...  22 us
    pallas_call x1, Pallas kernels, per_device(): call(second_kernel, [f32(3 * ROWS, LANES), f32(ROWS, LANES), f32(3 * ROWS...  4.46 us
    pallas_call x1, Pallas kernels, per_device(): call(third_kernel, [f32(3 * ROWS, LANES), send], [SMEM] + [VMEM] * 6, [to...  4.44 us
    pallas_call x1, Pallas kernels, per_device(): call(first_kernel, [f32(4 * ROWS, LANES), f32(4 * ROWS, LANES), send], [S...  2.85 us
    unnamed x15, local copies, waits for them, and re-layouts  2.73 us
  transfers between devices with their start and end apart: 1, of which 1 were waited for; matrix products, arithmetic and copies ran while one was open for 1% of the time, Pallas kernels for 0%

profile of v1, /device:TPU:2, one launch (start us, length us, event | category | flops | bytes accessed | tf_op | source)
XLA Modules:
  0.0 133.4 jit_solution(1060856992903943089)
XLA Ops:
  0.0 0.0 copy-start.3
  0.0 1.4 %copy.18.jac_ref = f32[16,8]{1,0:T(8,128)} copy(f32[16,8]{0,1:T(8,128)} %bitcast.32) | data formatting | bytes 1024 | tf_op jit(solution)/shard_map/squeeze | solution.py:339
  1.4 0.0 copy-done.3
  1.4 0.0 copy-start.4
  1.4 0.7 copy.19.cross_ref
  2.0 0.0 copy-start.2
  2.0 0.0 copy-done.4
  2.1 0.7 copy.20.cor_ref
  2.7 0.0 copy-done.2
  2.7 0.7 copy.17
  3.4 1.8 %pack.1 = f32[512,128]{1,0:T(8,128)} custom-call(f32[128,192]{1,0:T(8,128)} %bitcast.24, f32[16,8]{1,0:T(8,128)} %copy.18.jac_ref, f32[2,16,8]{2,1,0:T(8,128)} %bitcast.28, f32[16,8]{1,0:T(8,128)} %copy.19.cross_ref, f32[16,8]{1,0:T(8,128)} %copy.20.cor_ref), custom_call_target="tpu_custom_call" | custom-call | tf_op jit(solution)/shard_map/pack/pallas_call | solution.py:338
  5.3 0.0 copy-start.5
  5.3 39.9 %all_to_all.25 = f32[64,8,128]{2,1,0:T(8,128)S(1)} all-to-all(f32[64,8,128]{2,1,0:T(8,128)} %bitcast.20), channel_id=1, replica_groups={{0,1,2,3,4,5,6,7,8,9,10,11,12,13,14,15,32,33,34,35,36,37,38,39,40,41,42..., dimensions={0} | all-to-all | bytes 524288 | tf_op jit(solution)/shard_map/all_to_all | solution.py:341
  45.2 0.0 copy-start
  45.2 1.9 %collective-permute-start = (f32[64,8,128]{2,1,0:T(8,128)S(1)}, f32[64,8,128]{2,1,0:T(8,128)S(1)}, u32[]{:S(2)}, u32[]{:S(2)}) collective-permute-start(f32[64,8,128]{2,1,0:T(8,128)S(1)} %all_to_all.25), channel_id=1, source_target_pairs={{0,16},{16,0},{32,48},{48,32},{64,80},{80,64},{96,112},{112,96},{1... | collective-permute-start | bytes 786440 | tf_op jit(solution)/shard_map/ppermute | solution.py:344
  47.1 0.0 copy-done.5
  47.1 0.7 copy.24.nbr_ref
  47.8 0.8 collective-permute-done
  48.6 0.0 copy-start.1
  48.6 0.0 copy-done
  48.6 0.7 copy-done.1
  49.3 2.9 %first.1 = (f32[512,128]{1,0:T(8,128)}, f32[512,128]{1,0:T(8,128)}, f32[48,128]{1,0:T(8,128)}) custom-call(s32[6,4]{1,0:T(8,128)} %copy.24.nbr_ref, f32[512,128]{1,0:T(8,128)} %bitcast.19, f32[512,128]{1,0:T(8,128)} %bitcast.23, f32[128,128]{1,0:T(8,128)} %constant.4.clone.dx_ref, f32[128,128]{1,0:T(8,128)} %constant.5.clone.dy_ref), custom_call_target="tpu_custom_call" | custom-call | tf_op jit(solution)/shard_map/first/pallas_call | solution.py:352
  52.2 19.4 %all_to_all.26 = f32[6,8,128]{2,1,0:T(8,128)} all-to-all(f32[6,8,128]{2,1,0:T(8,128)} %bitcast.31), channel_id=1, replica_groups=mesh['face'=6,'fy'=8,'fx'=16] {'face'}, dimensions={0} | all-to-all | bytes 49152 | tf_op jit(solution)/shard_map/all_to_all | solution.py:347
  71.5 4.5 %second.1 = (f32[384,128]{1,0:T(8,128)}, f32[128,128]{1,0:T(8,128)}, f32[384,128]{1,0:T(8,128)}, f32[48,128]{1,0:T(8,128)}) custom-call(s32[6,4]{1,0:T(8,128)} %copy.24.nbr_ref, f32[48,128]{1,0:T(8,128)} %bitcast.26, f32[512,128]{1,0:T(8,128)} %get-tuple-element.15.summed_ref, f32[512,128]{1,0:T(8,128)} %get-tuple-element.16.geometry_ref, ...), custom_call_target="tpu_custom_call" | custom-call | tf_op jit(solution)/shard_map/second/pallas_call | solution.py:358
  76.0 12.6 %all_to_all.27 = f32[6,8,128]{2,1,0:T(8,128)} all-to-all(f32[6,8,128]{2,1,0:T(8,128)} %bitcast.30), channel_id=1, replica_groups=mesh['face'=6,'fy'=8,'fx'=16] {'face'}, dimensions={0} | all-to-all | bytes 49152 | tf_op jit(solution)/shard_map/all_to_all | solution.py:347
  88.6 4.4 %third.1 = (f32[384,128]{1,0:T(8,128)}, f32[48,128]{1,0:T(8,128)}) custom-call(s32[6,4]{1,0:T(8,128)} %copy.24.nbr_ref, f32[48,128]{1,0:T(8,128)} %bitcast.27, f32[384,128]{1,0:T(8,128)} %get-tuple-element.18.summed_ref, f32[128,128]{1,0:T(8,128)} %get-tuple-element.19.mass_ref, f32[512,128]{1,0:T(8,128)} %get-tuple-element.16.geometry_ref, ...), custom_call_target="tpu_custom_call" | custom-call | tf_op jit(solution)/shard_map/third/pallas_call | solution.py:365
  93.1 12.6 %all_to_all.28 = f32[6,8,128]{2,1,0:T(8,128)} all-to-all(f32[6,8,128]{2,1,0:T(8,128)} %bitcast.29), channel_id=1, replica_groups=mesh['face'=6,'fy'=8,'fx'=16] {'face'}, dimensions={0} | all-to-all | bytes 49152 | tf_op jit(solution)/shard_map/all_to_all | solution.py:347
  105.7 2.5 %last.1 = f32[64,384]{1,0:T(8,128)} custom-call(s32[6,4]{1,0:T(8,128)} %copy.24.nbr_ref, f32[48,128]{1,0:T(8,128)} %bitcast.25, f32[384,128]{1,0:T(8,128)} %get-tuple-element.21.summed_ref, f32[128,128]{1,0:T(8,128)} %get-tuple-element.19.mass_ref, f32[384,128]{1,0:T(8,128)} %get-tuple-element.22.sectioned_ref), custom_call_target="tpu_custom_call" | custom-call | tf_op jit(solution)/shard_map/last/pallas_call | solution.py:372
  108.1 1.0 copy.25
  109.1 22.0 %all_to_all.29 = f32[64,1,384]{2,1,0:T(1,128)S(1)} all-to-all(f32[64,1,384]{2,1,0:T(1,128)S(1)} %copy.25), channel_id=1, replica_groups={{0,1,2,3,4,5,6,7,8,9,10,11,12,13,14,15,32,33,34,35,36,37,38,39,40,41,42..., dimensions={0} | all-to-all | bytes 196608 | tf_op jit(solution)/shard_map/all_to_all | solution.py:375
  131.1 0.6 copy.28
  131.8 1.6 %unpack.1 = f32[128,192]{1,0:T(8,128)} custom-call(f32[64,384]{1,0:T(8,128)} %bitcast.22), custom_call_target="tpu_custom_call" | custom-call | tf_op jit(solution)/shard_map/unpack/pallas_call | solution.py:378
Async XLA Ops:
  0.0 1.4 %copy-start.3 = (f32[1,16,8]{1,2,0:T(8,128)S(1)}, f32[1,16,8]{1,2,0:T(8,128)}, u32[]{:S(2)}) copy-start(f32[1,16,8]{1,2,0:T(8,128)} %param.12) | copy-start | bytes 1540
  1.4 0.7 copy-start.4
  2.0 0.7 copy-start.2
  5.3 41.9 %copy-start.5 = (s32[6,4]{0,1:T(4,128)S(1)}, s32[6,4]{0,1:T(4,128)}, u32[]{:S(2)}) copy-start(s32[6,4]{0,1:T(4,128)} %param.14) | copy-start | bytes 292
  45.2 3.4 %copy-start = (f32[64,8,128]{2,1,0:T(8,128)}, f32[64,8,128]{2,1,0:T(8,128)S(1)}, u32[]{:S(2)}) copy-start(f32[64,8,128]{2,1,0:T(8,128)S(1)} %all_to_all.25) | copy-start | bytes 786436
  45.2 3.4 %collective-permute-start = (f32[64,8,128]{2,1,0:T(8,128)S(1)}, f32[64,8,128]{2,1,0:T(8,128)S(1)}, u32[]{:S(2)}, u32[]{:S(2)}) collective-permute-start(f32[64,8,128]{2,1,0:T(8,128)S(1)} %all_to_all.25), channel_id=1, source_target_pairs={{0,16},{16,0},{32,48},{48,32},{64,80},{80,64},{96,112},{112,96},{1... | collective-permute-start | bytes 786440 | tf_op jit(solution)/shard_map/ppermute | solution.py:344
  48.6 0.7 copy-start.1

commit v2 on v1

v2 whole, which is shorter than its diff:
```python
import functools

import jax
import jax.numpy as jnp
import numpy as np
from jax import lax
from jax.experimental import pallas as pl
from jax.experimental.pallas import tpu as pltpu
from jax.sharding import PartitionSpec as P

time_step = 0.05
hyper_coeff = 0.0005

FACES = 6
ROWS = 128
LANES = 128
EDGES = 4
RING = (3, 2, 1, 0)
RING_ROWS = 64
SLOT = 64


def deriv_table():
    gll_nodes = np.array([-1.0, -1.0 / np.sqrt(5.0), 1.0 / np.sqrt(5.0), 1.0])
    bary_weights = np.ones(4)
    for j in range(4):
        for m in range(4):
            if m != j:
                bary_weights[j] = bary_weights[j] / (gll_nodes[j] - gll_nodes[m])
    matrix = np.zeros((4, 4))
    for i in range(4):
        for j in range(4):
            if i != j:
                matrix[i, j] = bary_weights[j] / bary_weights[i] / (gll_nodes[i] - gll_nodes[j])
        matrix[i, i] = -np.sum(matrix[i])
    return matrix


def deriv_operands():
    table = deriv_table()
    along_x = np.kron(np.eye(32), table.T)
    along_y = np.kron(np.kron(np.eye(4), table.T), np.eye(8))
    return along_x.astype(np.float32), along_y.astype(np.float32)


def roll(values, shift, axis):
    return pltpu.roll(values, shift % values.shape[axis], axis)


def iota(shape, dim):
    return lax.broadcasted_iota(jnp.int32, shape, dim)


def dot(a, b):
    return jnp.dot(a, b, precision=lax.Precision.HIGHEST, preferred_element_type=jnp.float32)


def dot_t(a, b):
    return lax.dot_general(
        a,
        b,
        (((1,), (1,)), ((), ())),
        precision=lax.Precision.HIGHEST,
        preferred_element_type=jnp.float32,
    )


def stacked(parts, axis=0):
    return jnp.concatenate(parts, axis=axis)


def gll_weight(position):
    return jnp.where((position % 4 == 0) | (position % 4 == 3), 1.0 / 6.0, 5.0 / 6.0)


def mass_weight():
    lane = iota((1, LANES), 1)
    return gll_weight(lane // 8) * gll_weight(lane % 8)


def beside(field):
    return (
        roll(field, 1, 1),
        roll(field, -1, 1),
        roll(roll(field, 1, 0), -7, 1),
        roll(roll(field, -1, 0), 7, 1),
    )


def summed_along_x(field):
    lane = iota(field.shape, 1)
    block = iota(field.shape, 0) % 16
    c = lane % 8
    before, after, before_block, after_block = beside(field)
    summed = field + jnp.where(
        c == 4, before, jnp.where((c == 0) & (block > 0), before_block, 0.0)
    )
    return summed + jnp.where(
        c == 3, after, jnp.where((c == 7) & (block < 15), after_block, 0.0)
    )


def in_face(field):
    summed = summed_along_x(field)
    r = iota(field.shape, 1) // 8
    above = roll(summed, 8, 1)
    below = roll(summed, -8, 1)
    edge_rows = jnp.zeros((16, LANES), jnp.float32)
    above_block = stacked([edge_rows, above[: ROWS - 16]])
    below_block = stacked([below[16:], edge_rows])
    total = summed + jnp.where(r == 0, above_block, jnp.where(r % 4 == 0, above, 0.0))
    return total + jnp.where(r == 15, below_block, jnp.where(r % 4 == 3, below, 0.0))


def in_strips(field):
    summed = summed_along_x(field)
    r = iota(field.shape, 1) // 8
    return (
        summed
        + jnp.where(r == 4, roll(summed, 8, 1), 0.0)
        + jnp.where(r == 3, roll(summed, -8, 1), 0.0)
    )


def between_strips(field):
    block = iota(field.shape, 0) % 16
    c = iota(field.shape, 1) % 8
    _, _, before_block, after_block = beside(field)
    first = (c == 0) & (block == 0)
    last = (c == 7) & (block == 15)
    return jnp.where(first, before_block, jnp.where(last, after_block, 0.0))


def rim_tables(edge, reverse=False):
    lane = iota((LANES, LANES), 0)
    k = iota((LANES, LANES), 1)
    count = 16 if edge in (0, 2) else 8
    block = iota((count, LANES), 0)
    at = iota((count, LANES), 1)
    if reverse:
        k, at = 127 - k, 127 - at
    if edge == 0:
        hit, mask = lane == k % 8, block == at // 8
    elif edge == 1:
        hit, mask = lane == 8 * (k % 16) + 7, block == at // 16
    elif edge == 2:
        hit, mask = lane == 127 - k % 8, block == 15 - at // 8
    else:
        hit, mask = lane == 8 * (15 - k % 16), block == 7 - at // 16
    return jnp.where(hit, 1.0, 0.0), jnp.where(mask, 1.0, 0.0)


def rim_rows(edge, base=0):
    if edge == 0:
        return pl.ds(base, 16)
    if edge == 1:
        return pl.ds(base + 15, 8, 16)
    if edge == 2:
        return pl.ds(base + 112, 16)
    return pl.ds(base, 8, 16)


def turned(u, v, quarter):
    quarter = quarter % 4
    if quarter == 0:
        return u, v
    if quarter == 1:
        return -v, u
    if quarter == 2:
        return -u, -v
    return v, -u


def block_sums(values, mask):
    count = mask.shape[0]
    return [
        jnp.sum(values[n : n + count] * mask, axis=0, keepdims=True)
        for n in range(0, values.shape[0], count)
    ]


def join(face_ref, ring, channels):
    south, south_mask = rim_tables(0)
    spread, mask = rim_tables(0, reverse=True)
    up = block_sums(dot(stacked(ring), spread), mask)
    down = []
    for edge in range(EDGES):
        spread, mask = rim_tables(edge, reverse=True)
        rows = stacked([face_ref[rim_rows(edge, ROWS * ch), :] for ch in range(channels)])
        line = block_sums(dot(rows, spread), mask)
        down.append([*turned(line[0], line[1], 2 - edge), *line[2:]])
    down_rows = [down[edge][ch] * south_mask for ch in range(channels) for edge in RING]
    placed = dot_t(stacked(down_rows), south)
    ring_total = [
        ring[ch] + between_strips(ring[ch]) + placed[RING_ROWS * ch : RING_ROWS * ch + RING_ROWS]
        for ch in range(channels)
    ]
    for n, edge in enumerate(RING):
        line = [up[EDGES * ch + n] for ch in range(channels)]
        line = [*turned(line[0], line[1], edge + 2), *line[2:]]
        spread, mask = rim_tables(edge)
        count = mask.shape[0]
        placed = dot_t(stacked([part * mask for part in line]), spread)
        for ch in range(channels):
            rows = rim_rows(edge, ROWS * ch)
            face_ref[rows, :] = face_ref[rows, :] + placed[ch * count : (ch + 1) * count]
    return ring_total


def pack_kernel(state_ref, jac_ref, diag_ref, cross_ref, cor_ref, out_ref):
    turned_state = jnp.transpose(state_ref[...])
    for part in range(3):
        out_ref[pl.ds(part, 64, 8), :] = turned_state[64 * part : 64 * part + 64]
    spread = jnp.where(iota((16, LANES), 1) // 8 == iota((16, LANES), 0), 1.0, 0.0)
    mask = jnp.where(iota((8, LANES), 1) % 8 == iota((8, LANES), 0), 1.0, 0.0)
    fields = [jac_ref[...], diag_ref[0], diag_ref[1], cross_ref[...], cor_ref[...]]
    for k, line in enumerate(block_sums(dot(stacked(fields), spread), mask)):
        out_ref[pl.ds(3 + k, 64, 8), :] = jnp.broadcast_to(line, (64, LANES))


def strip_of(edge, fields_ref):
    rows = stacked([fields_ref[rim_rows(edge, ROWS * k), :] for k in range(8)])
    if edge == 0:
        return rows
    lane = iota((LANES, LANES), 0)
    m = iota((LANES, LANES), 1)
    if edge == 2:
        nodes = dot(rows, jnp.where(lane == 127 - m, 1.0, 0.0))
        return dot(jnp.where((lane // 16 == m // 16) & (lane % 16 == 15 - m % 16), 1.0, 0.0), nodes)
    near = m < 64
    if edge == 1:
        source = 8 * (m % 8) + 7 - m // 8
    else:
        source = 8 * (7 - m % 8) + m // 8
    halves = [
        dot(rows, jnp.where(near & (lane == source + 64 * half), 1.0, 0.0)) for half in range(2)
    ]
    j = lane % 16 if edge == 1 else 15 - lane % 16
    wanted = 64 * (j % 2) + 8 * (lane // 16) + j // 2
    return dot(jnp.where(m == wanted, 1.0, 0.0), stacked(halves))


def put_strips(fields_ref, nbr_ref, face, send_ref):
    near = iota((16, LANES), 1) < 64
    for edge in range(EDGES):
        rows = strip_of(edge, fields_ref)
        u, v, t, mass, volume, m_xx, m_yy, m_xy = [rows[16 * k : 16 * k + 16] for k in range(8)]
        u, v = turned(u, v, -edge)
        if edge % 2:
            m_xx, m_yy, m_xy = m_yy, m_xx, -m_xy
        slot = [
            jnp.where(near, low, roll(high, 64, 1))
            for low, high in ((u, v), (t, mass), (volume, m_xx), (m_yy, m_xy))
        ]
        start = pl.multiple_of(SLOT * nbr_ref[face, edge], SLOT)
        send_ref[pl.ds(start, SLOT), :] = stacked(slot)


def got_strips(nbr_ref, face, got_ref):
    near = iota((RING_ROWS, LANES), 1) < 64
    pairs = [[] for _ in range(4)]
    for edge in RING:
        start = pl.multiple_of(SLOT * nbr_ref[face, edge], SLOT)
        slot = got_ref[pl.ds(start, SLOT), :]
        for n in range(4):
            pairs[n].append(slot[16 * n : 16 * n + 16])
    fields = []
    for pair in pairs:
        rows = stacked(pair)
        fields += [jnp.where(near, rows, 0.0), jnp.where(near, roll(rows, 64, 1), 0.0)]
    fields[3] = jnp.where(near, fields[3], 1.0)
    fields[4] = jnp.where(near, fields[4], 1.0)
    return fields


def first_kernel(nbr_ref, own_ref, other_ref, dx_ref, dy_ref, fields_ref, send_ref):
    core = lax.axis_index("fy") % 2
    face = lax.axis_index("face")
    fields = []
    for k in range(8):
        own = own_ref[pl.ds(k, 64, 8), :]
        other = other_ref[pl.ds(k, 64, 8), :]
        even = jnp.where(core == 0, own, other)
        odd = jnp.where(core == 0, other, own)
        pieces = []
        for x in range(4):
            pieces += [even[16 * x : 16 * x + 16], odd[16 * x : 16 * x + 16]]
        fields.append(stacked(pieces))
    u, v, t, volume, m_xx, m_yy, m_xy, planet = fields
    contra_u = m_xx * u + m_xy * v
    contra_v = m_xy * u + m_yy * v
    energy = 0.5 * (u * contra_u + v * contra_v) + t
    x_derivs = dot(stacked([v, t, energy]), dx_ref[...])
    y_derivs = dot(stacked([u, t, energy]), dy_ref[...])
    dx_v, dx_t, dx_e = x_derivs[:ROWS], x_derivs[ROWS : 2 * ROWS], x_derivs[2 * ROWS :]
    dy_u, dy_t, dy_e = y_derivs[:ROWS], y_derivs[ROWS : 2 * ROWS], y_derivs[2 * ROWS :]
    absolute = (dx_v - dy_u) / volume + planet
    mass = mass_weight() * volume
    raw_u = u + time_step * (absolute * volume * contra_v - dx_e)
    raw_v = v + time_step * (-absolute * volume * contra_u - dy_e)
    raw_t = t - time_step * (contra_u * dx_t + contra_v * dy_t)
    sums = [in_face(field) for field in (mass * raw_u, mass * raw_v, mass * raw_t, mass)]
    for k, field in enumerate([*sums, volume, m_xx, m_yy, m_xy]):
        fields_ref[ROWS * k : ROWS * k + ROWS, :] = field
    put_strips(fields_ref, nbr_ref, face, send_ref)


def laplace(fields, geometry, along_x, along_y):
    volume, m_xx, m_yy, m_xy = geometry
    count = volume.shape[0]
    values = stacked(fields)
    grad_x, grad_y = dot(values, along_x), dot(values, along_y)
    flux_x, flux_y = [], []
    for ch in range(3):
        part = slice(count * ch, count * ch + count)
        flux_x.append(volume * (m_xx * grad_x[part] + m_xy * grad_y[part]))
        flux_y.append(volume * (m_xy * grad_x[part] + m_yy * grad_y[part]))
    spread = dot(stacked(flux_x), along_x) + dot(stacked(flux_y), along_y)
    mass = mass_weight() * volume
    return [mass * (spread[count * ch : count * ch + count] / volume) for ch in range(3)]


def second_kernel(nbr_ref, got_ref, fields_ref, dx_ref, dy_ref, out_ref, total_ref):
    face = lax.axis_index("face")
    core = lax.axis_index("fy") % 2
    along_x, along_y = dx_ref[...], dy_ref[...]
    ring_fields = got_strips(nbr_ref, face, got_ref)
    geometry = [
        stacked([fields_ref[ROWS * k : ROWS * k + ROWS, :], ring_fields[k]]) for k in range(4, 8)
    ]

    total_ref[...] = fields_ref[: 4 * ROWS, :]
    ring = join(total_ref, ring_fields[:4], 4)
    face_mass = total_ref[3 * ROWS : 4 * ROWS, :]
    total_mass = stacked([face_mass, ring[3]])
    sectioned = [total_ref[ROWS * ch : ROWS * ch + ROWS, :] / face_mass for ch in range(3)]
    fields = [stacked([sectioned[ch], ring[ch] / ring[3]]) for ch in range(3)]
    for step in range(2):
        lapped = laplace(fields, geometry, along_x, along_y)
        for ch in range(3):
            total_ref[ROWS * ch : ROWS * ch + ROWS, :] = in_face(lapped[ch][:ROWS])
        ring = join(total_ref, [in_strips(field[ROWS:]) for field in lapped], 3)
        if step == 0:
            fields = [
                stacked([total_ref[ROWS * ch : ROWS * ch + ROWS, :], ring[ch]]) / total_mass
                for ch in range(3)
            ]
    for ch in range(3):
        part = slice(ROWS * ch, ROWS * ch + ROWS)
        total_ref[part, :] = sectioned[ch] - hyper_coeff * (total_ref[part, :] / face_mass)
    for x in range(4):
        for ch in range(3):
            start = pl.multiple_of(ROWS * ch + 32 * x + 16 * core, 16)
            out_ref[16 * x : 16 * x + 16, LANES * ch : LANES * ch + LANES] = total_ref[
                pl.ds(start, 16), :
            ]


def unpack_kernel(got_ref, out_ref):
    levels = got_ref[...]
    columns = stacked([levels[:, LANES * ch : LANES * ch + LANES] for ch in range(3)])
    out_ref[...] = jnp.transpose(columns)


def f32(*shape):
    return jax.ShapeDtypeStruct(shape, jnp.float32)


VMEM = pl.BlockSpec(memory_space=pltpu.VMEM)
SMEM = pl.BlockSpec(memory_space=pltpu.SMEM)


def call(kernel, outs, ins, scratch=(), name=None):
    return pl.pallas_call(
        kernel,
        out_shape=outs,
        in_specs=ins,
        out_specs=jax.tree.map(lambda _: VMEM, outs),
        scratch_shapes=scratch,
        name=name,
    )


def level_groups():
    return [
        [(8 * face + 2 * x + core) * 16 + fx for x in range(4) for fx in range(16)]
        for face in range(FACES)
        for core in range(2)
    ]


def per_device(state, jacobian, metric_diag, metric_cross, coriolis, nbr_face, nbr_edge):
    axes = ("face", "fy", "fx")
    groups = level_groups()
    along_x, along_y = deriv_operands()

    packed = call(pack_kernel, f32(512, LANES), [VMEM] * 5, name="pack")(
        state.reshape(128, 192),
        jacobian[0].T,
        metric_diag[:, 0].transpose(0, 2, 1),
        metric_cross[0].T,
        coriolis[0].T,
    )
    own = lax.all_to_all(
        packed.reshape(64, 8, LANES), axes, 0, 0, axis_index_groups=groups, tiled=True
    )
    other = lax.ppermute(own, "fy", [(i, i ^ 1) for i in range(8)])
    fields, send = call(
        first_kernel,
        [f32(8 * ROWS, LANES), f32(SLOT * FACES, LANES)],
        [SMEM] + [VMEM] * 4,
        name="first",
    )(nbr_face, own.reshape(512, LANES), other.reshape(512, LANES), along_x, along_y)
    got = lax.all_to_all(send.reshape(FACES, SLOT, LANES), "face", 0, 0, tiled=True)
    updated = call(
        second_kernel,
        f32(64, 3 * LANES),
        [SMEM] + [VMEM] * 4,
        [pltpu.VMEM((4 * ROWS, LANES), jnp.float32)],
        name="second",
    )(nbr_face, got.reshape(SLOT * FACES, LANES), fields, along_x, along_y)
    back = lax.all_to_all(
        updated.reshape(64, 1, 3 * LANES), axes, 0, 0, axis_index_groups=groups, tiled=True
    )
    nodes = call(unpack_kernel, f32(128, 192), [VMEM], name="unpack")(
        back.reshape(64, 3 * LANES)
    )
    return nodes.reshape(1, 16, 8, 192)


def solution(mesh):
    return jax.shard_map(
        per_device,
        mesh=mesh,
        in_specs=(
            P("face", "fy", "fx", None),
            P("face", "fy", "fx"),
            P(None, "face", "fy", "fx"),
            P("face", "fy", "fx"),
            P("face", "fy", "fx"),
            P(),
            P(),
        ),
        out_specs=P("face", "fy", "fx", None),
        check_vma=False,
    )
```

time: 134 us -> 107 us (0.80)
  blocking collectives: 107 us -> 84.8 us
  local copies, waits for them, and re-layouts: 6.42 us -> 3.02 us
  Pallas kernels: 17.7 us -> 15.9 us
    all_to_all x3 -> x1, blocking collectives: 44.6 us -> 22.9 us  [per_device(): lax.all_to_all(send.reshape(FACES, SLOT, LANES), 'face', 0, 0, tiled=True)]
    squeeze x3 -> x0, local copies, waits for them, and re-layouts: 2.7 us -> none  [the longest x1 1.37 us: per_device(): jacobian[0]]
    pallas_call x4 -> x2, Pallas kernels: 14.2 us -> 12.4 us  [the longest x1 8.92 us: per_device(): call(second_kernel, f32(64, 3 * LANES), [SMEM] + [VMEM] * 4, [pltpu.VMEM(...]
    unnamed x15 -> x8, local copies, waits for them, and re-layouts: 2.73 us -> 2.03 us
where the time goes in v2:
time: 107 us; the launch traced here: 106 us
  blocking collectives  84.8 us (79%)
  Pallas kernels  15.9 us (15%)
  local copies, waits for them, and re-layouts  3.02 us (3%)
  starting transfers between devices  1.91 us (2%)
    all_to_all x1, blocking collectives, per_device(): lax.all_to_all(packed.reshape(64, 8, LANES), axes, 0, 0, axis_index_group...  39.9 us
    all_to_all x1, blocking collectives, per_device(): lax.all_to_all(send.reshape(FACES, SLOT, LANES), 'face', 0, 0, tiled=True)  22.9 us
    all_to_all x1, blocking collectives, per_device(): lax.all_to_all(updated.reshape(64, 1, 3 * LANES), axes, 0, 0, axis_index_...  22 us
    pallas_call x1, Pallas kernels, per_device(): call(second_kernel, f32(64, 3 * LANES), [SMEM] + [VMEM] * 4, [pltpu.VMEM(...  8.92 us
    pallas_call x1, Pallas kernels, per_device(): call(first_kernel, [f32(8 * ROWS, LANES), f32(SLOT * FACES, LANES)], [SME...  3.46 us
  transfers between devices with their start and end apart: 1, of which 1 were waited for; matrix products, arithmetic and copies ran while one was open for 1% of the time, Pallas kernels for 0%

profile of v2, /device:TPU:2, one launch (start us, length us, event | category | flops | bytes accessed | tf_op | source)
XLA Modules:
  0.0 106.5 jit_solution(546809498561803816)
XLA Ops:
  0.0 1.8 %pack.1 = f32[512,128]{1,0:T(8,128)} custom-call(f32[128,192]{1,0:T(8,128)} %bitcast.30, f32[8,16]{1,0:T(8,128)} %bitcast.32, f32[2,8,16]{2,1,0:T(8,128)} %bitcast.31, f32[8,16]{1,0:T(8,128)} %bitcast.33, f32[8,16]{1,0:T(8,128)} %bitcast.34), custom_call_target="tpu_custom_call" | custom-call | tf_op jit(solution)/shard_map/pack/pallas_call | solution.py:397
  1.8 0.0 copy-start.2
  1.8 39.9 %all_to_all.15 = f32[64,8,128]{2,1,0:T(8,128)S(1)} all-to-all(f32[64,8,128]{2,1,0:T(8,128)} %bitcast.24), channel_id=1, replica_groups={{0,1,2,3,4,5,6,7,8,9,10,11,12,13,14,15,32,33,34,35,36,37,38,39,40,41,42..., dimensions={0} | all-to-all | bytes 524288 | tf_op jit(solution)/shard_map/all_to_all | solution.py:404
  41.8 0.0 copy-start
  41.8 1.9 %collective-permute-start = (f32[64,8,128]{2,1,0:T(8,128)S(1)}, f32[64,8,128]{2,1,0:T(8,128)S(1)}, u32[]{:S(2)}, u32[]{:S(2)}) collective-permute-start(f32[64,8,128]{2,1,0:T(8,128)S(1)} %all_to_all.15), channel_id=1, source_target_pairs={{0,16},{16,0},{32,48},{48,32},{64,80},{80,64},{96,112},{112,96},{1... | collective-permute-start | bytes 786440 | tf_op jit(solution)/shard_map/ppermute | solution.py:407
  43.7 0.0 copy-done.2
  43.7 0.7 copy.12.nbr_ref
  44.4 0.8 collective-permute-done
  45.2 0.0 copy-start.1
  45.2 0.0 copy-done
  45.2 0.7 copy-done.1
  45.9 3.5 %first.1 = (f32[1024,128]{1,0:T(8,128)}, f32[384,128]{1,0:T(8,128)}) custom-call(s32[6,4]{1,0:T(8,128)} %copy.12.nbr_ref, f32[512,128]{1,0:T(8,128)} %bitcast.23, f32[512,128]{1,0:T(8,128)} %bitcast.28, f32[128,128]{1,0:T(8,128)} %constant.4.clone.dx_ref, f32[128,128]{1,0:T(8,128)} %constant.5.clone.dy_ref), custom_call_target="tpu_custom_call" | custom-call | tf_op jit(solution)/shard_map/first/pallas_call | solution.py:408
  49.4 22.9 %all_to_all.16 = f32[6,64,128]{2,1,0:T(8,128)} all-to-all(f32[6,64,128]{2,1,0:T(8,128)} %bitcast.29), channel_id=1, replica_groups=mesh['face'=6,'fy'=8,'fx'=16] {'face'}, dimensions={0} | all-to-all | bytes 393216 | tf_op jit(solution)/shard_map/all_to_all | solution.py:414
  72.3 8.9 %second.1 = f32[64,384]{1,0:T(8,128)} custom-call(s32[6,4]{1,0:T(8,128)} %copy.12.nbr_ref, f32[384,128]{1,0:T(8,128)} %bitcast.25, f32[1024,128]{1,0:T(8,128)} %get-tuple-element.8.fields_ref, f32[128,128]{1,0:T(8,128)} %constant.4.clone.dx_ref, f32[128,128]{1,0:T(8,128)} %constant.5.clone.dy_ref), custom_call_target="tpu_custom_call" | custom-call | tf_op jit(solution)/shard_map/second/pallas_call | solution.py:415
  81.2 1.0 copy.13
  82.2 22.0 %all_to_all.17 = f32[64,1,384]{2,1,0:T(1,128)S(1)} all-to-all(f32[64,1,384]{2,1,0:T(1,128)S(1)} %copy.13), channel_id=1, replica_groups={{0,1,2,3,4,5,6,7,8,9,10,11,12,13,14,15,32,33,34,35,36,37,38,39,40,41,42..., dimensions={0} | all-to-all | bytes 196608 | tf_op jit(solution)/shard_map/all_to_all | solution.py:422
  104.2 0.6 copy.16
  104.8 1.6 %unpack.1 = f32[128,192]{1,0:T(8,128)} custom-call(f32[64,384]{1,0:T(8,128)} %bitcast.27), custom_call_target="tpu_custom_call" | custom-call | tf_op jit(solution)/shard_map/unpack/pallas_call | solution.py:425
Async XLA Ops:
  1.8 41.9 %copy-start.2 = (s32[6,4]{0,1:T(4,128)S(1)}, s32[6,4]{0,1:T(4,128)}, u32[]{:S(2)}) copy-start(s32[6,4]{0,1:T(4,128)} %param.14) | copy-start | bytes 292
  41.8 3.4 %copy-start = (f32[64,8,128]{2,1,0:T(8,128)}, f32[64,8,128]{2,1,0:T(8,128)S(1)}, u32[]{:S(2)}) copy-start(f32[64,8,128]{2,1,0:T(8,128)S(1)} %all_to_all.15) | copy-start | bytes 786436
  41.8 3.4 %collective-permute-start = (f32[64,8,128]{2,1,0:T(8,128)S(1)}, f32[64,8,128]{2,1,0:T(8,128)S(1)}, u32[]{:S(2)}, u32[]{:S(2)}) collective-permute-start(f32[64,8,128]{2,1,0:T(8,128)S(1)} %all_to_all.15), channel_id=1, source_target_pairs={{0,16},{16,0},{32,48},{48,32},{64,80},{80,64},{96,112},{112,96},{1... | collective-permute-start | bytes 786440 | tf_op jit(solution)/shard_map/ppermute | solution.py:407
  45.2 0.7 copy-start.1

commit v3 on v2

--- a/solution.py
+++ b/solution.py
@@ -252,7 +252,7 @@
             jnp.where(near, low, roll(high, 64, 1))
             for low, high in ((u, v), (t, mass), (volume, m_xx), (m_yy, m_xy))
         ]
-        start = pl.multiple_of(SLOT * nbr_ref[face, edge], SLOT)
+        start = pl.multiple_of(SLOT * nbr_ref[edge, face], SLOT)
         send_ref[pl.ds(start, SLOT), :] = stacked(slot)
 
 
@@ -260,7 +260,7 @@
     near = iota((RING_ROWS, LANES), 1) < 64
     pairs = [[] for _ in range(4)]
     for edge in RING:
-        start = pl.multiple_of(SLOT * nbr_ref[face, edge], SLOT)
+        start = pl.multiple_of(SLOT * nbr_ref[edge, face], SLOT)
         slot = got_ref[pl.ds(start, SLOT), :]
         for n in range(4):
             pairs[n].append(slot[16 * n : 16 * n + 16])
@@ -351,19 +351,27 @@
     for x in range(4):
         for ch in range(3):
             start = pl.multiple_of(ROWS * ch + 32 * x + 16 * core, 16)
-            out_ref[16 * x : 16 * x + 16, LANES * ch : LANES * ch + LANES] = total_ref[
+            out_ref[16 * x : 16 * x + 16, 0, LANES * ch : LANES * ch + LANES] = total_ref[
                 pl.ds(start, 16), :
             ]
 
 
 def unpack_kernel(got_ref, out_ref):
     levels = got_ref[...]
-    columns = stacked([levels[:, LANES * ch : LANES * ch + LANES] for ch in range(3)])
+    columns = stacked([levels[:, 0, LANES * ch : LANES * ch + LANES] for ch in range(3)])
     out_ref[...] = jnp.transpose(columns)
 
 
 def f32(*shape):
     return jax.ShapeDtypeStruct(shape, jnp.float32)
+
+
+def near(*shape):
+    return pltpu.VMEM(shape, jnp.float32)
+
+
+def held(values):
+    return pltpu.with_memory_space_constraint(values, pltpu.VMEM)
 
 
 VMEM = pl.BlockSpec(memory_space=pltpu.VMEM)
@@ -394,7 +402,7 @@
     groups = level_groups()
     along_x, along_y = deriv_operands()
 
-    packed = call(pack_kernel, f32(512, LANES), [VMEM] * 5, name="pack")(
+    packed = call(pack_kernel, near(512, LANES), [VMEM] * 5, name="pack")(
         state.reshape(128, 192),
         jacobian[0].T,
         metric_diag[:, 0].transpose(0, 2, 1),
@@ -407,23 +415,23 @@
     other = lax.ppermute(own, "fy", [(i, i ^ 1) for i in range(8)])
     fields, send = call(
         first_kernel,
-        [f32(8 * ROWS, LANES), f32(SLOT * FACES, LANES)],
+        [near(8 * ROWS, LANES), near(SLOT * FACES, LANES)],
         [SMEM] + [VMEM] * 4,
         name="first",
-    )(nbr_face, own.reshape(512, LANES), other.reshape(512, LANES), along_x, along_y)
+    )(nbr_face.T, held(own.reshape(512, LANES)), held(other.reshape(512, LANES)), along_x, along_y)
     got = lax.all_to_all(send.reshape(FACES, SLOT, LANES), "face", 0, 0, tiled=True)
     updated = call(
         second_kernel,
-        f32(64, 3 * LANES),
+        near(64, 1, 3 * LANES),
         [SMEM] + [VMEM] * 4,
         [pltpu.VMEM((4 * ROWS, LANES), jnp.float32)],
         name="second",
-    )(nbr_face, got.reshape(SLOT * FACES, LANES), fields, along_x, along_y)
+    )(nbr_face.T, held(got.reshape(SLOT * FACES, LANES)), held(fields), along_x, along_y)
     back = lax.all_to_all(
-        updated.reshape(64, 1, 3 * LANES), axes, 0, 0, axis_index_groups=groups, tiled=True
+        updated, axes, 0, 0, axis_index_groups=groups, tiled=True
     )
     nodes = call(unpack_kernel, f32(128, 192), [VMEM], name="unpack")(
-        back.reshape(64, 3 * LANES)
+        held(back)
     )
     return nodes.reshape(1, 16, 8, 192)
 

time: 107 us -> 101 us (0.944)
  Pallas kernels: 15.9 us -> 12.6 us
  local copies, waits for them, and re-layouts: 3.02 us -> 0 us
    pallas_call x4, Pallas kernels: 15.9 us -> 12.6 us  [the longest x1 8.07 us: per_device(): call(second_kernel, near(64, 1, 3 * LANES), [SMEM] + [VMEM] * 4, [pltpu.V...]
    unnamed x8 -> x0, local copies, waits for them, and re-layouts: 2.03 us -> none
  transfers between devices with their start and end apart: 1 -> 1, of which waited for: 1 -> 1; matrix products, arithmetic and copies ran while one was open for 1% -> 0% of each run, Pallas kernels for 0% -> 0%
where the time goes in v3:
time: 101 us; the launch traced here: 100 us
  blocking collectives  84.2 us (83%)
  Pallas kernels  12.6 us (12%)
  starting transfers between devices  1.91 us (2%)
  waiting for transfers between devices  1.5 us (1%)
    all_to_all x1, blocking collectives, per_device(): lax.all_to_all(packed.reshape(64, 8, LANES), axes, 0, 0, axis_index_group...  39.6 us
    all_to_all x1, blocking collectives, per_device(): lax.all_to_all(send.reshape(FACES, SLOT, LANES), 'face', 0, 0, tiled=True)  22.6 us
    all_to_all x1, blocking collectives, per_device(): lax.all_to_all(updated, axes, 0, 0, axis_index_groups=groups, tiled=True)  22 us
    pallas_call x1, Pallas kernels, per_device(): call(second_kernel, near(64, 1, 3 * LANES), [SMEM] + [VMEM] * 4, [pltpu.V...  8.07 us
    pallas_call x1, Pallas kernels, per_device(): call(first_kernel, [near(8 * ROWS, LANES), near(SLOT * FACES, LANES)], [S...  2.62 us
  transfers between devices with their start and end apart: 1, of which 1 were waited for; matrix products, arithmetic and copies ran while one was open for 0% of the time, Pallas kernels for 0%

profile of v3, /device:TPU:2, one launch (start us, length us, event | category | flops | bytes accessed | tf_op | source)
XLA Modules:
  0.0 100.3 jit_solution(13964598206862270948)
XLA Ops:
  0.0 1.1 %pack.1 = f32[512,128]{1,0:T(8,128)S(1)} custom-call(f32[128,192]{1,0:T(8,128)} %bitcast.25, f32[8,16]{1,0:T(8,128)} %bitcast.29, f32[2,8,16]{2,1,0:T(8,128)} %bitcast.28, f32[8,16]{1,0:T(8,128)} %bitcast.30, f32[8,16]{1,0:T(8,128)} %bitcast.31), custom_call_target="tpu_custom_call" | custom-call | tf_op jit(solution)/shard_map/pack/pallas_call | solution.py:405
  1.1 39.6 %all_to_all.15 = f32[64,8,128]{2,1,0:T(8,128)S(1)} all-to-all(f32[64,8,128]{2,1,0:T(8,128)S(1)} %bitcast.21), channel_id=1, replica_groups={{0,1,2,3,4,5,6,7,8,9,10,11,12,13,14,15,32,33,34,35,36,37,38,39,40,41,42..., dimensions={0} | all-to-all | bytes 524288 | tf_op jit(solution)/shard_map/all_to_all | solution.py:412
  40.7 1.9 %collective-permute-start = (f32[64,8,128]{2,1,0:T(8,128)S(1)}, f32[64,8,128]{2,1,0:T(8,128)S(1)}, u32[]{:S(2)}, u32[]{:S(2)}) collective-permute-start(f32[64,8,128]{2,1,0:T(8,128)S(1)} %all_to_all.15), channel_id=1, source_target_pairs={{0,16},{16,0},{32,48},{48,32},{64,80},{80,64},{96,112},{112,96},{1... | collective-permute-start | bytes 786440 | tf_op jit(solution)/shard_map/ppermute | solution.py:415
  42.7 1.5 %collective-permute-done = f32[64,8,128]{2,1,0:T(8,128)S(1)} collective-permute-done((f32[64,8,128]{2,1,0:T(8,128)S(1)}, f32[64,8,128]{2,1,0:T(8,128)S(1)}, u32[]{:S(2)}, u32[]{:S(2)}) %collective-permute-start) | collective-permute-done | bytes 262176 | tf_op jit(solution)/shard_map/ppermute | solution.py:415
  44.2 2.6 %first.1 = (f32[1024,128]{1,0:T(8,128)S(1)}, f32[384,128]{1,0:T(8,128)S(1)}) custom-call(s32[4,6]{1,0:T(4,128)} %bitcast.26, f32[512,128]{1,0:T(8,128)S(1)} %bitcast.20, f32[512,128]{1,0:T(8,128)S(1)} %bitcast.23, f32[128,128]{1,0:T(8,128)} %constant.4.clone.dx_ref, f32[128,128]{1,0:T(8,128)} %constant.5.clone.dy_ref), custom_call_target="tpu_custom_call" | custom-call | tf_op jit(solution)/shard_map/first/pallas_call | solution.py:416
  46.8 22.6 %all_to_all.16 = f32[6,64,128]{2,1,0:T(8,128)S(1)} all-to-all(f32[6,64,128]{2,1,0:T(8,128)S(1)} %bitcast.24), channel_id=1, replica_groups=mesh['face'=6,'fy'=8,'fx'=16] {'face'}, dimensions={0} | all-to-all | bytes 393216 | tf_op jit(solution)/shard_map/all_to_all | solution.py:422
  69.4 8.1 %second.1 = f32[64,1,384]{2,1,0:T(1,128)S(1)} custom-call(s32[4,6]{1,0:T(4,128)} %bitcast.27, f32[384,128]{1,0:T(8,128)S(1)} %bitcast.22, f32[1024,128]{1,0:T(8,128)S(1)} %get-tuple-element.8.fields_ref, f32[128,128]{1,0:T(8,128)} %constant.4.clone.dx_ref, f32[128,128]{1,0:T(8,128)} %constant.5.clone.dy_ref), custom_call_target="tpu_custom_call" | custom-call | tf_op jit(solution)/shard_map/second/pallas_call | solution.py:423
  77.5 22.0 %all_to_all.17.got_ref = f32[64,1,384]{2,1,0:T(1,128)S(1)} all-to-all(f32[64,1,384]{2,1,0:T(1,128)S(1)} %second.1), channel_id=1, replica_groups={{0,1,2,3,4,5,6,7,8,9,10,11,12,13,14,15,32,33,34,35,36,37,38,39,40,41,42..., dimensions={0} | all-to-all | bytes 196608 | tf_op jit(solution)/shard_map/all_to_all | solution.py:430
  99.5 0.8 unpack.1
Async XLA Ops:
  40.7 3.4 %collective-permute-start = (f32[64,8,128]{2,1,0:T(8,128)S(1)}, f32[64,8,128]{2,1,0:T(8,128)S(1)}, u32[]{:S(2)}, u32[]{:S(2)}) collective-permute-start(f32[64,8,128]{2,1,0:T(8,128)S(1)} %all_to_all.15), channel_id=1, source_target_pairs={{0,16},{16,0},{32,48},{48,32},{64,80},{80,64},{96,112},{112,96},{1... | collective-permute-start | bytes 786440 | tf_op jit(solution)/shard_map/ppermute | solution.py:415

commit v4 on v3

v4 whole, which is shorter than its diff:
```python
import jax
import jax.numpy as jnp
import ml_dtypes
import numpy as np
from jax import lax
from jax.experimental import pallas as pl
from jax.experimental.pallas import tpu as pltpu
from jax.sharding import PartitionSpec as P

time_step = 0.05
hyper_coeff = 0.0005

FACES = 6
ROWS = 128
LANES = 128
EDGES = 4
RING_ROWS = 48
ALL_ROWS = ROWS + RING_ROWS
SLOT = 56
ENDS = ("S0", "S15", "N0", "N15", "E0", "E7", "W0", "W7")
END_ROWS = (0, 15, 16, 31, 32, 39, 40, 47)
MEETS = (6, 4, 7, 5, 1, 3, 0, 2)
TURNS = (1, -1, -1, 1, 1, -1, -1, 1)


def deriv_table():
    gll_nodes = np.array([-1.0, -1.0 / np.sqrt(5.0), 1.0 / np.sqrt(5.0), 1.0])
    bary_weights = np.ones(4)
    for j in range(4):
        for m in range(4):
            if m != j:
                bary_weights[j] = bary_weights[j] / (gll_nodes[j] - gll_nodes[m])
    matrix = np.zeros((4, 4))
    for i in range(4):
        for j in range(4):
            if i != j:
                matrix[i, j] = bary_weights[j] / bary_weights[i] / (gll_nodes[i] - gll_nodes[j])
        matrix[i, i] = -np.sum(matrix[i])
    return matrix


def in_parts(matrix):
    rest = np.asarray(matrix, np.float64)
    parts = []
    for _ in range(3):
        part = rest.astype(ml_dtypes.bfloat16)
        parts.append(part)
        rest = rest - part.astype(np.float64)
    return parts


def face_node(edge, depth, k):
    row, col = ((depth, k), (k, 127 - depth), (127 - depth, 127 - k), (127 - k, depth))[edge]
    return row // 16, col // 8, 8 * (row % 16) + col % 8


def ring_node(edge, depth, k):
    if edge == 1:
        return k // 16, 8 * (k % 16) + depth
    row = 127 - k
    return row // 16, 8 * (row % 16) + 7 - depth


def end_lane(end, depth):
    return {
        "S0": 8 * (15 - depth),
        "S15": 8 * (15 - depth) + 7,
        "N0": 8 * depth,
        "N15": 8 * depth + 7,
        "E0": depth,
        "E7": 120 + depth,
        "W0": 7 - depth,
        "W7": 127 - depth,
    }[end]


def tables():
    deriv = deriv_table()
    along_x = np.kron(np.eye(32), deriv.T)
    along_y = np.kron(np.kron(np.eye(4), deriv.T), np.eye(8))
    lane = np.arange(LANES)
    r, c = lane // 8, lane % 8
    weights = np.array([1.0, 5.0, 5.0, 1.0]) / 6.0
    within = np.eye(LANES)
    across = np.zeros((LANES, LANES))
    for l in range(LANES):
        if c[l] in (3, 4):
            within[l, l + 1 if c[l] == 3 else l - 1] = 1.0
        if c[l] == 7:
            across[l, l - 7] = 1.0
        if c[l] == 0:
            across[l, l + 7] = 1.0
    both = np.concatenate([within, across], 1)
    gradient = in_parts(np.concatenate([along_x, along_y], 1))
    weighted = np.diag(weights[r % 4] * weights[c % 4])
    spread = in_parts(np.concatenate([along_x @ weighted @ both, along_y @ weighted @ both], 0))

    wide = {
        "gradient": np.concatenate([gradient[n] for n in (0, 0, 1, 1, 0, 2)], 0),
        "spread": np.concatenate([spread[n] for n in (0, 0, 0, 1, 1, 2)], 0),
        "both": np.concatenate([both] * 3, 0),
    }
    narrow = {"reverse": np.eye(LANES)[::-1]}
    narrow["reverse_rows"] = np.kron(np.eye(8), np.eye(16)[::-1])
    for edge, name in ((1, "east"), (3, "west")):
        out = np.zeros((2, LANES, LANES))
        out_rows = np.zeros((LANES, LANES))
        into = np.zeros((2, LANES, LANES))
        into_rows = np.zeros((LANES, LANES))
        for k in range(128):
            j, i = k // 8, k % 8
            j2, i2 = (127 - k) // 8, (127 - k) % 8
            for depth in range(8):
                fy, _, at = face_node(edge, depth, k)
                out[j % 2, at, 8 * depth + i] = 1.0
                ring_fy, ring_at = ring_node(edge, depth, k)
                into[j2 % 2, 8 * depth + i2, ring_at] = 1.0
                for field in range(8):
                    out_rows[16 * field + j, 64 * (j % 2) + 8 * field + fy] = 1.0
                    into_rows[64 * (j2 % 2) + 8 * field + ring_fy, 16 * field + j2] = 1.0
        wide[name + "_out"] = np.concatenate([out[0], out[1]], 1)
        narrow[name + "_out_rows"] = out_rows
        narrow[name + "_in_rows"] = into_rows
        narrow[name + "_in"] = np.concatenate([into[0]] * 3 + [into[1]] * 3, 0)
    take = np.zeros((LANES, LANES))
    give = np.zeros((LANES, LANES))
    masks = np.zeros((32, LANES), np.float32)
    for t, end in enumerate(ENDS):
        for depth in range(8):
            take[end_lane(end, depth), 8 * t + depth] = 1.0
            give[8 * t + depth, end_lane(ENDS[MEETS[t]], depth)] = 1.0
            masks[t, end_lane(end, depth)] = 1.0
            masks[8 + t, 8 * t + depth] = 1.0
            masks[16 + t, 8 * MEETS[t] + depth] = 1.0
        masks[24 + t] = TURNS[t]
    narrow["take"] = np.concatenate([take] * 3, 0)
    narrow["give"] = np.concatenate([give] * 3, 0)

    arrays, places = [], {}
    for group in (wide, narrow):
        start = 0
        for name, matrix in group.items():
            places[name] = (start, start + matrix.shape[0])
            start += matrix.shape[0]
        arrays.append(
            np.concatenate([m.astype(ml_dtypes.bfloat16) for m in group.values()], 0)
        )
    return arrays[0], arrays[1], masks, places


WIDE, NARROW, MASKS, PLACES = tables()


def of(ref, name):
    start, end = PLACES[name]
    return ref[start:end, :]


def roll(values, shift, axis):
    return pltpu.roll(values, shift % values.shape[axis], axis)


def iota(shape, dim):
    return lax.broadcasted_iota(jnp.int32, shape, dim)


def dot(a, b):
    return jnp.dot(a, b, preferred_element_type=jnp.float32)


def stacked(parts, axis=0):
    return jnp.concatenate(parts, axis=axis)


def split(values):
    high = values.astype(jnp.bfloat16)
    rest = values - high.astype(jnp.float32)
    mid = rest.astype(jnp.bfloat16)
    return high, mid, (rest - mid.astype(jnp.float32)).astype(jnp.bfloat16)


def gradient(values, wide_ref):
    high, mid, low = split(values)
    both = dot(stacked([high, mid, high, mid, low, high], 1), of(wide_ref, "gradient"))
    return both[:, :LANES], both[:, LANES:]


def mass_weight():
    lane = iota((1, LANES), 1)
    r, c = lane // 8 % 4, lane % 4
    along_y = jnp.where((r == 0) | (r == 3), 1.0 / 6.0, 5.0 / 6.0)
    return along_y * jnp.where((c == 0) | (c == 3), 1.0 / 6.0, 5.0 / 6.0)


def assembled(inner, outer):
    shape = inner.shape
    row = iota(shape, 0)
    lane = iota(shape, 1)
    c = lane % 8
    r = lane // 8
    here = row < ROWS + 32
    from_before = here & (c == 0) & (row % 16 > 0)
    from_after = here & (c == 7) & (row % 16 < 15)
    summed = (
        inner
        + jnp.where(from_before, roll(outer, 1, 0), 0.0)
        + jnp.where(from_after, roll(outer, -1, 0), 0.0)
    )
    above = roll(summed, 8, 1)
    below = roll(summed, -8, 1)
    total = (
        summed
        + jnp.where((r % 4 == 0) & (r > 0), above, 0.0)
        + jnp.where((r % 4 == 3) & (r < 15), below, 0.0)
    )
    edge_rows = jnp.zeros((16, LANES), jnp.float32)
    above_block = [edge_rows, above[: ROWS - 16]]
    below_block = [below[16:ROWS], edge_rows]
    if shape[0] > ROWS:
        sides = slice(ROWS + 32, ROWS + 48)
        fy = iota((16, LANES), 0) % 8
        above_block += [edge_rows] * 2 + [jnp.where(fy > 0, roll(above[sides], 1, 0), 0.0)]
        below_block += [edge_rows] * 2 + [jnp.where(fy < 7, roll(below[sides], -1, 0), 0.0)]
    return (
        total
        + jnp.where(r == 0, stacked(above_block), 0.0)
        + jnp.where(r == 15, stacked(below_block), 0.0)
    )


def rim_rows(edge, base=0):
    if edge == 0:
        return pl.ds(base, 16)
    if edge == 1:
        return pl.ds(base + 15, 8, 16)
    if edge == 2:
        return pl.ds(base + 112, 16)
    return pl.ds(base, 8, 16)


def turned(u, v, quarter):
    quarter = quarter % 4
    if quarter == 0:
        return u, v
    if quarter == 1:
        return -v, u
    if quarter == 2:
        return -u, -v
    return v, -u


def ends_meet(ring, channels, narrow_ref, mask_ref):
    ends = stacked(
        [ring[ch][row : row + 1] for ch in range(channels) for row in END_ROWS]
    )
    own = stacked([mask_ref[0:8, :]] * channels)
    taken = dot(stacked(split(ends * own), 1), of(narrow_ref, "take"))
    lines = []
    for ch in range(channels):
        line = jnp.sum(taken[8 * ch : 8 * ch + 8] * mask_ref[8:16, :], axis=0, keepdims=True)
        lines.append(line * mask_ref[16:24, :])
    given = dot(stacked(split(stacked(lines)), 1), of(narrow_ref, "give"))
    given = [given[8 * ch : 8 * ch + 8] for ch in range(channels)]
    sense = mask_ref[24:32, :]
    return [-sense * given[1], sense * given[0], *given[2:]]


def join(face_ref, ring, channels, narrow_ref, mask_ref, ring_too=True):
    ends = ends_meet(ring, channels, narrow_ref, mask_ref) if ring_too else None
    totals = []
    for ch in range(channels):
        south, north = ring[ch][0:16], ring[ch][16:32]
        east, west = ring[ch][32:40], ring[ch][40:48]
        rows = [rim_rows(edge, ROWS * ch) for edge in range(EDGES)]
        lane = iota((16, LANES), 1)
        lane_8 = iota((8, LANES), 1)
        if ring_too:
            block = iota((16, LANES), 0)
            fy = iota((8, LANES), 0)
            of_end = [ends[ch][t : t + 1] for t in range(8)]

            def at_ends(first, last, position, count):
                return jnp.where(
                    position == 0, first, jnp.where(position == count - 1, last, 0.0)
                )

            totals.append(
                stacked(
                    [
                        south
                        + jnp.where(lane // 8 == 15, roll(face_ref[rows[0], :], -8, 1), 0.0)
                        + at_ends(of_end[0], of_end[1], block, 16),
                        north
                        + jnp.where(lane // 8 == 0, roll(face_ref[rows[2], :], 8, 1), 0.0)
                        + at_ends(of_end[2], of_end[3], block, 16),
                        east
                        + jnp.where(lane_8 % 8 == 0, roll(face_ref[rows[1], :], -7, 1), 0.0)
                        + at_ends(of_end[4], of_end[5], fy, 8),
                        west
                        + jnp.where(lane_8 % 8 == 7, roll(face_ref[rows[3], :], 7, 1), 0.0)
                        + at_ends(of_end[6], of_end[7], fy, 8),
                    ]
                )
            )
        from_south = jnp.where(lane // 8 == 0, roll(south, 8, 1), 0.0)
        from_north = jnp.where(lane // 8 == 15, roll(north, -8, 1), 0.0)
        from_east = jnp.where(lane_8 % 8 == 7, roll(east, 7, 1), 0.0)
        from_west = jnp.where(lane_8 % 8 == 0, roll(west, -7, 1), 0.0)
        for edge, part in enumerate((from_south, from_east, from_north, from_west)):
            face_ref[rows[edge], :] = face_ref[rows[edge], :] + part
    return totals


def pack_kernel(state_ref, jac_ref, diag_ref, cross_ref, cor_ref, out_ref):
    turned_state = jnp.transpose(state_ref[...])
    for part in range(3):
        out_ref[pl.ds(part, 64, 8), :] = turned_state[64 * part : 64 * part + 64]
    spread = jnp.where(iota((16, LANES), 1) // 8 == iota((16, LANES), 0), 1.0, 0.0)
    mask = jnp.where(iota((8, LANES), 1) % 8 == iota((8, LANES), 0), 1.0, 0.0)
    fields = [jac_ref[...], diag_ref[0], diag_ref[1], cross_ref[...], cor_ref[...]]
    lines = jnp.dot(
        stacked(fields),
        spread,
        precision=lax.Precision.HIGHEST,
        preferred_element_type=jnp.float32,
    )
    for k in range(5):
        line = jnp.sum(lines[8 * k : 8 * k + 8] * mask, axis=0, keepdims=True)
        out_ref[pl.ds(3 + k, 64, 8), :] = jnp.broadcast_to(line, (64, LANES))


def reversed_blocks(rows, narrow_ref):
    parts = stacked([part.astype(jnp.float32) for part in split(rows)]).astype(jnp.bfloat16)
    moved = dot(parts, of(narrow_ref, "reverse"))
    count = rows.shape[0]
    moved = stacked([moved[n * count : n * count + count] for n in range(3)], 1)
    moved = dot(of(narrow_ref, "reverse_rows"), moved.astype(jnp.bfloat16))
    return moved[:, :LANES] + moved[:, LANES : 2 * LANES] + moved[:, 2 * LANES :]


def strip_of(edge, fields_ref, wide_ref, narrow_ref):
    rows = [fields_ref[rim_rows(edge, ROWS * k), :] for k in range(7)]
    rows = stacked([*rows, jnp.zeros_like(rows[0])])
    if edge == 0:
        return rows
    if edge == 2:
        return reversed_blocks(rows, narrow_ref)
    name = "east" if edge == 1 else "west"
    moved = dot(stacked(split(rows)), of(wide_ref, name + "_out"))
    halves = stacked([moved[:, :LANES], moved[:, LANES:]], 0)
    moved = stacked(
        [stacked([halves[64 * n : 64 * n + 64], halves[192 + 64 * n : 256 + 64 * n]]) for n in range(3)],
        1,
    )
    moved = dot(of(narrow_ref, name + "_out_rows"), moved.astype(jnp.bfloat16))
    return moved[:, :LANES] + moved[:, LANES : 2 * LANES] + moved[:, 2 * LANES :]


def put_strips(fields_ref, nbr_ref, face, send_ref, wide_ref, narrow_ref):
    near = iota((16, LANES), 1) < 64
    for edge in range(EDGES):
        rows = strip_of(edge, fields_ref, wide_ref, narrow_ref)
        u, v, t, mass, flux_xx, flux_xy, flux_yy = [rows[16 * k : 16 * k + 16] for k in range(7)]
        u, v = turned(u, v, -edge)
        if edge % 2:
            flux_xx, flux_xy, flux_yy = flux_yy, -flux_xy, flux_xx
        slot = [
            jnp.where(near, low, roll(high, 64, 1))
            for low, high in ((u, v), (t, mass), (flux_xx, flux_xy))
        ]
        slot.append(jnp.where(near[:8], flux_yy[:8], roll(flux_yy[8:], 64, 1)))
        start = pl.multiple_of(SLOT * nbr_ref[edge, face], 8)
        send_ref[pl.ds(start, SLOT), :] = stacked(slot)


def ring_of(nbr_ref, face, got_ref, narrow_ref):
    near = iota((16, LANES), 1) < 64
    strips = []
    for edge in range(EDGES):
        start = pl.multiple_of(SLOT * nbr_ref[edge, face], 8)
        slot = got_ref[pl.ds(start, SLOT), :]
        fields = []
        for n in range(3):
            rows = slot[16 * n : 16 * n + 16]
            fields += [jnp.where(near, rows, 0.0), jnp.where(near, roll(rows, 64, 1), 0.0)]
        rows = slot[48:56]
        fields.append(stacked([rows, roll(rows, 64, 1)]))
        fields[6] = jnp.where(near, fields[6], 0.0)
        rows = stacked([*fields, jnp.zeros_like(near, jnp.float32)])
        count = 16
        if edge == 0:
            rows = reversed_blocks(rows, narrow_ref)
        elif edge % 2:
            name = "east" if edge == 1 else "west"
            moved = dot(of(narrow_ref, name + "_in_rows"), stacked(split(rows), 1))
            moved = stacked([moved[:64], moved[64:]], 1)
            rows = dot(moved.astype(jnp.bfloat16), of(narrow_ref, name + "_in"))
            count = 8
        fields = [rows[count * k : count * k + count] for k in range(7)]
        fields[0], fields[1] = turned(fields[0], fields[1], edge + 2)
        if edge % 2:
            fields[4], fields[5], fields[6] = fields[6], -fields[5], fields[4]
        else:
            far = near if edge == 0 else ~near
            fields[3] = jnp.where(far, 1.0, fields[3])
        strips.append(fields)
    return [stacked([strips[edge][k] for edge in (0, 2, 1, 3)]) for k in range(7)]


def first_kernel(nbr_ref, own_ref, other_ref, wide_ref, narrow_ref, fields_ref, send_ref):
    core = lax.axis_index("fy") % 2
    face = lax.axis_index("face")
    fields = []
    for k in range(8):
        own = own_ref[pl.ds(k, 64, 8), :]
        other = other_ref[pl.ds(k, 64, 8), :]
        even = jnp.where(core == 0, own, other)
        odd = jnp.where(core == 0, other, own)
        pieces = []
        for x in range(4):
            pieces += [even[16 * x : 16 * x + 16], odd[16 * x : 16 * x + 16]]
        fields.append(stacked(pieces))
    u, v, t, volume, m_xx, m_yy, m_xy, planet = fields
    contra_u = m_xx * u + m_xy * v
    contra_v = m_xy * u + m_yy * v
    energy = 0.5 * (u * contra_u + v * contra_v) + t
    grad_x, grad_y = gradient(stacked([u, v, t, energy]), wide_ref)
    dy_u, dx_v = grad_y[:ROWS], grad_x[ROWS : 2 * ROWS]
    dx_t, dy_t = grad_x[2 * ROWS : 3 * ROWS], grad_y[2 * ROWS : 3 * ROWS]
    dx_e, dy_e = grad_x[3 * ROWS :], grad_y[3 * ROWS :]
    absolute = dx_v - dy_u + planet * volume
    mass = mass_weight() * volume
    raw_u = u + time_step * (absolute * contra_v - dx_e)
    raw_v = v + time_step * (-absolute * contra_u - dy_e)
    raw_t = t - time_step * (contra_u * dx_t + contra_v * dy_t)
    values = stacked([mass * raw_u, mass * raw_v, mass * raw_t, mass])
    sums = dot(stacked(split(values), 1), of(wide_ref, "both"))
    for ch in range(4):
        part = slice(ROWS * ch, ROWS * ch + ROWS)
        fields_ref[part, :] = assembled(sums[part, :LANES], sums[part, LANES:])
    for k, field in enumerate([m_xx, m_xy, m_yy]):
        fields_ref[ROWS * (4 + k) : ROWS * (5 + k), :] = volume * field
    put_strips(fields_ref, nbr_ref, face, send_ref, wide_ref, narrow_ref)


def laplace(fields, metric, wide_ref):
    flux_xx, flux_xy, flux_yy = metric
    count = flux_xx.shape[0]
    grad_x, grad_y = gradient(stacked(fields), wide_ref)
    flux = []
    for ch in range(3):
        part = slice(count * ch, count * ch + count)
        flux.append(
            stacked(
                [
                    flux_xx * grad_x[part] + flux_xy * grad_y[part],
                    flux_xy * grad_x[part] + flux_yy * grad_y[part],
                ],
                1,
            )
        )
    high, mid, low = split(stacked(flux))
    sums = dot(stacked([high, mid, low, high, mid, high], 1), of(wide_ref, "spread"))
    return [
        assembled(sums[count * ch : count * ch + count, :LANES], sums[count * ch : count * ch + count, LANES:])
        for ch in range(3)
    ]


def second_kernel(nbr_ref, got_ref, fields_ref, wide_ref, narrow_ref, mask_ref, out_ref, total_ref):
    face = lax.axis_index("face")
    core = lax.axis_index("fy") % 2
    ring_fields = ring_of(nbr_ref, face, got_ref, narrow_ref)
    metric = [
        stacked([fields_ref[ROWS * k : ROWS * k + ROWS, :], ring_fields[k]]) for k in range(4, 7)
    ]
    total_ref[...] = fields_ref[: 4 * ROWS, :]
    ring = join(total_ref, ring_fields[:4], 4, narrow_ref, mask_ref)
    share = 1.0 / stacked([total_ref[3 * ROWS : 4 * ROWS, :], ring[3]])
    fields = [
        stacked([total_ref[ROWS * ch : ROWS * ch + ROWS, :], ring[ch]]) * share for ch in range(3)
    ]
    sectioned = [field[:ROWS] for field in fields]
    for step in range(2):
        sums = laplace(fields, metric, wide_ref)
        for ch in range(3):
            total_ref[ROWS * ch : ROWS * ch + ROWS, :] = sums[ch][:ROWS]
        ring = join(
            total_ref, [field[ROWS:] for field in sums], 3, narrow_ref, mask_ref, step == 0
        )
        if step == 0:
            fields = [
                stacked([total_ref[ROWS * ch : ROWS * ch + ROWS, :], ring[ch]]) * share
                for ch in range(3)
            ]
    for ch in range(3):
        part = slice(ROWS * ch, ROWS * ch + ROWS)
        total_ref[part, :] = sectioned[ch] - hyper_coeff * (total_ref[part, :] * share[:ROWS])
    for x in range(4):
        for ch in range(3):
            start = pl.multiple_of(ROWS * ch + 32 * x + 16 * core, 16)
            out_ref[16 * x : 16 * x + 16, 0, LANES * ch : LANES * ch + LANES] = total_ref[
                pl.ds(start, 16), :
            ]


def unpack_kernel(got_ref, out_ref):
    levels = got_ref[...]
    columns = stacked([levels[:, 0, LANES * ch : LANES * ch + LANES] for ch in range(3)])
    out_ref[...] = jnp.transpose(columns)


def f32(*shape):
    return jax.ShapeDtypeStruct(shape, jnp.float32)


def near(*shape):
    return pltpu.VMEM(shape, jnp.float32)


def held(values):
    return pltpu.with_memory_space_constraint(values, pltpu.VMEM)


VMEM = pl.BlockSpec(memory_space=pltpu.VMEM)
SMEM = pl.BlockSpec(memory_space=pltpu.SMEM)


def call(kernel, outs, ins, scratch=(), name=None):
    return pl.pallas_call(
        kernel,
        out_shape=outs,
        in_specs=ins,
        out_specs=jax.tree.map(lambda _: VMEM, outs),
        scratch_shapes=scratch,
        name=name,
    )


def level_groups():
    return [
        [(8 * face + 2 * x + core) * 16 + fx for x in range(4) for fx in range(16)]
        for face in range(FACES)
        for core in range(2)
    ]


def per_device(state, jacobian, metric_diag, metric_cross, coriolis, nbr_face, nbr_edge):
    axes = ("face", "fy", "fx")
    groups = level_groups()
    wide, narrow = held(jnp.asarray(WIDE)), held(jnp.asarray(NARROW))

    packed = call(pack_kernel, near(512, LANES), [VMEM] * 5, name="pack")(
        state.reshape(128, 192),
        jacobian[0].T,
        metric_diag[:, 0].transpose(0, 2, 1),
        metric_cross[0].T,
        coriolis[0].T,
    )
    own = lax.all_to_all(
        packed.reshape(64, 8, LANES), axes, 0, 0, axis_index_groups=groups, tiled=True
    )
    other = lax.ppermute(own, "fy", [(i, i ^ 1) for i in range(8)])
    fields, send = call(
        first_kernel,
        [near(7 * ROWS, LANES), near(SLOT * FACES, LANES)],
        [SMEM] + [VMEM] * 4,
        name="first",
    )(nbr_face.T, held(own.reshape(512, LANES)), held(other.reshape(512, LANES)), wide, narrow)
    got = lax.all_to_all(send.reshape(FACES, SLOT, LANES), "face", 0, 0, tiled=True)
    updated = call(
        second_kernel,
        near(64, 1, 3 * LANES),
        [SMEM] + [VMEM] * 5,
        [pltpu.VMEM((4 * ROWS, LANES), jnp.float32)],
        name="second",
    )(nbr_face.T, held(got.reshape(SLOT * FACES, LANES)), held(fields), wide, narrow, MASKS)
    back = lax.all_to_all(
        updated, axes, 0, 0, axis_index_groups=groups, tiled=True
    )
    nodes = call(unpack_kernel, f32(128, 192), [VMEM], name="unpack")(
        held(back)
    )
    return nodes.reshape(1, 16, 8, 192)


def solution(mesh):
    return jax.shard_map(
        per_device,
        mesh=mesh,
        in_specs=(
            P("face", "fy", "fx", None),
            P("face", "fy", "fx"),
            P(None, "face", "fy", "fx"),
            P("face", "fy", "fx"),
            P("face", "fy", "fx"),
            P(),
            P(),
        ),
        out_specs=P("face", "fy", "fx", None),
        check_vma=False,
    )
```

time: 101 us -> 106 us (1.050)
  local copies, waits for them, and re-layouts: 0 us -> 10.1 us
  Pallas kernels: 12.6 us -> 9.11 us
    unnamed x0 -> x20, local copies, waits for them, and re-layouts: none -> 10.1 us
    pallas_call x2, Pallas kernels: 10.7 us -> 7.19 us  [the longest x1 4.71 us: per_device(): call(second_kernel, near(64, 1, 3 * LANES), [SMEM] + [VMEM] * 5, [pltpu.V...]
where the time goes in v4:
time: 106 us; the launch traced here: 105 us
  blocking collectives  83.5 us (79%)
  local copies, waits for them, and re-layouts  10.1 us (10%)
  Pallas kernels  9.11 us (9%)
  starting transfers between devices  1.91 us (2%)
    all_to_all x1, blocking collectives, per_device(): lax.all_to_all(packed.reshape(64, 8, LANES), axes, 0, 0, axis_index_group...  39.6 us
    all_to_all x1, blocking collectives, per_device(): lax.all_to_all(updated, axes, 0, 0, axis_index_groups=groups, tiled=True)  22 us
    all_to_all x1, blocking collectives, per_device(): lax.all_to_all(send.reshape(FACES, SLOT, LANES), 'face', 0, 0, tiled=True)  21.9 us
    unnamed x20, local copies, waits for them, and re-layouts  10.1 us
    pallas_call x1, Pallas kernels, per_device(): call(second_kernel, near(64, 1, 3 * LANES), [SMEM] + [VMEM] * 5, [pltpu.V...  4.71 us
    pallas_call x1, Pallas kernels, per_device(): call(first_kernel, [near(7 * ROWS, LANES), near(SLOT * FACES, LANES)], [S...  2.48 us
  transfers between devices with their start and end apart: 1, of which 1 were waited for; matrix products, arithmetic and copies ran while one was open for 0% of the time, Pallas kernels for 0%

profile of v4, /device:TPU:2, one launch (start us, length us, event | category | flops | bytes accessed | tf_op | source)
XLA Modules:
  0.0 105.5 jit_solution(10614498216717124852)
XLA Ops:
  0.0 1.1 %pack.1 = f32[512,128]{1,0:T(8,128)S(1)} custom-call(f32[128,192]{1,0:T(8,128)} %bitcast.25, f32[8,16]{1,0:T(8,128)} %bitcast.29, f32[2,8,16]{2,1,0:T(8,128)} %bitcast.26, f32[8,16]{1,0:T(8,128)} %bitcast.30, f32[8,16]{1,0:T(8,128)} %bitcast.31), custom_call_target="tpu_custom_call" | custom-call | tf_op jit(solution)/shard_map/pack/pallas_call | solution.py:553
  1.1 39.6 %all_to_all.15 = f32[64,8,128]{2,1,0:T(8,128)S(1)} all-to-all(f32[64,8,128]{2,1,0:T(8,128)S(1)} %bitcast.21), channel_id=1, replica_groups={{0,1,2,3,4,5,6,7,8,9,10,11,12,13,14,15,32,33,34,35,36,37,38,39,40,41,42..., dimensions={0} | all-to-all | bytes 524288 | tf_op jit(solution)/shard_map/all_to_all | solution.py:560
  40.7 1.9 %collective-permute-start = (f32[64,8,128]{2,1,0:T(8,128)S(1)}, f32[64,8,128]{2,1,0:T(8,128)S(1)}, u32[]{:S(2)}, u32[]{:S(2)}) collective-permute-start(f32[64,8,128]{2,1,0:T(8,128)S(1)} %all_to_all.15), channel_id=1, source_target_pairs={{0,16},{16,0},{32,48},{48,32},{64,80},{80,64},{96,112},{112,96},{1... | collective-permute-start | bytes 786440 | tf_op jit(solution)/shard_map/ppermute | solution.py:563
  42.7 0.0 copy-start.4
  42.7 0.7 copy-done.4
  43.4 0.8 collective-permute-done
  44.2 0.0 copy-start.8
  44.2 0.7 copy-done.8
  44.9 0.0 copy-start
  44.9 1.4 %copy-done = bf16[2944,256]{1,0:T(8,128)(2,1)S(1)} copy-done((bf16[2944,256]{1,0:T(8,128)(2,1)S(1)}, bf16[2944,256]{1,0:T(8,128)(2,1)}, u32[]{:S(2)}) %copy-start) | copy-done | bytes 1507352
  46.2 0.0 copy-start.2
  46.2 1.1 %copy-done.2 = bf16[3072,128]{1,0:T(8,128)(2,1)S(1)} copy-done((bf16[3072,128]{1,0:T(8,128)(2,1)S(1)}, bf16[3072,128]{1,0:T(8,128)(2,1)}, u32[]{:S(2)}) %copy-start.2) | copy-done | bytes 786456
  47.4 0.0 copy-start.5
  47.4 0.9 copy-done.5
  48.3 0.0 copy-start.9
  48.3 0.9 copy-done.9
  49.3 2.5 %first.1 = (f32[896,128]{1,0:T(8,128)S(1)}, f32[336,128]{1,0:T(8,128)S(1)}) custom-call(s32[4,6]{1,0:T(4,128)} %bitcast.27, f32[512,128]{1,0:T(8,128)S(1)} %bitcast.20, f32[512,128]{1,0:T(8,128)S(1)} %bitcast.23, bf16[2944,256]{1,0:T(8,128)(2,1)S(1)} %copy-done, bf16[3072,128]{1,0:T(8,128)(2,1)S(1)} %copy-done.2), custom_call_target="tpu_custom_call" | custom-call | tf_op jit(solution)/shard_map/first/pallas_call | solution.py:564
  51.8 0.0 copy-start.6
  51.8 0.8 copy-done.6
  52.5 21.9 %all_to_all.16 = f32[6,56,128]{2,1,0:T(8,128)S(1)} all-to-all(f32[6,56,128]{2,1,0:T(8,128)S(1)} %bitcast.24), channel_id=1, replica_groups=mesh['face'=6,'fy'=8,'fx'=16] {'face'}, dimensions={0} | all-to-all | bytes 344064 | tf_op jit(solution)/shard_map/all_to_all | solution.py:570
  74.4 0.0 copy-start.1
  74.4 1.4 %copy-done.1 = bf16[2944,256]{1,0:T(8,128)(2,1)S(1)} copy-done((bf16[2944,256]{1,0:T(8,128)(2,1)S(1)}, bf16[2944,256]{1,0:T(8,128)(2,1)}, u32[]{:S(2)}) %copy-start.1) | copy-done | bytes 1507352
  75.8 0.0 copy-start.3
  75.8 1.1 %copy-done.3 = bf16[3072,128]{1,0:T(8,128)(2,1)S(1)} copy-done((bf16[3072,128]{1,0:T(8,128)(2,1)S(1)}, bf16[3072,128]{1,0:T(8,128)(2,1)}, u32[]{:S(2)}) %copy-start.3) | copy-done | bytes 786456
  76.9 0.0 copy-start.7
  76.9 1.0 copy-done.7
  78.0 4.7 %second.1 = f32[64,1,384]{2,1,0:T(1,128)S(1)} custom-call(s32[4,6]{1,0:T(4,128)} %bitcast.28, f32[336,128]{1,0:T(8,128)S(1)} %bitcast.22, f32[896,128]{1,0:T(8,128)S(1)} %copy-done.7, bf16[2944,256]{1,0:T(8,128)(2,1)S(1)} %copy-done.1, bf16[3072,128]{1,0:T(8,128)(2,1)S(1)} %copy-done.3, f32[32,128]{1,0:T(8,128)} %constant.8.clone.mask_ref), custom_call_target="tpu_custom_call" | custom-call | tf_op jit(solution)/shard_map/second/pallas_call | solution.py:571
  82.7 22.0 %all_to_all.17.got_ref = f32[64,1,384]{2,1,0:T(1,128)S(1)} all-to-all(f32[64,1,384]{2,1,0:T(1,128)S(1)} %second.1), channel_id=1, replica_groups={{0,1,2,3,4,5,6,7,8,9,10,11,12,13,14,15,32,33,34,35,36,37,38,39,40,41,42..., dimensions={0} | all-to-all | bytes 196608 | tf_op jit(solution)/shard_map/all_to_all | solution.py:578
  104.7 0.8 unpack.1
Async XLA Ops:
  40.7 3.4 %collective-permute-start = (f32[64,8,128]{2,1,0:T(8,128)S(1)}, f32[64,8,128]{2,1,0:T(8,128)S(1)}, u32[]{:S(2)}, u32[]{:S(2)}) collective-permute-start(f32[64,8,128]{2,1,0:T(8,128)S(1)} %all_to_all.15), channel_id=1, source_target_pairs={{0,16},{16,0},{32,48},{48,32},{64,80},{80,64},{96,112},{112,96},{1... | collective-permute-start | bytes 786440 | tf_op jit(solution)/shard_map/ppermute | solution.py:563
  42.7 0.7 copy-start.4
  44.2 0.7 copy-start.8
  44.9 1.4 %copy-start = (bf16[2944,256]{1,0:T(8,128)(2,1)S(1)}, bf16[2944,256]{1,0:T(8,128)(2,1)}, u32[]{:S(2)}) copy-start(bf16[2944,256]{1,0:T(8,128)(2,1)} %constant.6.clone.wide_ref) | copy-start | bytes 4521988
  46.2 1.1 %copy-start.2 = (bf16[3072,128]{1,0:T(8,128)(2,1)S(1)}, bf16[3072,128]{1,0:T(8,128)(2,1)}, u32[]{:S(2)}) copy-start(bf16[3072,128]{1,0:T(8,128)(2,1)} %constant.7.clone.narrow_ref) | copy-start | bytes 2359300
  47.4 0.9 copy-start.5
  48.3 0.9 copy-start.9
  51.8 0.8 copy-start.6
  74.4 1.4 %copy-start.1 = (bf16[2944,256]{1,0:T(8,128)(2,1)S(1)}, bf16[2944,256]{1,0:T(8,128)(2,1)}, u32[]{:S(2)}) copy-start(bf16[2944,256]{1,0:T(8,128)(2,1)} %constant.6.clone.wide_ref) | copy-start | bytes 4521988
  75.8 1.1 %copy-start.3 = (bf16[3072,128]{1,0:T(8,128)(2,1)S(1)}, bf16[3072,128]{1,0:T(8,128)(2,1)}, u32[]{:S(2)}) copy-start(bf16[3072,128]{1,0:T(8,128)(2,1)} %constant.7.clone.narrow_ref) | copy-start | bytes 2359300
  76.9 1.0 copy-start.7

commit v5 on v4

--- a/solution.py
+++ b/solution.py
@@ -95,36 +95,26 @@
     weighted = np.diag(weights[r % 4] * weights[c % 4])
     spread = in_parts(np.concatenate([along_x @ weighted @ both, along_y @ weighted @ both], 0))
 
-    wide = {
-        "gradient": np.concatenate([gradient[n] for n in (0, 0, 1, 1, 0, 2)], 0),
-        "spread": np.concatenate([spread[n] for n in (0, 0, 0, 1, 1, 2)], 0),
-        "both": np.concatenate([both] * 3, 0),
-    }
-    narrow = {"reverse": np.eye(LANES)[::-1]}
-    narrow["reverse_rows"] = np.kron(np.eye(8), np.eye(16)[::-1])
-    for edge, name in ((1, "east"), (3, "west")):
-        out = np.zeros((2, LANES, LANES))
-        out_rows = np.zeros((LANES, LANES))
-        into = np.zeros((2, LANES, LANES))
-        into_rows = np.zeros((LANES, LANES))
+    out, out_rows, into, into_rows = [], [], [], []
+    for edge in (1, 3):
+        out.append(np.zeros((2, LANES, LANES)))
+        out_rows.append(np.zeros((LANES, LANES)))
+        into.append(np.zeros((2, LANES, LANES)))
+        into_rows.append(np.zeros((LANES, LANES)))
         for k in range(128):
             j, i = k // 8, k % 8
             j2, i2 = (127 - k) // 8, (127 - k) % 8
             for depth in range(8):
                 fy, _, at = face_node(edge, depth, k)
-                out[j % 2, at, 8 * depth + i] = 1.0
+                out[-1][j % 2, at, 8 * depth + i] = 1.0
                 ring_fy, ring_at = ring_node(edge, depth, k)
-                into[j2 % 2, 8 * depth + i2, ring_at] = 1.0
+                into[-1][j2 % 2, 8 * depth + i2, ring_at] = 1.0
                 for field in range(8):
-                    out_rows[16 * field + j, 64 * (j % 2) + 8 * field + fy] = 1.0
-                    into_rows[64 * (j2 % 2) + 8 * field + ring_fy, 16 * field + j2] = 1.0
-        wide[name + "_out"] = np.concatenate([out[0], out[1]], 1)
-        narrow[name + "_out_rows"] = out_rows
-        narrow[name + "_in_rows"] = into_rows
-        narrow[name + "_in"] = np.concatenate([into[0]] * 3 + [into[1]] * 3, 0)
+                    out_rows[-1][16 * field + j, 64 * (j % 2) + 8 * field + fy] = 1.0
+                    into_rows[-1][64 * (j2 % 2) + 8 * field + ring_fy, 16 * field + j2] = 1.0
     take = np.zeros((LANES, LANES))
     give = np.zeros((LANES, LANES))
-    masks = np.zeros((32, LANES), np.float32)
+    masks = np.zeros((32, 2 * LANES))
     for t, end in enumerate(ENDS):
         for depth in range(8):
             take[end_lane(end, depth), 8 * t + depth] = 1.0
@@ -133,27 +123,64 @@
             masks[8 + t, 8 * t + depth] = 1.0
             masks[16 + t, 8 * MEETS[t] + depth] = 1.0
         masks[24 + t] = TURNS[t]
-    narrow["take"] = np.concatenate([take] * 3, 0)
-    narrow["give"] = np.concatenate([give] * 3, 0)
-
-    arrays, places = [], {}
-    for group in (wide, narrow):
+
+    def pair(left, right):
+        return np.concatenate([left, right], 1)
+
+    reverse = pair(np.eye(LANES)[::-1], np.kron(np.eye(8), np.eye(16)[::-1]))
+    groups = (
+        {
+            "gradient": np.concatenate(gradient, 0),
+            "both": both,
+            "east_out": pair(*out[0]),
+            "west_out": pair(*out[1]),
+            "out_rows": pair(*out_rows),
+            "reverse": reverse,
+        },
+        {
+            "gradient": np.concatenate(gradient, 0),
+            "spread": np.concatenate(spread, 0),
+            "east_in": pair(*into[0]),
+            "west_in": pair(*into[1]),
+            "in_rows": pair(*into_rows),
+            "reverse": reverse,
+            "ends": pair(take, give),
+            "masks": masks,
+        },
+    )
+    arrays, places = [], []
+    for group in groups:
         start = 0
+        places.append({})
         for name, matrix in group.items():
-            places[name] = (start, start + matrix.shape[0])
+            places[-1][name] = (start, start + matrix.shape[0])
             start += matrix.shape[0]
-        arrays.append(
-            np.concatenate([m.astype(ml_dtypes.bfloat16) for m in group.values()], 0)
-        )
-    return arrays[0], arrays[1], masks, places
-
-
-WIDE, NARROW, MASKS, PLACES = tables()
-
-
-def of(ref, name):
-    start, end = PLACES[name]
-    return ref[start:end, :]
+        arrays.append(np.concatenate([m.astype(ml_dtypes.bfloat16) for m in group.values()], 0))
+    return arrays, places
+
+
+TABLES, PLACES = tables()
+
+
+class Table:
+    def __init__(self, ref, which):
+        self.ref, self.places = ref, PLACES[which]
+
+    def whole(self, name):
+        start, end = self.places[name]
+        return self.ref[start:end, :]
+
+    def left(self, name):
+        start, end = self.places[name]
+        return self.ref[start:end, :LANES]
+
+    def right(self, name):
+        start, end = self.places[name]
+        return self.ref[start:end, LANES:]
+
+    def part(self, name, n, rows):
+        start = self.places[name][0] + n * rows
+        return self.ref[start : start + rows, :]
 
 
 def roll(values, shift, axis):
@@ -179,9 +206,10 @@
     return high, mid, (rest - mid.astype(jnp.float32)).astype(jnp.bfloat16)
 
 
-def gradient(values, wide_ref):
+def gradient(values, table):
     high, mid, low = split(values)
-    both = dot(stacked([high, mid, high, mid, low, high], 1), of(wide_ref, "gradient"))
+    parts = [table.part("gradient", n, LANES) for n in (0, 0, 1, 1, 0, 2)]
+    both = dot(stacked([high, mid, high, mid, low, high], 1), stacked(parts))
     return both[:, :LANES], both[:, LANES:]
 
 
@@ -249,24 +277,25 @@
     return v, -u
 
 
-def ends_meet(ring, channels, narrow_ref, mask_ref):
+def ends_meet(ring, channels, table):
     ends = stacked(
         [ring[ch][row : row + 1] for ch in range(channels) for row in END_ROWS]
     )
-    own = stacked([mask_ref[0:8, :]] * channels)
-    taken = dot(stacked(split(ends * own), 1), of(narrow_ref, "take"))
+    masks = table.left("masks").astype(jnp.float32)
+    own = stacked([masks[0:8]] * channels)
+    taken = dot(stacked(split(ends * own), 1), stacked([table.left("ends")] * 3))
     lines = []
     for ch in range(channels):
-        line = jnp.sum(taken[8 * ch : 8 * ch + 8] * mask_ref[8:16, :], axis=0, keepdims=True)
-        lines.append(line * mask_ref[16:24, :])
-    given = dot(stacked(split(stacked(lines)), 1), of(narrow_ref, "give"))
+        line = jnp.sum(taken[8 * ch : 8 * ch + 8] * masks[8:16], axis=0, keepdims=True)
+        lines.append(line * masks[16:24])
+    given = dot(stacked(split(stacked(lines)), 1), stacked([table.right("ends")] * 3))
     given = [given[8 * ch : 8 * ch + 8] for ch in range(channels)]
-    sense = mask_ref[24:32, :]
+    sense = masks[24:32]
     return [-sense * given[1], sense * given[0], *given[2:]]
 
 
-def join(face_ref, ring, channels, narrow_ref, mask_ref, ring_too=True):
-    ends = ends_meet(ring, channels, narrow_ref, mask_ref) if ring_too else None
+def join(face_ref, ring, channels, table, ring_too=True):
+    ends = ends_meet(ring, channels, table) if ring_too else None
     totals = []
     for ch in range(channels):
         south, north = ring[ch][0:16], ring[ch][16:32]
@@ -311,7 +340,11 @@
     return totals
 
 
-def pack_kernel(state_ref, jac_ref, diag_ref, cross_ref, cor_ref, out_ref):
+def pack_kernel(
+    state_ref, jac_ref, diag_ref, cross_ref, cor_ref, later_ref, out_ref, kept_ref, sem
+):
+    keep = pltpu.make_async_copy(later_ref, kept_ref, sem)
+    keep.start()
     turned_state = jnp.transpose(state_ref[...])
     for part in range(3):
         out_ref[pl.ds(part, 64, 8), :] = turned_state[64 * part : 64 * part + 64]
@@ -327,39 +360,41 @@
     for k in range(5):
         line = jnp.sum(lines[8 * k : 8 * k + 8] * mask, axis=0, keepdims=True)
         out_ref[pl.ds(3 + k, 64, 8), :] = jnp.broadcast_to(line, (64, LANES))
-
-
-def reversed_blocks(rows, narrow_ref):
+    keep.wait()
+
+
+def reversed_blocks(rows, table):
     parts = stacked([part.astype(jnp.float32) for part in split(rows)]).astype(jnp.bfloat16)
-    moved = dot(parts, of(narrow_ref, "reverse"))
+    moved = dot(parts, table.left("reverse"))
     count = rows.shape[0]
     moved = stacked([moved[n * count : n * count + count] for n in range(3)], 1)
-    moved = dot(of(narrow_ref, "reverse_rows"), moved.astype(jnp.bfloat16))
+    moved = dot(table.right("reverse"), moved.astype(jnp.bfloat16))
     return moved[:, :LANES] + moved[:, LANES : 2 * LANES] + moved[:, 2 * LANES :]
 
 
-def strip_of(edge, fields_ref, wide_ref, narrow_ref):
+def strip_of(edge, fields_ref, table):
     rows = [fields_ref[rim_rows(edge, ROWS * k), :] for k in range(7)]
     rows = stacked([*rows, jnp.zeros_like(rows[0])])
     if edge == 0:
         return rows
     if edge == 2:
-        return reversed_blocks(rows, narrow_ref)
+        return reversed_blocks(rows, table)
     name = "east" if edge == 1 else "west"
-    moved = dot(stacked(split(rows)), of(wide_ref, name + "_out"))
+    moved = dot(stacked(split(rows)), table.whole(name + "_out"))
     halves = stacked([moved[:, :LANES], moved[:, LANES:]], 0)
     moved = stacked(
         [stacked([halves[64 * n : 64 * n + 64], halves[192 + 64 * n : 256 + 64 * n]]) for n in range(3)],
         1,
     )
-    moved = dot(of(narrow_ref, name + "_out_rows"), moved.astype(jnp.bfloat16))
+    order = table.left("out_rows") if edge == 1 else table.right("out_rows")
+    moved = dot(order, moved.astype(jnp.bfloat16))
     return moved[:, :LANES] + moved[:, LANES : 2 * LANES] + moved[:, 2 * LANES :]
 
 
-def put_strips(fields_ref, nbr_ref, face, send_ref, wide_ref, narrow_ref):
+def put_strips(fields_ref, nbr_ref, face, send_ref, table):
     near = iota((16, LANES), 1) < 64
     for edge in range(EDGES):
-        rows = strip_of(edge, fields_ref, wide_ref, narrow_ref)
+        rows = strip_of(edge, fields_ref, table)
         u, v, t, mass, flux_xx, flux_xy, flux_yy = [rows[16 * k : 16 * k + 16] for k in range(7)]
         u, v = turned(u, v, -edge)
         if edge % 2:
@@ -373,7 +408,7 @@
         send_ref[pl.ds(start, SLOT), :] = stacked(slot)
 
 
-def ring_of(nbr_ref, face, got_ref, narrow_ref):
+def ring_of(nbr_ref, face, got_ref, table):
     near = iota((16, LANES), 1) < 64
     strips = []
     for edge in range(EDGES):
@@ -389,12 +424,14 @@
         rows = stacked([*fields, jnp.zeros_like(near, jnp.float32)])
         count = 16
         if edge == 0:
-            rows = reversed_blocks(rows, narrow_ref)
+            rows = reversed_blocks(rows, table)
         elif edge % 2:
             name = "east" if edge == 1 else "west"
-            moved = dot(of(narrow_ref, name + "_in_rows"), stacked(split(rows), 1))
+            order = table.left("in_rows") if edge == 1 else table.right("in_rows")
+            moved = dot(order, stacked(split(rows), 1))
             moved = stacked([moved[:64], moved[64:]], 1)
-            rows = dot(moved.astype(jnp.bfloat16), of(narrow_ref, name + "_in"))
+            into = [table.left(name + "_in")] * 3 + [table.right(name + "_in")] * 3
+            rows = dot(moved.astype(jnp.bfloat16), stacked(into))
             count = 8
         fields = [rows[count * k : count * k + count] for k in range(7)]
         fields[0], fields[1] = turned(fields[0], fields[1], edge + 2)
@@ -407,7 +444,12 @@
     return [stacked([strips[edge][k] for edge in (0, 2, 1, 3)]) for k in range(7)]
 
 
-def first_kernel(nbr_ref, own_ref, other_ref, wide_ref, narrow_ref, fields_ref, send_ref):
+def first_kernel(
+    nbr_ref, own_ref, other_ref, table_ref, later_ref, fields_ref, send_ref, kept_ref, sem
+):
+    keep = pltpu.make_async_copy(later_ref, kept_ref, sem)
+    keep.start()
+    table = Table(table_ref, 0)
     core = lax.axis_index("fy") % 2
     face = lax.axis_index("face")
     fields = []
@@ -424,7 +466,7 @@
     contra_u = m_xx * u + m_xy * v
     contra_v = m_xy * u + m_yy * v
     energy = 0.5 * (u * contra_u + v * contra_v) + t
-    grad_x, grad_y = gradient(stacked([u, v, t, energy]), wide_ref)
+    grad_x, grad_y = gradient(stacked([u, v, t, energy]), table)
     dy_u, dx_v = grad_y[:ROWS], grad_x[ROWS : 2 * ROWS]
     dx_t, dy_t = grad_x[2 * ROWS : 3 * ROWS], grad_y[2 * ROWS : 3 * ROWS]
     dx_e, dy_e = grad_x[3 * ROWS :], grad_y[3 * ROWS :]
@@ -434,19 +476,20 @@
     raw_v = v + time_step * (-absolute * contra_u - dy_e)
     raw_t = t - time_step * (contra_u * dx_t + contra_v * dy_t)
     values = stacked([mass * raw_u, mass * raw_v, mass * raw_t, mass])
-    sums = dot(stacked(split(values), 1), of(wide_ref, "both"))
+    sums = dot(stacked(split(values), 1), stacked([table.whole("both")] * 3))
     for ch in range(4):
         part = slice(ROWS * ch, ROWS * ch + ROWS)
         fields_ref[part, :] = assembled(sums[part, :LANES], sums[part, LANES:])
     for k, field in enumerate([m_xx, m_xy, m_yy]):
         fields_ref[ROWS * (4 + k) : ROWS * (5 + k), :] = volume * field
-    put_strips(fields_ref, nbr_ref, face, send_ref, wide_ref, narrow_ref)
-
-
-def laplace(fields, metric, wide_ref):
+    put_strips(fields_ref, nbr_ref, face, send_ref, table)
+    keep.wait()
+
+
+def laplace(fields, metric, table):
     flux_xx, flux_xy, flux_yy = metric
     count = flux_xx.shape[0]
-    grad_x, grad_y = gradient(stacked(fields), wide_ref)
+    grad_x, grad_y = gradient(stacked(fields), table)
     flux = []
     for ch in range(3):
         part = slice(count * ch, count * ch + count)
@@ -460,34 +503,34 @@
             )
         )
     high, mid, low = split(stacked(flux))
-    sums = dot(stacked([high, mid, low, high, mid, high], 1), of(wide_ref, "spread"))
+    parts = [table.part("spread", n, 2 * LANES) for n in (0, 0, 0, 1, 1, 2)]
+    sums = dot(stacked([high, mid, low, high, mid, high], 1), stacked(parts))
     return [
         assembled(sums[count * ch : count * ch + count, :LANES], sums[count * ch : count * ch + count, LANES:])
         for ch in range(3)
     ]
 
 
-def second_kernel(nbr_ref, got_ref, fields_ref, wide_ref, narrow_ref, mask_ref, out_ref, total_ref):
+def second_kernel(nbr_ref, got_ref, fields_ref, table_ref, out_ref, total_ref):
+    table = Table(table_ref, 1)
     face = lax.axis_index("face")
     core = lax.axis_index("fy") % 2
-    ring_fields = ring_of(nbr_ref, face, got_ref, narrow_ref)
+    ring_fields = ring_of(nbr_ref, face, got_ref, table)
     metric = [
         stacked([fields_ref[ROWS * k : ROWS * k + ROWS, :], ring_fields[k]]) for k in range(4, 7)
     ]
     total_ref[...] = fields_ref[: 4 * ROWS, :]
-    ring = join(total_ref, ring_fields[:4], 4, narrow_ref, mask_ref)
+    ring = join(total_ref, ring_fields[:4], 4, table)
     share = 1.0 / stacked([total_ref[3 * ROWS : 4 * ROWS, :], ring[3]])
     fields = [
         stacked([total_ref[ROWS * ch : ROWS * ch + ROWS, :], ring[ch]]) * share for ch in range(3)
     ]
     sectioned = [field[:ROWS] for field in fields]
     for step in range(2):
-        sums = laplace(fields, metric, wide_ref)
+        sums = laplace(fields, metric, table)
         for ch in range(3):
             total_ref[ROWS * ch : ROWS * ch + ROWS, :] = sums[ch][:ROWS]
-        ring = join(
-            total_ref, [field[ROWS:] for field in sums], 3, narrow_ref, mask_ref, step == 0
-        )
+        ring = join(total_ref, [field[ROWS:] for field in sums], 3, table, step == 0)
         if step == 0:
             fields = [
                 stacked([total_ref[ROWS * ch : ROWS * ch + ROWS, :], ring[ch]]) * share
@@ -518,12 +561,17 @@
     return pltpu.VMEM(shape, jnp.float32)
 
 
+def kept(table):
+    return pltpu.VMEM(table.shape, jnp.bfloat16)
+
+
 def held(values):
     return pltpu.with_memory_space_constraint(values, pltpu.VMEM)
 
 
 VMEM = pl.BlockSpec(memory_space=pltpu.VMEM)
 SMEM = pl.BlockSpec(memory_space=pltpu.SMEM)
+ANY = pl.BlockSpec(memory_space=pl.ANY)
 
 
 def call(kernel, outs, ins, scratch=(), name=None):
@@ -548,33 +596,46 @@
 def per_device(state, jacobian, metric_diag, metric_cross, coriolis, nbr_face, nbr_edge):
     axes = ("face", "fy", "fx")
     groups = level_groups()
-    wide, narrow = held(jnp.asarray(WIDE)), held(jnp.asarray(NARROW))
-
-    packed = call(pack_kernel, near(512, LANES), [VMEM] * 5, name="pack")(
+    tables = [jnp.asarray(table) for table in TABLES]
+    packed, table = call(
+        pack_kernel,
+        [near(512, LANES), kept(TABLES[0])],
+        [VMEM] * 5 + [ANY],
+        [pltpu.SemaphoreType.DMA],
+        name="pack",
+    )(
         state.reshape(128, 192),
         jacobian[0].T,
         metric_diag[:, 0].transpose(0, 2, 1),
         metric_cross[0].T,
         coriolis[0].T,
+        tables[0],
     )
     own = lax.all_to_all(
         packed.reshape(64, 8, LANES), axes, 0, 0, axis_index_groups=groups, tiled=True
     )
     other = lax.ppermute(own, "fy", [(i, i ^ 1) for i in range(8)])
-    fields, send = call(
+    fields, send, table = call(
         first_kernel,
-        [near(7 * ROWS, LANES), near(SLOT * FACES, LANES)],
-        [SMEM] + [VMEM] * 4,
+        [near(7 * ROWS, LANES), near(SLOT * FACES, LANES), kept(TABLES[1])],
+        [SMEM] + [VMEM] * 3 + [ANY],
+        [pltpu.SemaphoreType.DMA],
         name="first",
-    )(nbr_face.T, held(own.reshape(512, LANES)), held(other.reshape(512, LANES)), wide, narrow)
+    )(
+        nbr_face.T,
+        held(own.reshape(512, LANES)),
+        held(other.reshape(512, LANES)),
+        held(table),
+        tables[1],
+    )
     got = lax.all_to_all(send.reshape(FACES, SLOT, LANES), "face", 0, 0, tiled=True)
     updated = call(
         second_kernel,
         near(64, 1, 3 * LANES),
-        [SMEM] + [VMEM] * 5,
+        [SMEM] + [VMEM] * 3,
         [pltpu.VMEM((4 * ROWS, LANES), jnp.float32)],
         name="second",
-    )(nbr_face.T, held(got.reshape(SLOT * FACES, LANES)), held(fields), wide, narrow, MASKS)
+    )(nbr_face.T, held(got.reshape(SLOT * FACES, LANES)), held(fields), held(table))
     back = lax.all_to_all(
         updated, axes, 0, 0, axis_index_groups=groups, tiled=True
     )

time: 106 us -> 97.3 us (0.918)
  local copies, waits for them, and re-layouts: 10.1 us -> 0 us
    unnamed x20 -> x0, local copies, waits for them, and re-layouts: 10.1 us -> none
where the time goes in v5:
time: 97.3 us; the launch traced here: 96.9 us
  blocking collectives  83.5 us (86%)
  Pallas kernels  9.97 us (10%)
  starting transfers between devices  1.91 us (2%)
  waiting for transfers between devices  1.5 us (2%)
    all_to_all x1, blocking collectives, per_device(): lax.all_to_all(packed.reshape(64, 8, LANES), axes, 0, 0, axis_index_group...  39.6 us
    all_to_all x1, blocking collectives, per_device(): lax.all_to_all(updated, axes, 0, 0, axis_index_groups=groups, tiled=True)  22 us
    all_to_all x1, blocking collectives, per_device(): lax.all_to_all(send.reshape(FACES, SLOT, LANES), 'face', 0, 0, tiled=True)  21.9 us
    pallas_call x1, Pallas kernels, per_device(): call(second_kernel, near(64, 1, 3 * LANES), [SMEM] + [VMEM] * 3, [pltpu.V...  4.69 us
    pallas_call x1, Pallas kernels, per_device(): call(first_kernel, [near(7 * ROWS, LANES), near(SLOT * FACES, LANES), kep...  2.5 us
    pallas_call x1, Pallas kernels, per_device(): call(pack_kernel, [near(512, LANES), kept(TABLES[0])], [VMEM] * 5 + [ANY]...  1.99 us
  transfers between devices with their start and end apart: 1, of which 1 were waited for; matrix products, arithmetic and copies ran while one was open for 0% of the time, Pallas kernels for 0%

profile of v5, /device:TPU:2, one launch (start us, length us, event | category | flops | bytes accessed | tf_op | source)
XLA Modules:
  0.0 96.9 jit_solution(3245348371443565851)
XLA Ops:
  0.0 2.0 %pack.1 = (f32[512,128]{1,0:T(8,128)S(1)}, bf16[1024,256]{1,0:T(8,128)(2,1)S(1)}) custom-call(f32[128,192]{1,0:T(8,128)} %bitcast.25, f32[8,16]{1,0:T(8,128)} %bitcast.29, f32[2,8,16]{2,1,0:T(8,128)} %bitcast.26, f32[8,16]{1,0:T(8,128)} %bitcast.30, f32[8,16]{1,0:T(8,128)} %bitcast.31, bf16[1024,256]{1,0:T(8,128)(2,1)} %constant.4.clone.later_ref), custom_call_target="tpu_custom_call" | custom-call | tf_op jit(solution)/shard_map/pack/pallas_call | solution.py:600
  2.0 39.6 %all_to_all.15 = f32[64,8,128]{2,1,0:T(8,128)S(1)} all-to-all(f32[64,8,128]{2,1,0:T(8,128)S(1)} %bitcast.23), channel_id=1, replica_groups={{0,1,2,3,4,5,6,7,8,9,10,11,12,13,14,15,32,33,34,35,36,37,38,39,40,41,42..., dimensions={0} | all-to-all | bytes 524288 | tf_op jit(solution)/shard_map/all_to_all | solution.py:614
  41.6 1.9 %collective-permute-start = (f32[64,8,128]{2,1,0:T(8,128)S(1)}, f32[64,8,128]{2,1,0:T(8,128)S(1)}, u32[]{:S(2)}, u32[]{:S(2)}) collective-permute-start(f32[64,8,128]{2,1,0:T(8,128)S(1)} %all_to_all.15), channel_id=1, source_target_pairs={{0,16},{16,0},{32,48},{48,32},{64,80},{80,64},{96,112},{112,96},{1... | collective-permute-start | bytes 786440 | tf_op jit(solution)/shard_map/ppermute | solution.py:617
  43.5 1.5 %collective-permute-done = f32[64,8,128]{2,1,0:T(8,128)S(1)} collective-permute-done((f32[64,8,128]{2,1,0:T(8,128)S(1)}, f32[64,8,128]{2,1,0:T(8,128)S(1)}, u32[]{:S(2)}, u32[]{:S(2)}) %collective-permute-start) | collective-permute-done | bytes 262176 | tf_op jit(solution)/shard_map/ppermute | solution.py:617
  45.0 2.5 %first.1 = (f32[896,128]{1,0:T(8,128)S(1)}, f32[336,128]{1,0:T(8,128)S(1)}, bf16[1824,256]{1,0:T(8,128)(2,1)S(1)}) custom-call(s32[4,6]{1,0:T(4,128)} %bitcast.27, f32[512,128]{1,0:T(8,128)S(1)} %bitcast.20, f32[512,128]{1,0:T(8,128)S(1)} %bitcast.22, bf16[1024,256]{1,0:T(8,128)(2,1)S(1)} %get-tuple-element.11.table_ref, ...), custom_call_target="tpu_custom_call" | custom-call | tf_op jit(solution)/shard_map/first/pallas_call | solution.py:618
  47.5 21.9 %all_to_all.16 = f32[6,56,128]{2,1,0:T(8,128)S(1)} all-to-all(f32[6,56,128]{2,1,0:T(8,128)S(1)} %bitcast.24), channel_id=1, replica_groups=mesh['face'=6,'fy'=8,'fx'=16] {'face'}, dimensions={0} | all-to-all | bytes 344064 | tf_op jit(solution)/shard_map/all_to_all | solution.py:631
  69.4 4.7 %second.1 = f32[64,1,384]{2,1,0:T(1,128)S(1)} custom-call(s32[4,6]{1,0:T(4,128)} %bitcast.28, f32[336,128]{1,0:T(8,128)S(1)} %bitcast.21, f32[896,128]{1,0:T(8,128)S(1)} %get-tuple-element.13.fields_ref, bf16[1824,256]{1,0:T(8,128)(2,1)S(1)} %get-tuple-element.14.table_ref), custom_call_target="tpu_custom_call" | custom-call | tf_op jit(solution)/shard_map/second/pallas_call | solution.py:632
  74.1 22.0 %all_to_all.17.got_ref = f32[64,1,384]{2,1,0:T(1,128)S(1)} all-to-all(f32[64,1,384]{2,1,0:T(1,128)S(1)} %second.1), channel_id=1, replica_groups={{0,1,2,3,4,5,6,7,8,9,10,11,12,13,14,15,32,33,34,35,36,37,38,39,40,41,42..., dimensions={0} | all-to-all | bytes 196608 | tf_op jit(solution)/shard_map/all_to_all | solution.py:639
  96.1 0.8 unpack.1
Async XLA Ops:
  41.6 3.4 %collective-permute-start = (f32[64,8,128]{2,1,0:T(8,128)S(1)}, f32[64,8,128]{2,1,0:T(8,128)S(1)}, u32[]{:S(2)}, u32[]{:S(2)}) collective-permute-start(f32[64,8,128]{2,1,0:T(8,128)S(1)} %all_to_all.15), channel_id=1, source_target_pairs={{0,16},{16,0},{32,48},{48,32},{64,80},{80,64},{96,112},{112,96},{1... | collective-permute-start | bytes 786440 | tf_op jit(solution)/shard_map/ppermute | solution.py:617

commit v6 on v5

--- a/solution.py
+++ b/solution.py
@@ -195,6 +195,11 @@
     return jnp.dot(a, b, preferred_element_type=jnp.float32)
 
 
+def dot_halves(a, b):
+    half = a.shape[0] // 32 * 16
+    return jnp.concatenate([dot(a[:half], b), dot(a[half:], b)], axis=0)
+
+
 def stacked(parts, axis=0):
     return jnp.concatenate(parts, axis=axis)
 
@@ -209,7 +214,7 @@
 def gradient(values, table):
     high, mid, low = split(values)
     parts = [table.part("gradient", n, LANES) for n in (0, 0, 1, 1, 0, 2)]
-    both = dot(stacked([high, mid, high, mid, low, high], 1), stacked(parts))
+    both = dot_halves(stacked([high, mid, high, mid, low, high], 1), stacked(parts))
     return both[:, :LANES], both[:, LANES:]
 
 
@@ -340,11 +345,7 @@
     return totals
 
 
-def pack_kernel(
-    state_ref, jac_ref, diag_ref, cross_ref, cor_ref, later_ref, out_ref, kept_ref, sem
-):
-    keep = pltpu.make_async_copy(later_ref, kept_ref, sem)
-    keep.start()
+def pack_kernel(state_ref, jac_ref, diag_ref, cross_ref, cor_ref, out_ref):
     turned_state = jnp.transpose(state_ref[...])
     for part in range(3):
         out_ref[pl.ds(part, 64, 8), :] = turned_state[64 * part : 64 * part + 64]
@@ -360,6 +361,12 @@
     for k in range(5):
         line = jnp.sum(lines[8 * k : 8 * k + 8] * mask, axis=0, keepdims=True)
         out_ref[pl.ds(3 + k, 64, 8), :] = jnp.broadcast_to(line, (64, LANES))
+
+
+def keep_kernel(after_ref, table_ref, kept_ref, sem):
+    del after_ref
+    keep = pltpu.make_async_copy(table_ref, kept_ref, sem)
+    keep.start()
     keep.wait()
 
 
@@ -393,8 +400,8 @@
 
 def put_strips(fields_ref, nbr_ref, face, send_ref, table):
     near = iota((16, LANES), 1) < 64
-    for edge in range(EDGES):
-        rows = strip_of(edge, fields_ref, table)
+    strips = [strip_of(edge, fields_ref, table) for edge in range(EDGES)]
+    for edge, rows in enumerate(strips):
         u, v, t, mass, flux_xx, flux_xy, flux_yy = [rows[16 * k : 16 * k + 16] for k in range(7)]
         u, v = turned(u, v, -edge)
         if edge % 2:
@@ -408,12 +415,14 @@
         send_ref[pl.ds(start, SLOT), :] = stacked(slot)
 
 
-def ring_of(nbr_ref, face, got_ref, table):
+def ring_of(which_ref, got_ref, table):
     near = iota((16, LANES), 1) < 64
     strips = []
     for edge in range(EDGES):
-        start = pl.multiple_of(SLOT * nbr_ref[edge, face], 8)
-        slot = got_ref[pl.ds(start, SLOT), :]
+        slot = got_ref[:SLOT, :]
+        which = jnp.broadcast_to(which_ref[edge : edge + 1, :], (SLOT, LANES))
+        for other in range(1, FACES):
+            slot = jnp.where(which == other, got_ref[SLOT * other : SLOT * other + SLOT, :], slot)
         fields = []
         for n in range(3):
             rows = slot[16 * n : 16 * n + 16]
@@ -445,8 +454,11 @@
 
 
 def first_kernel(
-    nbr_ref, own_ref, other_ref, table_ref, later_ref, fields_ref, send_ref, kept_ref, sem
+    nbr_from, own_ref, other_ref, table_ref, later_ref,
+    fields_ref, send_ref, which_ref, kept_ref, nbr_ref, nbr_sem, sem,
 ):
+    fetch = pltpu.make_async_copy(nbr_from, nbr_ref, nbr_sem)
+    fetch.start()
     keep = pltpu.make_async_copy(later_ref, kept_ref, sem)
     keep.start()
     table = Table(table_ref, 0)
@@ -476,12 +488,15 @@
     raw_v = v + time_step * (-absolute * contra_u - dy_e)
     raw_t = t - time_step * (contra_u * dx_t + contra_v * dy_t)
     values = stacked([mass * raw_u, mass * raw_v, mass * raw_t, mass])
-    sums = dot(stacked(split(values), 1), stacked([table.whole("both")] * 3))
+    sums = dot_halves(stacked(split(values), 1), stacked([table.whole("both")] * 3))
     for ch in range(4):
         part = slice(ROWS * ch, ROWS * ch + ROWS)
         fields_ref[part, :] = assembled(sums[part, :LANES], sums[part, LANES:])
     for k, field in enumerate([m_xx, m_xy, m_yy]):
         fields_ref[ROWS * (4 + k) : ROWS * (5 + k), :] = volume * field
+    fetch.wait()
+    for edge in range(8):
+        which_ref[edge : edge + 1, :] = jnp.full((1, LANES), nbr_ref[edge % EDGES, face], jnp.int32)
     put_strips(fields_ref, nbr_ref, face, send_ref, table)
     keep.wait()
 
@@ -504,18 +519,17 @@
         )
     high, mid, low = split(stacked(flux))
     parts = [table.part("spread", n, 2 * LANES) for n in (0, 0, 0, 1, 1, 2)]
-    sums = dot(stacked([high, mid, low, high, mid, high], 1), stacked(parts))
+    sums = dot_halves(stacked([high, mid, low, high, mid, high], 1), stacked(parts))
     return [
         assembled(sums[count * ch : count * ch + count, :LANES], sums[count * ch : count * ch + count, LANES:])
         for ch in range(3)
     ]
 
 
-def second_kernel(nbr_ref, got_ref, fields_ref, table_ref, out_ref, total_ref):
+def second_kernel(which_ref, got_ref, fields_ref, table_ref, out_ref, total_ref):
     table = Table(table_ref, 1)
-    face = lax.axis_index("face")
     core = lax.axis_index("fy") % 2
-    ring_fields = ring_of(nbr_ref, face, got_ref, table)
+    ring_fields = ring_of(which_ref, got_ref, table)
     metric = [
         stacked([fields_ref[ROWS * k : ROWS * k + ROWS, :], ring_fields[k]]) for k in range(4, 7)
     ]
@@ -570,7 +584,6 @@
 
 
 VMEM = pl.BlockSpec(memory_space=pltpu.VMEM)
-SMEM = pl.BlockSpec(memory_space=pltpu.SMEM)
 ANY = pl.BlockSpec(memory_space=pl.ANY)
 
 
@@ -597,29 +610,38 @@
     axes = ("face", "fy", "fx")
     groups = level_groups()
     tables = [jnp.asarray(table) for table in TABLES]
-    packed, table = call(
-        pack_kernel,
-        [near(512, LANES), kept(TABLES[0])],
-        [VMEM] * 5 + [ANY],
-        [pltpu.SemaphoreType.DMA],
-        name="pack",
-    )(
+    packed = call(pack_kernel, near(512, LANES), [VMEM] * 5, name="pack")(
         state.reshape(128, 192),
         jacobian[0].T,
         metric_diag[:, 0].transpose(0, 2, 1),
         metric_cross[0].T,
         coriolis[0].T,
-        tables[0],
     )
     own = lax.all_to_all(
         packed.reshape(64, 8, LANES), axes, 0, 0, axis_index_groups=groups, tiled=True
     )
     other = lax.ppermute(own, "fy", [(i, i ^ 1) for i in range(8)])
-    fields, send, table = call(
+    table = call(
+        keep_kernel,
+        kept(TABLES[0]),
+        [VMEM, ANY],
+        [pltpu.SemaphoreType.DMA],
+        name="keep",
+    )(held(own.reshape(512, LANES)), tables[0])
+    fields, send, which, table = call(
         first_kernel,
-        [near(7 * ROWS, LANES), near(SLOT * FACES, LANES), kept(TABLES[1])],
-        [SMEM] + [VMEM] * 3 + [ANY],
-        [pltpu.SemaphoreType.DMA],
+        [
+            near(7 * ROWS, LANES),
+            near(SLOT * FACES, LANES),
+            pltpu.VMEM((8, LANES), jnp.int32),
+            kept(TABLES[1]),
+        ],
+        [ANY] + [VMEM] * 3 + [ANY],
+        [
+            pltpu.SMEM((EDGES, FACES), jnp.int32),
+            pltpu.SemaphoreType.DMA,
+            pltpu.SemaphoreType.DMA,
+        ],
         name="first",
     )(
         nbr_face.T,
@@ -632,10 +654,10 @@
     updated = call(
         second_kernel,
         near(64, 1, 3 * LANES),
-        [SMEM] + [VMEM] * 3,
+        [VMEM] * 4,
         [pltpu.VMEM((4 * ROWS, LANES), jnp.float32)],
         name="second",
-    )(nbr_face.T, held(got.reshape(SLOT * FACES, LANES)), held(fields), held(table))
+    )(held(which), held(got.reshape(SLOT * FACES, LANES)), held(fields), held(table))
     back = lax.all_to_all(
         updated, axes, 0, 0, axis_index_groups=groups, tiled=True
     )

time: 97.3 us -> 94.1 us (0.967)
  Pallas kernels: 9.97 us -> 7.87 us
  waiting for transfers between devices: 1.5 us -> 0.44 us
    pallas_call x3 -> x4, Pallas kernels: 9.18 us -> 7.09 us  [the longest x1 3.33 us: per_device(): call(second_kernel, near(64, 1, 3 * LANES), [VMEM] * 4, [pltpu.VMEM((4 *...]
    ppermute x1, waiting for transfers between devices: 1.5 us -> 0.44 us  [per_device(): other = lax.ppermute(own, 'fy', [(i, i ^ 1) for i in range(8)])]
  transfers between devices with their start and end apart: 1 -> 1, of which waited for: 1 -> 1; matrix products, arithmetic and copies ran while one was open for 0% -> 0% of each run, Pallas kernels for 0% -> 1%
where the time goes in v6:
time: 94.1 us; the launch traced here: 93.8 us
  blocking collectives  83.5 us (89%)
  Pallas kernels  7.87 us (8%)
  starting transfers between devices  1.91 us (2%)
    all_to_all x1, blocking collectives, per_device(): lax.all_to_all(packed.reshape(64, 8, LANES), axes, 0, 0, axis_index_group...  39.6 us
    all_to_all x1, blocking collectives, per_device(): lax.all_to_all(updated, axes, 0, 0, axis_index_groups=groups, tiled=True)  22 us
    all_to_all x1, blocking collectives, per_device(): lax.all_to_all(send.reshape(FACES, SLOT, LANES), 'face', 0, 0, tiled=True)  21.9 us
    pallas_call x1, Pallas kernels, per_device(): call(second_kernel, near(64, 1, 3 * LANES), [VMEM] * 4, [pltpu.VMEM((4 *...  3.33 us
    ppermute x1, starting transfers between devices, per_device(): other = lax.ppermute(own, 'fy', [(i, i ^ 1) for i in range(8)])  1.91 us
  transfers between devices with their start and end apart: 1, of which 1 were waited for; matrix products, arithmetic and copies ran while one was open for 0% of the time, Pallas kernels for 1%

profile of v6, /device:TPU:2, one launch (start us, length us, event | category | flops | bytes accessed | tf_op | source)
XLA Modules:
  0.0 93.8 jit_solution(2077290234018626286)
XLA Ops:
  0.0 1.1 %pack.1 = f32[512,128]{1,0:T(8,128)S(1)} custom-call(f32[128,192]{1,0:T(8,128)} %bitcast.26, f32[8,16]{1,0:T(8,128)} %bitcast.28, f32[2,8,16]{2,1,0:T(8,128)} %bitcast.27, f32[8,16]{1,0:T(8,128)} %bitcast.29, f32[8,16]{1,0:T(8,128)} %bitcast.30), custom_call_target="tpu_custom_call" | custom-call | tf_op jit(solution)/shard_map/pack/pallas_call | solution.py:613
  1.1 39.6 %all_to_all.15 = f32[64,8,128]{2,1,0:T(8,128)S(1)} all-to-all(f32[64,8,128]{2,1,0:T(8,128)S(1)} %bitcast.22), channel_id=1, replica_groups={{0,1,2,3,4,5,6,7,8,9,10,11,12,13,14,15,32,33,34,35,36,37,38,39,40,41,42..., dimensions={0} | all-to-all | bytes 524288 | tf_op jit(solution)/shard_map/all_to_all | solution.py:620
  40.7 1.9 %collective-permute-start = (f32[64,8,128]{2,1,0:T(8,128)S(1)}, f32[64,8,128]{2,1,0:T(8,128)S(1)}, u32[]{:S(2)}, u32[]{:S(2)}) collective-permute-start(f32[64,8,128]{2,1,0:T(8,128)S(1)} %all_to_all.15), channel_id=1, source_target_pairs={{0,16},{16,0},{32,48},{48,32},{64,80},{80,64},{96,112},{112,96},{1... | collective-permute-start | bytes 786440 | tf_op jit(solution)/shard_map/ppermute | solution.py:623
  42.7 1.1 %keep.1.table_ref = bf16[1024,256]{1,0:T(8,128)(2,1)S(1)} custom-call(f32[512,128]{1,0:T(8,128)S(1)} %bitcast.20, bf16[1024,256]{1,0:T(8,128)(2,1)} %constant.4.clone.table_ref), custom_call_target="tpu_custom_call" | custom-call | tf_op jit(solution)/shard_map/keep/pallas_call | solution.py:624
  43.7 0.4 collective-permute-done
  44.2 1.6 %first.1 = (f32[896,128]{1,0:T(8,128)S(1)}, f32[336,128]{1,0:T(8,128)S(1)}, s32[8,128]{1,0:T(8,128)S(1)}, bf16[1824,256]{1,0:T(8,128)(2,1)S(1)}) custom-call(s32[4,6]{1,0:T(4,128)} %bitcast.31, f32[512,128]{1,0:T(8,128)S(1)} %bitcast.21, f32[512,128]{1,0:T(8,128)S(1)} %bitcast.24, bf16[1024,256]{1,0:T(8,128)(2,1)S(1)} %keep.1.table_ref, ...), custom_call_target="tpu_custom_call" | custom-call | tf_op jit(solution)/shard_map/first/pallas_call | solution.py:631
  45.7 21.9 %all_to_all.16 = f32[6,56,128]{2,1,0:T(8,128)S(1)} all-to-all(f32[6,56,128]{2,1,0:T(8,128)S(1)} %bitcast.25), channel_id=1, replica_groups=mesh['face'=6,'fy'=8,'fx'=16] {'face'}, dimensions={0} | all-to-all | bytes 344064 | tf_op jit(solution)/shard_map/all_to_all | solution.py:653
  67.6 3.3 %second.1 = f32[64,1,384]{2,1,0:T(1,128)S(1)} custom-call(s32[8,128]{1,0:T(8,128)S(1)} %get-tuple-element.9.which_ref, f32[336,128]{1,0:T(8,128)S(1)} %bitcast.23, f32[896,128]{1,0:T(8,128)S(1)} %get-tuple-element.11.fields_ref, bf16[1824,256]{1,0:T(8,128)(2,1)S(1)} %get-tuple-element.12.table_ref), custom_call_target="tpu_custom_call" | custom-call | tf_op jit(solution)/shard_map/second/pallas_call | solution.py:654
  71.0 22.0 %all_to_all.17.got_ref = f32[64,1,384]{2,1,0:T(1,128)S(1)} all-to-all(f32[64,1,384]{2,1,0:T(1,128)S(1)} %second.1), channel_id=1, replica_groups={{0,1,2,3,4,5,6,7,8,9,10,11,12,13,14,15,32,33,34,35,36,37,38,39,40,41,42..., dimensions={0} | all-to-all | bytes 196608 | tf_op jit(solution)/shard_map/all_to_all | solution.py:661
  93.0 0.8 unpack.1
Async XLA Ops:
  40.7 3.4 %collective-permute-start = (f32[64,8,128]{2,1,0:T(8,128)S(1)}, f32[64,8,128]{2,1,0:T(8,128)S(1)}, u32[]{:S(2)}, u32[]{:S(2)}) collective-permute-start(f32[64,8,128]{2,1,0:T(8,128)S(1)} %all_to_all.15), channel_id=1, source_target_pairs={{0,16},{16,0},{32,48},{48,32},{64,80},{80,64},{96,112},{112,96},{1... | collective-permute-start | bytes 786440 | tf_op jit(solution)/shard_map/ppermute | solution.py:623

commit v7 on v6

--- a/solution.py
+++ b/solution.py
@@ -211,10 +211,11 @@
     return high, mid, (rest - mid.astype(jnp.float32)).astype(jnp.bfloat16)
 
 
-def gradient(values, table):
+def gradient(values, table, parts=3):
     high, mid, low = split(values)
-    parts = [table.part("gradient", n, LANES) for n in (0, 0, 1, 1, 0, 2)]
-    both = dot_halves(stacked([high, mid, high, mid, low, high], 1), stacked(parts))
+    left = [high, mid, high, mid, low, high][: 2 * parts]
+    right = [table.part("gradient", n, LANES) for n in (0, 0, 1, 1, 0, 2)[: 2 * parts]]
+    both = dot_halves(stacked(left, 1), stacked(right))
     return both[:, :LANES], both[:, LANES:]
 
 
@@ -299,43 +300,33 @@
     return [-sense * given[1], sense * given[0], *given[2:]]
 
 
-def join(face_ref, ring, channels, table, ring_too=True):
-    ends = ends_meet(ring, channels, table) if ring_too else None
+def placed_ends(ends):
+    block, fy = iota((16, LANES), 0), iota((8, LANES), 0)
+    parts = []
+    for side, position, count in ((0, block, 16), (1, block, 16), (2, fy, 8), (3, fy, 8)):
+        first, last = ends[2 * side : 2 * side + 1], ends[2 * side + 1 : 2 * side + 2]
+        parts.append(
+            jnp.where(position == 0, first, jnp.where(position == count - 1, last, 0.0))
+        )
+    return stacked(parts)
+
+
+def join(face_ref, ring, channels, ends=None):
     totals = []
+    lane = iota((16, LANES), 1)
+    lane_8 = iota((8, LANES), 1)
     for ch in range(channels):
         south, north = ring[ch][0:16], ring[ch][16:32]
         east, west = ring[ch][32:40], ring[ch][40:48]
         rows = [rim_rows(edge, ROWS * ch) for edge in range(EDGES)]
-        lane = iota((16, LANES), 1)
-        lane_8 = iota((8, LANES), 1)
-        if ring_too:
-            block = iota((16, LANES), 0)
-            fy = iota((8, LANES), 0)
-            of_end = [ends[ch][t : t + 1] for t in range(8)]
-
-            def at_ends(first, last, position, count):
-                return jnp.where(
-                    position == 0, first, jnp.where(position == count - 1, last, 0.0)
-                )
-
-            totals.append(
-                stacked(
-                    [
-                        south
-                        + jnp.where(lane // 8 == 15, roll(face_ref[rows[0], :], -8, 1), 0.0)
-                        + at_ends(of_end[0], of_end[1], block, 16),
-                        north
-                        + jnp.where(lane // 8 == 0, roll(face_ref[rows[2], :], 8, 1), 0.0)
-                        + at_ends(of_end[2], of_end[3], block, 16),
-                        east
-                        + jnp.where(lane_8 % 8 == 0, roll(face_ref[rows[1], :], -7, 1), 0.0)
-                        + at_ends(of_end[4], of_end[5], fy, 8),
-                        west
-                        + jnp.where(lane_8 % 8 == 7, roll(face_ref[rows[3], :], 7, 1), 0.0)
-                        + at_ends(of_end[6], of_end[7], fy, 8),
-                    ]
-                )
-            )
+        if ends is not None:
+            rims = [
+                jnp.where(lane // 8 == 15, roll(face_ref[rows[0], :], -8, 1), 0.0),
+                jnp.where(lane // 8 == 0, roll(face_ref[rows[2], :], 8, 1), 0.0),
+                jnp.where(lane_8 % 8 == 0, roll(face_ref[rows[1], :], -7, 1), 0.0),
+                jnp.where(lane_8 % 8 == 7, roll(face_ref[rows[3], :], 7, 1), 0.0),
+            ]
+            totals.append(ring[ch] + ends[ch] + stacked(rims))
         from_south = jnp.where(lane // 8 == 0, roll(south, 8, 1), 0.0)
         from_north = jnp.where(lane // 8 == 15, roll(north, -8, 1), 0.0)
         from_east = jnp.where(lane_8 % 8 == 7, roll(east, 7, 1), 0.0)
@@ -416,8 +407,12 @@
 
 
 def ring_of(which_ref, got_ref, table):
-    near = iota((16, LANES), 1) < 64
-    strips = []
+    lane = iota((16, LANES), 1)
+    block = iota((16, LANES), 0)
+    near = lane < 64
+    first = (block == 0) & (lane % 8 == 0) & (lane >= 8)
+    last = (block == 15) & (lane % 8 == 7) & (lane >= 8)
+    got, strips, seams = [], [], []
     for edge in range(EDGES):
         slot = got_ref[:SLOT, :]
         which = jnp.broadcast_to(which_ref[edge : edge + 1, :], (SLOT, LANES))
@@ -430,7 +425,22 @@
         rows = slot[48:56]
         fields.append(stacked([rows, roll(rows, 64, 1)]))
         fields[6] = jnp.where(near, fields[6], 0.0)
-        rows = stacked([*fields, jnp.zeros_like(near, jnp.float32)])
+        got.append(fields)
+    for edge in range(EDGES):
+        fields = list(got[edge])
+        corner = jnp.zeros((16, LANES), jnp.float32)
+        for ch in range(4):
+            after, before = got[(edge + 1) % EDGES][ch], got[(edge - 1) % EDGES][ch]
+            at_first = (block == 0) & (lane == 8 * ch)
+            at_last = (block == 15) & (lane == 8 * ch + 7)
+            corner = jnp.where(at_first, roll(after[15:16], 8 * ch - 7, 1), corner)
+            corner = jnp.where(at_last, roll(before[0:1], 8 * ch + 7, 1), corner)
+            fields[ch] = (
+                fields[ch]
+                + jnp.where(first, roll(after[15:16], -7, 1), 0.0)
+                + jnp.where(last, roll(before[0:1], 7, 1), 0.0)
+            )
+        rows = stacked([*fields, corner])
         count = 16
         if edge == 0:
             rows = reversed_blocks(rows, table)
@@ -443,6 +453,13 @@
             rows = dot(moved.astype(jnp.bfloat16), stacked(into))
             count = 8
         fields = [rows[count * k : count * k + count] for k in range(7)]
+        corner = rows[7 * count : 8 * count]
+        low, high = ((120, 127), (0, 120), (0, 7), (7, 127))[edge]
+        position, at = iota((count, LANES), 0), iota((count, LANES), 1)
+        here = ((position == 0) & (at == low)) | ((position == count - 1) & (at == high))
+        step = (8, -1, -8, 1)[edge]
+        seam = [jnp.where(here, roll(corner, step * ch, 1), 0.0) for ch in range(4)]
+        seams.append([*turned(seam[0], seam[1], edge + 2), *seam[2:]])
         fields[0], fields[1] = turned(fields[0], fields[1], edge + 2)
         if edge % 2:
             fields[4], fields[5], fields[6] = fields[6], -fields[5], fields[4]
@@ -450,7 +467,9 @@
             far = near if edge == 0 else ~near
             fields[3] = jnp.where(far, 1.0, fields[3])
         strips.append(fields)
-    return [stacked([strips[edge][k] for edge in (0, 2, 1, 3)]) for k in range(7)]
+    order = (0, 2, 1, 3)
+    ring = [stacked([strips[edge][k] for edge in order]) for k in range(7)]
+    return ring, [stacked([seams[edge][ch] for edge in order]) for ch in range(4)]
 
 
 def first_kernel(
@@ -501,10 +520,10 @@
     keep.wait()
 
 
-def laplace(fields, metric, table):
+def laplace(fields, metric, table, parts):
     flux_xx, flux_xy, flux_yy = metric
     count = flux_xx.shape[0]
-    grad_x, grad_y = gradient(stacked(fields), table)
+    grad_x, grad_y = gradient(stacked(fields), table, parts)
     flux = []
     for ch in range(3):
         part = slice(count * ch, count * ch + count)
@@ -518,8 +537,9 @@
             )
         )
     high, mid, low = split(stacked(flux))
-    parts = [table.part("spread", n, 2 * LANES) for n in (0, 0, 0, 1, 1, 2)]
-    sums = dot_halves(stacked([high, mid, low, high, mid, high], 1), stacked(parts))
+    terms = [(high, 0), (mid, 0), (high, 1), (low, 0), (mid, 1), (high, 2)][: 3 * parts - 3]
+    right = [table.part("spread", n, 2 * LANES) for _, n in terms]
+    sums = dot_halves(stacked([part for part, _ in terms], 1), stacked(right))
     return [
         assembled(sums[count * ch : count * ch + count, :LANES], sums[count * ch : count * ch + count, LANES:])
         for ch in range(3)
@@ -529,36 +549,37 @@
 def second_kernel(which_ref, got_ref, fields_ref, table_ref, out_ref, total_ref):
     table = Table(table_ref, 1)
     core = lax.axis_index("fy") % 2
-    ring_fields = ring_of(which_ref, got_ref, table)
+    ring_fields, seams = ring_of(which_ref, got_ref, table)
     metric = [
         stacked([fields_ref[ROWS * k : ROWS * k + ROWS, :], ring_fields[k]]) for k in range(4, 7)
     ]
     total_ref[...] = fields_ref[: 4 * ROWS, :]
-    ring = join(total_ref, ring_fields[:4], 4, table)
+    ring = join(total_ref, ring_fields[:4], 4, seams)
     share = 1.0 / stacked([total_ref[3 * ROWS : 4 * ROWS, :], ring[3]])
     fields = [
         stacked([total_ref[ROWS * ch : ROWS * ch + ROWS, :], ring[ch]]) * share for ch in range(3)
     ]
     sectioned = [field[:ROWS] for field in fields]
     for step in range(2):
-        sums = laplace(fields, metric, table)
+        sums = laplace(fields, metric, table, 3 - step)
         for ch in range(3):
             total_ref[ROWS * ch : ROWS * ch + ROWS, :] = sums[ch][:ROWS]
-        ring = join(total_ref, [field[ROWS:] for field in sums], 3, table, step == 0)
+        ring = [field[ROWS:] for field in sums]
+        ends = [placed_ends(part) for part in ends_meet(ring, 3, table)] if step == 0 else None
+        ring = join(total_ref, ring, 3, ends)
         if step == 0:
             fields = [
                 stacked([total_ref[ROWS * ch : ROWS * ch + ROWS, :], ring[ch]]) * share
                 for ch in range(3)
             ]
     for ch in range(3):
-        part = slice(ROWS * ch, ROWS * ch + ROWS)
-        total_ref[part, :] = sectioned[ch] - hyper_coeff * (total_ref[part, :] * share[:ROWS])
-    for x in range(4):
-        for ch in range(3):
-            start = pl.multiple_of(ROWS * ch + 32 * x + 16 * core, 16)
-            out_ref[16 * x : 16 * x + 16, 0, LANES * ch : LANES * ch + LANES] = total_ref[
-                pl.ds(start, 16), :
-            ]
+        second_lap = total_ref[ROWS * ch : ROWS * ch + ROWS, :] * share[:ROWS]
+        updated = sectioned[ch] - hyper_coeff * second_lap
+        for x in range(4):
+            even, odd = updated[32 * x : 32 * x + 16], updated[32 * x + 16 : 32 * x + 32]
+            out_ref[16 * x : 16 * x + 16, 0, LANES * ch : LANES * ch + LANES] = jnp.where(
+                core == 0, even, odd
+            )
 
 
 def unpack_kernel(got_ref, out_ref):

time: 94.1 us -> 93.7 us (level)
  no operation moved by 1% of the time
where the time goes in v7:
time: 93.7 us; the launch traced here: 93.4 us
  blocking collectives  83.5 us (89%)
  Pallas kernels  7.47 us (8%)
  starting transfers between devices  1.91 us (2%)
    all_to_all x1, blocking collectives, per_device(): lax.all_to_all(packed.reshape(64, 8, LANES), axes, 0, 0, axis_index_group...  39.6 us
    all_to_all x1, blocking collectives, per_device(): lax.all_to_all(updated, axes, 0, 0, axis_index_groups=groups, tiled=True)  22 us
    all_to_all x1, blocking collectives, per_device(): lax.all_to_all(send.reshape(FACES, SLOT, LANES), 'face', 0, 0, tiled=True)  21.9 us
    pallas_call x1, Pallas kernels, per_device(): call(second_kernel, near(64, 1, 3 * LANES), [VMEM] * 4, [pltpu.VMEM((4 *...  2.93 us
    ppermute x1, starting transfers between devices, per_device(): other = lax.ppermute(own, 'fy', [(i, i ^ 1) for i in range(8)])  1.91 us
  transfers between devices with their start and end apart: 1, of which 1 were waited for; matrix products, arithmetic and copies ran while one was open for 0% of the time, Pallas kernels for 1%

profile of v7, /device:TPU:2, one launch (start us, length us, event | category | flops | bytes accessed | tf_op | source)
XLA Modules:
  0.0 93.4 jit_solution(1135754479737887124)
XLA Ops:
  0.0 1.1 %pack.1 = f32[512,128]{1,0:T(8,128)S(1)} custom-call(f32[128,192]{1,0:T(8,128)} %bitcast.26, f32[8,16]{1,0:T(8,128)} %bitcast.28, f32[2,8,16]{2,1,0:T(8,128)} %bitcast.27, f32[8,16]{1,0:T(8,128)} %bitcast.29, f32[8,16]{1,0:T(8,128)} %bitcast.30), custom_call_target="tpu_custom_call" | custom-call | tf_op jit(solution)/shard_map/pack/pallas_call | solution.py:634
  1.1 39.6 %all_to_all.15 = f32[64,8,128]{2,1,0:T(8,128)S(1)} all-to-all(f32[64,8,128]{2,1,0:T(8,128)S(1)} %bitcast.22), channel_id=1, replica_groups={{0,1,2,3,4,5,6,7,8,9,10,11,12,13,14,15,32,33,34,35,36,37,38,39,40,41,42..., dimensions={0} | all-to-all | bytes 524288 | tf_op jit(solution)/shard_map/all_to_all | solution.py:641
  40.7 1.9 %collective-permute-start = (f32[64,8,128]{2,1,0:T(8,128)S(1)}, f32[64,8,128]{2,1,0:T(8,128)S(1)}, u32[]{:S(2)}, u32[]{:S(2)}) collective-permute-start(f32[64,8,128]{2,1,0:T(8,128)S(1)} %all_to_all.15), channel_id=1, source_target_pairs={{0,16},{16,0},{32,48},{48,32},{64,80},{80,64},{96,112},{112,96},{1... | collective-permute-start | bytes 786440 | tf_op jit(solution)/shard_map/ppermute | solution.py:644
  42.7 1.1 %keep.1.table_ref = bf16[1024,256]{1,0:T(8,128)(2,1)S(1)} custom-call(f32[512,128]{1,0:T(8,128)S(1)} %bitcast.20, bf16[1024,256]{1,0:T(8,128)(2,1)} %constant.4.clone.table_ref), custom_call_target="tpu_custom_call" | custom-call | tf_op jit(solution)/shard_map/keep/pallas_call | solution.py:645
  43.7 0.4 collective-permute-done
  44.2 1.6 %first.1 = (f32[896,128]{1,0:T(8,128)S(1)}, f32[336,128]{1,0:T(8,128)S(1)}, s32[8,128]{1,0:T(8,128)S(1)}, bf16[1824,256]{1,0:T(8,128)(2,1)S(1)}) custom-call(s32[4,6]{1,0:T(4,128)} %bitcast.31, f32[512,128]{1,0:T(8,128)S(1)} %bitcast.21, f32[512,128]{1,0:T(8,128)S(1)} %bitcast.24, bf16[1024,256]{1,0:T(8,128)(2,1)S(1)} %keep.1.table_ref, ...), custom_call_target="tpu_custom_call" | custom-call | tf_op jit(solution)/shard_map/first/pallas_call | solution.py:652
  45.7 21.9 %all_to_all.16 = f32[6,56,128]{2,1,0:T(8,128)S(1)} all-to-all(f32[6,56,128]{2,1,0:T(8,128)S(1)} %bitcast.25), channel_id=1, replica_groups=mesh['face'=6,'fy'=8,'fx'=16] {'face'}, dimensions={0} | all-to-all | bytes 344064 | tf_op jit(solution)/shard_map/all_to_all | solution.py:674
  67.6 2.9 %second.1 = f32[64,1,384]{2,1,0:T(1,128)S(1)} custom-call(s32[8,128]{1,0:T(8,128)S(1)} %get-tuple-element.9.which_ref, f32[336,128]{1,0:T(8,128)S(1)} %bitcast.23, f32[896,128]{1,0:T(8,128)S(1)} %get-tuple-element.11.fields_ref, bf16[1824,256]{1,0:T(8,128)(2,1)S(1)} %get-tuple-element.12.table_ref), custom_call_target="tpu_custom_call" | custom-call | tf_op jit(solution)/shard_map/second/pallas_call | solution.py:675
  70.6 22.0 %all_to_all.17.got_ref = f32[64,1,384]{2,1,0:T(1,128)S(1)} all-to-all(f32[64,1,384]{2,1,0:T(1,128)S(1)} %second.1), channel_id=1, replica_groups={{0,1,2,3,4,5,6,7,8,9,10,11,12,13,14,15,32,33,34,35,36,37,38,39,40,41,42..., dimensions={0} | all-to-all | bytes 196608 | tf_op jit(solution)/shard_map/all_to_all | solution.py:682
  92.6 0.8 unpack.1
Async XLA Ops:
  40.7 3.4 %collective-permute-start = (f32[64,8,128]{2,1,0:T(8,128)S(1)}, f32[64,8,128]{2,1,0:T(8,128)S(1)}, u32[]{:S(2)}, u32[]{:S(2)}) collective-permute-start(f32[64,8,128]{2,1,0:T(8,128)S(1)} %all_to_all.15), channel_id=1, source_target_pairs={{0,16},{16,0},{32,48},{48,32},{64,80},{80,64},{96,112},{112,96},{1... | collective-permute-start | bytes 786440 | tf_op jit(solution)/shard_map/ppermute | solution.py:644

commit v8 on v7

--- a/solution.py
+++ b/solution.py
@@ -354,11 +354,36 @@
         out_ref[pl.ds(3 + k, 64, 8), :] = jnp.broadcast_to(line, (64, LANES))
 
 
-def keep_kernel(after_ref, table_ref, kept_ref, sem):
-    del after_ref
-    keep = pltpu.make_async_copy(table_ref, kept_ref, sem)
-    keep.start()
-    keep.wait()
+def weighted_raw(blocks_ref, table):
+    u, v, t, volume, m_xx, m_yy, m_xy, planet = [
+        blocks_ref[pl.ds(k, 64, 8), :] for k in range(8)
+    ]
+    contra_u = m_xx * u + m_xy * v
+    contra_v = m_xy * u + m_yy * v
+    energy = 0.5 * (u * contra_u + v * contra_v) + t
+    grad_x, grad_y = gradient(stacked([u, v, t, energy]), table)
+    dy_u, dx_v = grad_y[:64], grad_x[64:128]
+    dx_t, dy_t = grad_x[128:192], grad_y[128:192]
+    dx_e, dy_e = grad_x[192:], grad_y[192:]
+    absolute = dx_v - dy_u + planet * volume
+    mass = mass_weight() * volume
+    raw_u = u + time_step * (absolute * contra_v - dx_e)
+    raw_v = v + time_step * (-absolute * contra_u - dy_e)
+    raw_t = t - time_step * (contra_u * dx_t + contra_v * dy_t)
+    metric = [volume * m_xx, volume * m_xy, volume * m_yy]
+    return [mass * raw_u, mass * raw_v, mass * raw_t, mass, *metric]
+
+
+def early_kernel(own_ref, table_from, table_ref, half_ref, sem, late_sem):
+    rows = PLACES[0]["gradient"][1]
+    soon = pltpu.make_async_copy(table_from.at[:rows], table_ref.at[:rows], sem)
+    late = pltpu.make_async_copy(table_from.at[rows:], table_ref.at[rows:], late_sem)
+    soon.start()
+    late.start()
+    soon.wait()
+    for k, field in enumerate(weighted_raw(own_ref, Table(table_ref, 0))):
+        half_ref[64 * k : 64 * k + 64, :] = field
+    late.wait()
 
 
 def reversed_blocks(rows, table):
@@ -473,7 +498,7 @@
 
 
 def first_kernel(
-    nbr_from, own_ref, other_ref, table_ref, later_ref,
+    nbr_from, half_ref, other_ref, table_ref, later_ref,
     fields_ref, send_ref, which_ref, kept_ref, nbr_ref, nbr_sem, sem,
 ):
     fetch = pltpu.make_async_copy(nbr_from, nbr_ref, nbr_sem)
@@ -484,35 +509,21 @@
     core = lax.axis_index("fy") % 2
     face = lax.axis_index("face")
     fields = []
-    for k in range(8):
-        own = own_ref[pl.ds(k, 64, 8), :]
-        other = other_ref[pl.ds(k, 64, 8), :]
+    for k, other in enumerate(weighted_raw(other_ref, table)):
+        own = half_ref[64 * k : 64 * k + 64, :]
         even = jnp.where(core == 0, own, other)
         odd = jnp.where(core == 0, other, own)
         pieces = []
         for x in range(4):
             pieces += [even[16 * x : 16 * x + 16], odd[16 * x : 16 * x + 16]]
         fields.append(stacked(pieces))
-    u, v, t, volume, m_xx, m_yy, m_xy, planet = fields
-    contra_u = m_xx * u + m_xy * v
-    contra_v = m_xy * u + m_yy * v
-    energy = 0.5 * (u * contra_u + v * contra_v) + t
-    grad_x, grad_y = gradient(stacked([u, v, t, energy]), table)
-    dy_u, dx_v = grad_y[:ROWS], grad_x[ROWS : 2 * ROWS]
-    dx_t, dy_t = grad_x[2 * ROWS : 3 * ROWS], grad_y[2 * ROWS : 3 * ROWS]
-    dx_e, dy_e = grad_x[3 * ROWS :], grad_y[3 * ROWS :]
-    absolute = dx_v - dy_u + planet * volume
-    mass = mass_weight() * volume
-    raw_u = u + time_step * (absolute * contra_v - dx_e)
-    raw_v = v + time_step * (-absolute * contra_u - dy_e)
-    raw_t = t - time_step * (contra_u * dx_t + contra_v * dy_t)
-    values = stacked([mass * raw_u, mass * raw_v, mass * raw_t, mass])
+    values = stacked(fields[:4])
     sums = dot_halves(stacked(split(values), 1), stacked([table.whole("both")] * 3))
     for ch in range(4):
         part = slice(ROWS * ch, ROWS * ch + ROWS)
         fields_ref[part, :] = assembled(sums[part, :LANES], sums[part, LANES:])
-    for k, field in enumerate([m_xx, m_xy, m_yy]):
-        fields_ref[ROWS * (4 + k) : ROWS * (5 + k), :] = volume * field
+    for k in range(4, 7):
+        fields_ref[ROWS * k : ROWS * k + ROWS, :] = fields[k]
     fetch.wait()
     for edge in range(8):
         which_ref[edge : edge + 1, :] = jnp.full((1, LANES), nbr_ref[edge % EDGES, face], jnp.int32)
@@ -642,12 +653,12 @@
         packed.reshape(64, 8, LANES), axes, 0, 0, axis_index_groups=groups, tiled=True
     )
     other = lax.ppermute(own, "fy", [(i, i ^ 1) for i in range(8)])
-    table = call(
-        keep_kernel,
-        kept(TABLES[0]),
+    table, half = call(
+        early_kernel,
+        [kept(TABLES[0]), near(7 * 64, LANES)],
         [VMEM, ANY],
-        [pltpu.SemaphoreType.DMA],
-        name="keep",
+        [pltpu.SemaphoreType.DMA, pltpu.SemaphoreType.DMA],
+        name="early",
     )(held(own.reshape(512, LANES)), tables[0])
     fields, send, which, table = call(
         first_kernel,
@@ -666,7 +677,7 @@
         name="first",
     )(
         nbr_face.T,
-        held(own.reshape(512, LANES)),
+        held(half),
         held(other.reshape(512, LANES)),
         held(table),
         tables[1],

time: 93.7 us -> 93.4 us (level)
  no operation moved by 1% of the time
where the time goes in v8:
time: 93.4 us; the launch traced here: 93.1 us
  blocking collectives  83.6 us (90%)
  Pallas kernels  7.31 us (8%)
  starting transfers between devices  1.91 us (2%)
    all_to_all x1, blocking collectives, per_device(): lax.all_to_all(packed.reshape(64, 8, LANES), axes, 0, 0, axis_index_group...  39.6 us
    all_to_all x1, blocking collectives, per_device(): lax.all_to_all(send.reshape(FACES, SLOT, LANES), 'face', 0, 0, tiled=True)  22 us
    all_to_all x1, blocking collectives, per_device(): lax.all_to_all(updated, axes, 0, 0, axis_index_groups=groups, tiled=True)  22 us
    pallas_call x1, Pallas kernels, per_device(): call(second_kernel, near(64, 1, 3 * LANES), [VMEM] * 4, [pltpu.VMEM((4 *...  2.93 us
    ppermute x1, starting transfers between devices, per_device(): other = lax.ppermute(own, 'fy', [(i, i ^ 1) for i in range(8)])  1.91 us
  transfers between devices with their start and end apart: 1, of which 1 were waited for; matrix products, arithmetic and copies ran while one was open for 0% of the time, Pallas kernels for 1%

profile of v8, /device:TPU:2, one launch (start us, length us, event | category | flops | bytes accessed | tf_op | source)
XLA Modules:
  0.0 93.1 jit_solution(12402789388152229951)
XLA Ops:
  0.0 1.1 %pack.1 = f32[512,128]{1,0:T(8,128)S(1)} custom-call(f32[128,192]{1,0:T(8,128)} %bitcast.25, f32[8,16]{1,0:T(8,128)} %bitcast.27, f32[2,8,16]{2,1,0:T(8,128)} %bitcast.26, f32[8,16]{1,0:T(8,128)} %bitcast.28, f32[8,16]{1,0:T(8,128)} %bitcast.29), custom_call_target="tpu_custom_call" | custom-call | tf_op jit(solution)/shard_map/pack/pallas_call | solution.py:645
  1.1 39.6 %all_to_all.15 = f32[64,8,128]{2,1,0:T(8,128)S(1)} all-to-all(f32[64,8,128]{2,1,0:T(8,128)S(1)} %bitcast.21), channel_id=1, replica_groups={{0,1,2,3,4,5,6,7,8,9,10,11,12,13,14,15,32,33,34,35,36,37,38,39,40,41,42..., dimensions={0} | all-to-all | bytes 524288 | tf_op jit(solution)/shard_map/all_to_all | solution.py:652
  40.7 1.9 %collective-permute-start = (f32[64,8,128]{2,1,0:T(8,128)S(1)}, f32[64,8,128]{2,1,0:T(8,128)S(1)}, u32[]{:S(2)}, u32[]{:S(2)}) collective-permute-start(f32[64,8,128]{2,1,0:T(8,128)S(1)} %all_to_all.15), channel_id=1, source_target_pairs={{0,16},{16,0},{32,48},{48,32},{64,80},{80,64},{96,112},{112,96},{1... | collective-permute-start | bytes 786440 | tf_op jit(solution)/shard_map/ppermute | solution.py:655
  42.7 1.2 %early.1 = (bf16[1024,256]{1,0:T(8,128)(2,1)S(1)}, f32[448,128]{1,0:T(8,128)S(1)}) custom-call(f32[512,128]{1,0:T(8,128)S(1)} %bitcast.20, bf16[1024,256]{1,0:T(8,128)(2,1)} %constant.4.clone.table_from), custom_call_target="tpu_custom_call" | custom-call | tf_op jit(solution)/shard_map/early/pallas_call | solution.py:656
  43.9 0.3 collective-permute-done
  44.2 1.2 %first.1 = (f32[896,128]{1,0:T(8,128)S(1)}, f32[336,128]{1,0:T(8,128)S(1)}, s32[8,128]{1,0:T(8,128)S(1)}, bf16[1824,256]{1,0:T(8,128)(2,1)S(1)}) custom-call(s32[4,6]{1,0:T(4,128)} %bitcast.30, f32[448,128]{1,0:T(8,128)S(1)} %get-tuple-element.11.half_ref, f32[512,128]{1,0:T(8,128)S(1)} %bitcast.23, bf16[1024,256]{1,0:T(8,128)(2,1)S(1)} %get-tuple-element.12.table_ref, ...), custom_call_target="tpu_custom_call" | custom-call | tf_op jit(solution)/shard_map/first/pallas_call | solution.py:663
  45.4 22.0 %all_to_all.16 = f32[6,56,128]{2,1,0:T(8,128)S(1)} all-to-all(f32[6,56,128]{2,1,0:T(8,128)S(1)} %bitcast.24), channel_id=1, replica_groups=mesh['face'=6,'fy'=8,'fx'=16] {'face'}, dimensions={0} | all-to-all | bytes 344064 | tf_op jit(solution)/shard_map/all_to_all | solution.py:685
  67.4 2.9 %second.1 = f32[64,1,384]{2,1,0:T(1,128)S(1)} custom-call(s32[8,128]{1,0:T(8,128)S(1)} %get-tuple-element.13.which_ref, f32[336,128]{1,0:T(8,128)S(1)} %bitcast.22, f32[896,128]{1,0:T(8,128)S(1)} %get-tuple-element.15.fields_ref, bf16[1824,256]{1,0:T(8,128)(2,1)S(1)} %get-tuple-element.16.table_ref), custom_call_target="tpu_custom_call" | custom-call | tf_op jit(solution)/shard_map/second/pallas_call | solution.py:686
  70.3 22.0 %all_to_all.17.got_ref = f32[64,1,384]{2,1,0:T(1,128)S(1)} all-to-all(f32[64,1,384]{2,1,0:T(1,128)S(1)} %second.1), channel_id=1, replica_groups={{0,1,2,3,4,5,6,7,8,9,10,11,12,13,14,15,32,33,34,35,36,37,38,39,40,41,42..., dimensions={0} | all-to-all | bytes 196608 | tf_op jit(solution)/shard_map/all_to_all | solution.py:693
  92.4 0.8 unpack.1
Async XLA Ops:
  40.7 3.4 %collective-permute-start = (f32[64,8,128]{2,1,0:T(8,128)S(1)}, f32[64,8,128]{2,1,0:T(8,128)S(1)}, u32[]{:S(2)}, u32[]{:S(2)}) collective-permute-start(f32[64,8,128]{2,1,0:T(8,128)S(1)} %all_to_all.15), channel_id=1, source_target_pairs={{0,16},{16,0},{32,48},{48,32},{64,80},{80,64},{96,112},{112,96},{1... | collective-permute-start | bytes 786440 | tf_op jit(solution)/shard_map/ppermute | solution.py:655

commit v9 on v8

--- a/solution.py
+++ b/solution.py
@@ -14,11 +14,11 @@
 ROWS = 128
 LANES = 128
 EDGES = 4
-RING_ROWS = 48
+RING_ROWS = 32
 ALL_ROWS = ROWS + RING_ROWS
 SLOT = 56
 ENDS = ("S0", "S15", "N0", "N15", "E0", "E7", "W0", "W7")
-END_ROWS = (0, 15, 16, 31, 32, 39, 40, 47)
+END_ROWS = (0, 15, 0, 15, 16, 23, 24, 31)
 MEETS = (6, 4, 7, 5, 1, 3, 0, 2)
 TURNS = (1, -1, -1, 1, 1, -1, -1, 1)
 
@@ -232,7 +232,7 @@
     lane = iota(shape, 1)
     c = lane % 8
     r = lane // 8
-    here = row < ROWS + 32
+    here = row < ROWS + 16
     from_before = here & (c == 0) & (row % 16 > 0)
     from_after = here & (c == 7) & (row % 16 < 15)
     summed = (
@@ -251,10 +251,10 @@
     above_block = [edge_rows, above[: ROWS - 16]]
     below_block = [below[16:ROWS], edge_rows]
     if shape[0] > ROWS:
-        sides = slice(ROWS + 32, ROWS + 48)
+        sides = slice(ROWS + 16, ROWS + 32)
         fy = iota((16, LANES), 0) % 8
-        above_block += [edge_rows] * 2 + [jnp.where(fy > 0, roll(above[sides], 1, 0), 0.0)]
-        below_block += [edge_rows] * 2 + [jnp.where(fy < 7, roll(below[sides], -1, 0), 0.0)]
+        above_block += [edge_rows, jnp.where(fy > 0, roll(above[sides], 1, 0), 0.0)]
+        below_block += [edge_rows, jnp.where(fy < 7, roll(below[sides], -1, 0), 0.0)]
     return (
         total
         + jnp.where(r == 0, stacked(above_block), 0.0)
@@ -308,7 +308,7 @@
         parts.append(
             jnp.where(position == 0, first, jnp.where(position == count - 1, last, 0.0))
         )
-    return stacked(parts)
+    return stacked([parts[0] + parts[1], parts[2], parts[3]])
 
 
 def join(face_ref, ring, channels, ends=None):
@@ -316,19 +316,21 @@
     lane = iota((16, LANES), 1)
     lane_8 = iota((8, LANES), 1)
     for ch in range(channels):
-        south, north = ring[ch][0:16], ring[ch][16:32]
-        east, west = ring[ch][32:40], ring[ch][40:48]
+        outer, east, west = ring[ch][0:16], ring[ch][16:24], ring[ch][24:32]
         rows = [rim_rows(edge, ROWS * ch) for edge in range(EDGES)]
         if ends is not None:
             rims = [
-                jnp.where(lane // 8 == 15, roll(face_ref[rows[0], :], -8, 1), 0.0),
-                jnp.where(lane // 8 == 0, roll(face_ref[rows[2], :], 8, 1), 0.0),
+                jnp.where(
+                    lane // 8 == 15,
+                    roll(face_ref[rows[0], :], -8, 1),
+                    jnp.where(lane // 8 == 0, roll(face_ref[rows[2], :], 8, 1), 0.0),
+                ),
                 jnp.where(lane_8 % 8 == 0, roll(face_ref[rows[1], :], -7, 1), 0.0),
                 jnp.where(lane_8 % 8 == 7, roll(face_ref[rows[3], :], 7, 1), 0.0),
             ]
             totals.append(ring[ch] + ends[ch] + stacked(rims))
-        from_south = jnp.where(lane // 8 == 0, roll(south, 8, 1), 0.0)
-        from_north = jnp.where(lane // 8 == 15, roll(north, -8, 1), 0.0)
+        from_south = jnp.where(lane // 8 == 0, roll(outer, 8, 1), 0.0)
+        from_north = jnp.where(lane // 8 == 15, roll(outer, -8, 1), 0.0)
         from_east = jnp.where(lane_8 % 8 == 7, roll(east, 7, 1), 0.0)
         from_west = jnp.where(lane_8 % 8 == 0, roll(west, -7, 1), 0.0)
         for edge, part in enumerate((from_south, from_east, from_north, from_west)):
@@ -488,13 +490,12 @@
         fields[0], fields[1] = turned(fields[0], fields[1], edge + 2)
         if edge % 2:
             fields[4], fields[5], fields[6] = fields[6], -fields[5], fields[4]
-        else:
-            far = near if edge == 0 else ~near
-            fields[3] = jnp.where(far, 1.0, fields[3])
         strips.append(fields)
-    order = (0, 2, 1, 3)
-    ring = [stacked([strips[edge][k] for edge in order]) for k in range(7)]
-    return ring, [stacked([seams[edge][ch] for edge in order]) for ch in range(4)]
+    def around(sides, k):
+        south, east, north, west = [side[k] for side in sides]
+        return stacked([south + north, east, west])
+
+    return [around(strips, k) for k in range(7)], [around(seams, ch) for ch in range(4)]
 
 
 def first_kernel(

time: 93.4 us -> 93.3 us (level)
  no operation moved by 1% of the time
where the time goes in v9:
time: 93.3 us; the launch traced here: 93 us
  blocking collectives  83.6 us (90%)
  Pallas kernels  7.19 us (8%)
  starting transfers between devices  1.91 us (2%)
    all_to_all x1, blocking collectives, per_device(): lax.all_to_all(packed.reshape(64, 8, LANES), axes, 0, 0, axis_index_group...  39.6 us
    all_to_all x1, blocking collectives, per_device(): lax.all_to_all(send.reshape(FACES, SLOT, LANES), 'face', 0, 0, tiled=True)  22 us
    all_to_all x1, blocking collectives, per_device(): lax.all_to_all(updated, axes, 0, 0, axis_index_groups=groups, tiled=True)  22 us
    pallas_call x1, Pallas kernels, per_device(): call(second_kernel, near(64, 1, 3 * LANES), [VMEM] * 4, [pltpu.VMEM((4 *...  2.81 us
    ppermute x1, starting transfers between devices, per_device(): other = lax.ppermute(own, 'fy', [(i, i ^ 1) for i in range(8)])  1.91 us
  transfers between devices with their start and end apart: 1, of which 1 were waited for; matrix products, arithmetic and copies ran while one was open for 0% of the time, Pallas kernels for 1%

profile of v9, /device:TPU:2, one launch (start us, length us, event | category | flops | bytes accessed | tf_op | source)
XLA Modules:
  0.0 93.0 jit_solution(7654321783634357079)
XLA Ops:
  0.0 1.1 %pack.1 = f32[512,128]{1,0:T(8,128)S(1)} custom-call(f32[128,192]{1,0:T(8,128)} %bitcast.25, f32[8,16]{1,0:T(8,128)} %bitcast.27, f32[2,8,16]{2,1,0:T(8,128)} %bitcast.26, f32[8,16]{1,0:T(8,128)} %bitcast.28, f32[8,16]{1,0:T(8,128)} %bitcast.29), custom_call_target="tpu_custom_call" | custom-call | tf_op jit(solution)/shard_map/pack/pallas_call | solution.py:646
  1.1 39.6 %all_to_all.15 = f32[64,8,128]{2,1,0:T(8,128)S(1)} all-to-all(f32[64,8,128]{2,1,0:T(8,128)S(1)} %bitcast.21), channel_id=1, replica_groups={{0,1,2,3,4,5,6,7,8,9,10,11,12,13,14,15,32,33,34,35,36,37,38,39,40,41,42..., dimensions={0} | all-to-all | bytes 524288 | tf_op jit(solution)/shard_map/all_to_all | solution.py:653
  40.7 1.9 %collective-permute-start = (f32[64,8,128]{2,1,0:T(8,128)S(1)}, f32[64,8,128]{2,1,0:T(8,128)S(1)}, u32[]{:S(2)}, u32[]{:S(2)}) collective-permute-start(f32[64,8,128]{2,1,0:T(8,128)S(1)} %all_to_all.15), channel_id=1, source_target_pairs={{0,16},{16,0},{32,48},{48,32},{64,80},{80,64},{96,112},{112,96},{1... | collective-permute-start | bytes 786440 | tf_op jit(solution)/shard_map/ppermute | solution.py:656
  42.7 1.2 %early.1 = (bf16[1024,256]{1,0:T(8,128)(2,1)S(1)}, f32[448,128]{1,0:T(8,128)S(1)}) custom-call(f32[512,128]{1,0:T(8,128)S(1)} %bitcast.20, bf16[1024,256]{1,0:T(8,128)(2,1)} %constant.4.clone.table_from), custom_call_target="tpu_custom_call" | custom-call | tf_op jit(solution)/shard_map/early/pallas_call | solution.py:657
  43.9 0.3 collective-permute-done
  44.2 1.2 %first.1 = (f32[896,128]{1,0:T(8,128)S(1)}, f32[336,128]{1,0:T(8,128)S(1)}, s32[8,128]{1,0:T(8,128)S(1)}, bf16[1824,256]{1,0:T(8,128)(2,1)S(1)}) custom-call(s32[4,6]{1,0:T(4,128)} %bitcast.30, f32[448,128]{1,0:T(8,128)S(1)} %get-tuple-element.11.half_ref, f32[512,128]{1,0:T(8,128)S(1)} %bitcast.23, bf16[1024,256]{1,0:T(8,128)(2,1)S(1)} %get-tuple-element.12.table_ref, ...), custom_call_target="tpu_custom_call" | custom-call | tf_op jit(solution)/shard_map/first/pallas_call | solution.py:664
  45.4 22.0 %all_to_all.16 = f32[6,56,128]{2,1,0:T(8,128)S(1)} all-to-all(f32[6,56,128]{2,1,0:T(8,128)S(1)} %bitcast.24), channel_id=1, replica_groups=mesh['face'=6,'fy'=8,'fx'=16] {'face'}, dimensions={0} | all-to-all | bytes 344064 | tf_op jit(solution)/shard_map/all_to_all | solution.py:686
  67.4 2.8 %second.1 = f32[64,1,384]{2,1,0:T(1,128)S(1)} custom-call(s32[8,128]{1,0:T(8,128)S(1)} %get-tuple-element.13.which_ref, f32[336,128]{1,0:T(8,128)S(1)} %bitcast.22, f32[896,128]{1,0:T(8,128)S(1)} %get-tuple-element.15.fields_ref, bf16[1824,256]{1,0:T(8,128)(2,1)S(1)} %get-tuple-element.16.table_ref), custom_call_target="tpu_custom_call" | custom-call | tf_op jit(solution)/shard_map/second/pallas_call | solution.py:687
  70.2 22.0 %all_to_all.17.got_ref = f32[64,1,384]{2,1,0:T(1,128)S(1)} all-to-all(f32[64,1,384]{2,1,0:T(1,128)S(1)} %second.1), channel_id=1, replica_groups={{0,1,2,3,4,5,6,7,8,9,10,11,12,13,14,15,32,33,34,35,36,37,38,39,40,41,42..., dimensions={0} | all-to-all | bytes 196608 | tf_op jit(solution)/shard_map/all_to_all | solution.py:694
  92.2 0.8 unpack.1
Async XLA Ops:
  40.7 3.4 %collective-permute-start = (f32[64,8,128]{2,1,0:T(8,128)S(1)}, f32[64,8,128]{2,1,0:T(8,128)S(1)}, u32[]{:S(2)}, u32[]{:S(2)}) collective-permute-start(f32[64,8,128]{2,1,0:T(8,128)S(1)} %all_to_all.15), channel_id=1, source_target_pairs={{0,16},{16,0},{32,48},{48,32},{64,80},{80,64},{96,112},{112,96},{1... | collective-permute-start | bytes 786440 | tf_op jit(solution)/shard_map/ppermute | solution.py:656

commit v10 on v9

--- a/solution.py
+++ b/solution.py
@@ -388,9 +388,9 @@
     late.wait()
 
 
-def reversed_blocks(rows, table):
+def reversed_blocks(rows, table, product):
     parts = stacked([part.astype(jnp.float32) for part in split(rows)]).astype(jnp.bfloat16)
-    moved = dot(parts, table.left("reverse"))
+    moved = product(parts, table.left("reverse"))
     count = rows.shape[0]
     moved = stacked([moved[n * count : n * count + count] for n in range(3)], 1)
     moved = dot(table.right("reverse"), moved.astype(jnp.bfloat16))
@@ -403,7 +403,7 @@
     if edge == 0:
         return rows
     if edge == 2:
-        return reversed_blocks(rows, table)
+        return reversed_blocks(rows, table, dot)
     name = "east" if edge == 1 else "west"
     moved = dot(stacked(split(rows)), table.whole(name + "_out"))
     halves = stacked([moved[:, :LANES], moved[:, LANES:]], 0)
@@ -470,7 +470,7 @@
         rows = stacked([*fields, corner])
         count = 16
         if edge == 0:
-            rows = reversed_blocks(rows, table)
+            rows = reversed_blocks(rows, table, dot_halves)
         elif edge % 2:
             name = "east" if edge == 1 else "west"
             order = table.left("in_rows") if edge == 1 else table.right("in_rows")

time: 93.3 us -> 93.3 us (level)
  no operation moved by 1% of the time
where the time goes in v10:
time: 93.3 us; the launch traced here: 93 us
  blocking collectives  83.6 us (90%)
  Pallas kernels  7.2 us (8%)
  starting transfers between devices  1.91 us (2%)
    all_to_all x1, blocking collectives, per_device(): lax.all_to_all(packed.reshape(64, 8, LANES), axes, 0, 0, axis_index_group...  39.6 us
    all_to_all x1, blocking collectives, per_device(): lax.all_to_all(send.reshape(FACES, SLOT, LANES), 'face', 0, 0, tiled=True)  22 us
    all_to_all x1, blocking collectives, per_device(): lax.all_to_all(updated, axes, 0, 0, axis_index_groups=groups, tiled=True)  22 us
    pallas_call x1, Pallas kernels, per_device(): call(second_kernel, near(64, 1, 3 * LANES), [VMEM] * 4, [pltpu.VMEM((4 *...  2.82 us
    ppermute x1, starting transfers between devices, per_device(): other = lax.ppermute(own, 'fy', [(i, i ^ 1) for i in range(8)])  1.91 us
  transfers between devices with their start and end apart: 1, of which 1 were waited for; matrix products, arithmetic and copies ran while one was open for 0% of the time, Pallas kernels for 1%

profile of v10, /device:TPU:2, one launch (start us, length us, event | category | flops | bytes accessed | tf_op | source)
XLA Modules:
  0.0 93.0 jit_solution(1279715277768980441)
XLA Ops:
  0.0 1.1 %pack.1 = f32[512,128]{1,0:T(8,128)S(1)} custom-call(f32[128,192]{1,0:T(8,128)} %bitcast.25, f32[8,16]{1,0:T(8,128)} %bitcast.27, f32[2,8,16]{2,1,0:T(8,128)} %bitcast.26, f32[8,16]{1,0:T(8,128)} %bitcast.28, f32[8,16]{1,0:T(8,128)} %bitcast.29), custom_call_target="tpu_custom_call" | custom-call | tf_op jit(solution)/shard_map/pack/pallas_call | solution.py:646
  1.1 39.6 %all_to_all.15 = f32[64,8,128]{2,1,0:T(8,128)S(1)} all-to-all(f32[64,8,128]{2,1,0:T(8,128)S(1)} %bitcast.21), channel_id=1, replica_groups={{0,1,2,3,4,5,6,7,8,9,10,11,12,13,14,15,32,33,34,35,36,37,38,39,40,41,42..., dimensions={0} | all-to-all | bytes 524288 | tf_op jit(solution)/shard_map/all_to_all | solution.py:653
  40.7 1.9 %collective-permute-start = (f32[64,8,128]{2,1,0:T(8,128)S(1)}, f32[64,8,128]{2,1,0:T(8,128)S(1)}, u32[]{:S(2)}, u32[]{:S(2)}) collective-permute-start(f32[64,8,128]{2,1,0:T(8,128)S(1)} %all_to_all.15), channel_id=1, source_target_pairs={{0,16},{16,0},{32,48},{48,32},{64,80},{80,64},{96,112},{112,96},{1... | collective-permute-start | bytes 786440 | tf_op jit(solution)/shard_map/ppermute | solution.py:656
  42.7 1.2 %early.1 = (bf16[1024,256]{1,0:T(8,128)(2,1)S(1)}, f32[448,128]{1,0:T(8,128)S(1)}) custom-call(f32[512,128]{1,0:T(8,128)S(1)} %bitcast.20, bf16[1024,256]{1,0:T(8,128)(2,1)} %constant.4.clone.table_from), custom_call_target="tpu_custom_call" | custom-call | tf_op jit(solution)/shard_map/early/pallas_call | solution.py:657
  43.9 0.3 collective-permute-done
  44.2 1.2 %first.1 = (f32[896,128]{1,0:T(8,128)S(1)}, f32[336,128]{1,0:T(8,128)S(1)}, s32[8,128]{1,0:T(8,128)S(1)}, bf16[1824,256]{1,0:T(8,128)(2,1)S(1)}) custom-call(s32[4,6]{1,0:T(4,128)} %bitcast.30, f32[448,128]{1,0:T(8,128)S(1)} %get-tuple-element.11.half_ref, f32[512,128]{1,0:T(8,128)S(1)} %bitcast.23, bf16[1024,256]{1,0:T(8,128)(2,1)S(1)} %get-tuple-element.12.table_ref, ...), custom_call_target="tpu_custom_call" | custom-call | tf_op jit(solution)/shard_map/first/pallas_call | solution.py:664
  45.4 22.0 %all_to_all.16 = f32[6,56,128]{2,1,0:T(8,128)S(1)} all-to-all(f32[6,56,128]{2,1,0:T(8,128)S(1)} %bitcast.24), channel_id=1, replica_groups=mesh['face'=6,'fy'=8,'fx'=16] {'face'}, dimensions={0} | all-to-all | bytes 344064 | tf_op jit(solution)/shard_map/all_to_all | solution.py:686
  67.4 2.8 %second.1 = f32[64,1,384]{2,1,0:T(1,128)S(1)} custom-call(s32[8,128]{1,0:T(8,128)S(1)} %get-tuple-element.13.which_ref, f32[336,128]{1,0:T(8,128)S(1)} %bitcast.22, f32[896,128]{1,0:T(8,128)S(1)} %get-tuple-element.15.fields_ref, bf16[1824,256]{1,0:T(8,128)(2,1)S(1)} %get-tuple-element.16.table_ref), custom_call_target="tpu_custom_call" | custom-call | tf_op jit(solution)/shard_map/second/pallas_call | solution.py:687
  70.2 22.0 %all_to_all.17.got_ref = f32[64,1,384]{2,1,0:T(1,128)S(1)} all-to-all(f32[64,1,384]{2,1,0:T(1,128)S(1)} %second.1), channel_id=1, replica_groups={{0,1,2,3,4,5,6,7,8,9,10,11,12,13,14,15,32,33,34,35,36,37,38,39,40,41,42..., dimensions={0} | all-to-all | bytes 196608 | tf_op jit(solution)/shard_map/all_to_all | solution.py:694
  92.2 0.8 unpack.1
Async XLA Ops:
  40.7 3.4 %collective-permute-start = (f32[64,8,128]{2,1,0:T(8,128)S(1)}, f32[64,8,128]{2,1,0:T(8,128)S(1)}, u32[]{:S(2)}, u32[]{:S(2)}) collective-permute-start(f32[64,8,128]{2,1,0:T(8,128)S(1)} %all_to_all.15), channel_id=1, source_target_pairs={{0,16},{16,0},{32,48},{48,32},{64,80},{80,64},{96,112},{112,96},{1... | collective-permute-start | bytes 786440 | tf_op jit(solution)/shard_map/ppermute | solution.py:656
